TPU v7x, 32 devices: a whole 2x2x4 slice. The times are simulated.
32 devices in a mesh: rep: 8 (over y, x, core), grp: 4 (over z).
Axes of the slice: x: 2, y: 2, z: 4, core: 2. Of those that a mesh axis runs over, the one named last changes fastest.
Arguments:
- tokens: bfloat16 [8, 1024, 512], P('rep', 'grp'), may hold values from -6 to 6
- segments: int32 [8, 1024], P('rep', 'grp'), may hold values from 0 to 1024, as said below
- positions: int32 [8, 1024], P('rep', 'grp'), may hold values from 0 to 1023, as said below
- norm1_gain: bfloat16 [512], P('grp'), may hold values from 0.5 to 1.5
- w_query: bfloat16 [512, 512], P('grp'), may hold values from -0.25 to 0.25
- w_key: bfloat16 [512, 512], P('grp'), may hold values from -0.25 to 0.25
- w_value: bfloat16 [512, 512], P('grp'), may hold values from -0.25 to 0.25
- w_out: bfloat16 [512, 512], P('grp'), may hold values from -1 to 1
- norm2_gain: bfloat16 [512], P('grp'), may hold values from 0.5 to 1.5
- w_gate: bfloat16 [512, 1376], P('grp'), may hold values from -0.25 to 0.25
- w_up: bfloat16 [512, 1376], P('grp'), may hold values from -0.25 to 0.25
- w_down: bfloat16 [1376, 512], P('grp'), may hold values from -0.15625 to 0.15625
- cotangent: bfloat16 [8, 1024, 512], P('rep', 'grp'), may hold values from -6 to 6
Outputs:
- output: bfloat16 [8, 1024, 512], P('rep', 'grp')
- input_grad: float32 [8, 1024, 512], P('rep', 'grp')
- grad_norm1: float32 [512], P('grp')
- grad_query: float32 [512, 512], P('grp')
- grad_key: float32 [512, 512], P('grp')
- grad_value: float32 [512, 512], P('grp')
- grad_out: float32 [512, 512], P('grp')
- grad_norm2: float32 [512], P('grp')
- grad_gate: float32 [512, 1376], P('grp')
- grad_up: float32 [512, 1376], P('grp')
- grad_down: float32 [1376, 512], P('grp')
Inputs may be any that keep to these rules, and one draw needn't show every extreme that they name: `segments`: in each sequence the documents are runs of consecutive tokens numbered 1, 2, 3 in order; tokens after the last document, if any, are padding numbered 0. `positions`: A token's index in its sequence minus the index of the first token of its run (its document, or the padding).
All inputs are finite; a program needn't handle non-finite values.
Results may differ from a plain program's by a relative error of at most 0.019.
Values may be sent and summed in bfloat16 or wider, within the bound.
No kernel may reach another device: no remote copies, remote signals or barrier semaphores. Data moves between devices by JAX's collectives and lax.ppermute only.
A program may use at most 64 MiB of HBM per device.

v0:
```python
import jax
import jax.numpy as jnp
from jax import lax
from jax.sharding import PartitionSpec as P

D = 512
H = 8
KV = 8
HD = 64


EPSILON = 1e-05
NEGATIVE = -1e30


def norm_scale(values):
    return lax.rsqrt(jnp.mean(values * values, axis=-1, keepdims=True) + EPSILON)


def rotation_tables(positions, width):
    halves = width // 2
    frequency = 10000.0 ** (-2.0 * jnp.arange(halves, dtype=jnp.float32) / width)
    angles = positions.astype(jnp.float32)[..., None, None] * frequency
    return (jnp.cos(angles), jnp.sin(angles))


def rotate(values, cosine, sines):
    halves = values.shape[-1] // 2
    first_half = values[..., :halves]
    second_half = values[..., halves:]
    return jnp.concatenate(
        [first_half * cosine - second_half * sines, second_half * cosine + first_half * sines],
        axis=-1,
    )


def rotate_back(gradient, cosine, sines):
    halves = gradient.shape[-1] // 2
    first_half = gradient[..., :halves]
    second_half = gradient[..., halves:]
    return jnp.concatenate(
        [first_half * cosine + second_half * sines, second_half * cosine - first_half * sines],
        axis=-1,
    )


def contract_rows(left, right):
    return lax.dot_general(
        left, right, (((0,), (0,)), ((), ())), preferred_element_type=jnp.float32
    )


def against(left, right):
    return lax.dot_general(
        left, right, (((1,), (1,)), ((), ())), preferred_element_type=jnp.float32
    )


def fetch_attention(norm1_gain, w_query, w_key, w_value, w_out):
    return (
        lax.all_gather(norm1_gain, "grp", axis=0, tiled=True),
        lax.all_gather(w_query, "grp", axis=0, tiled=True),
        lax.all_gather(w_key, "grp", axis=0, tiled=True),
        lax.all_gather(w_value, "grp", axis=0, tiled=True),
        lax.all_gather(w_out, "grp", axis=0, tiled=True),
    )


def fetch_mlp(norm2_gain, w_gate, w_up, w_down):
    return (
        lax.all_gather(norm2_gain, "grp", axis=0, tiled=True),
        lax.all_gather(w_gate, "grp", axis=0, tiled=True),
        lax.all_gather(w_up, "grp", axis=0, tiled=True),
        lax.all_gather(w_down, "grp", axis=0, tiled=True),
    )


def replica_all(parts):
    return (
        lax.psum(parts[0].astype(jnp.bfloat16), "rep").astype(jnp.float32),
        lax.psum(parts[1].astype(jnp.bfloat16), "rep").astype(jnp.float32),
        lax.psum(parts[2].astype(jnp.bfloat16), "rep").astype(jnp.float32),
        lax.psum(parts[3].astype(jnp.bfloat16), "rep").astype(jnp.float32),
        lax.psum(parts[4].astype(jnp.bfloat16), "rep").astype(jnp.float32),
        lax.psum(parts[5].astype(jnp.bfloat16), "rep").astype(jnp.float32),
        lax.psum(parts[6].astype(jnp.bfloat16), "rep").astype(jnp.float32),
        lax.psum(parts[7].astype(jnp.bfloat16), "rep").astype(jnp.float32),
        lax.psum(parts[8].astype(jnp.bfloat16), "rep").astype(jnp.float32),
    )


def flat_body(
    tokens,
    segments,
    positions,
    norm1_gain,
    w_query,
    w_key,
    w_value,
    w_out,
    norm2_gain,
    w_gate,
    w_up,
    w_down,
    cotangent,
):
    seq_count = tokens.shape[0]
    local_len = tokens.shape[1]
    full_len = local_len * lax.axis_size("grp")
    row_count = seq_count * local_len
    group_size = H // KV
    score_scale = HD ** (-0.5)
    inputs = tokens.reshape(row_count, D).astype(jnp.float32)
    gain_in, query_full, key_full, value_full, out_full = fetch_attention(
        norm1_gain, w_query, w_key, w_value, w_out
    )
    scale_in = norm_scale(inputs)
    unit_in = inputs * scale_in
    normed_in = (unit_in * gain_in.astype(jnp.float32)).astype(jnp.bfloat16)
    query_raw = jnp.dot(normed_in, query_full, preferred_element_type=jnp.float32)
    key_raw = jnp.dot(normed_in, key_full, preferred_element_type=jnp.float32)
    value_raw = jnp.dot(normed_in, value_full, preferred_element_type=jnp.float32)
    cosine, sines = rotation_tables(positions, HD)
    query_rot = rotate(query_raw.reshape(seq_count, local_len, H, HD), cosine, sines).astype(
        jnp.bfloat16
    )
    key_rot = (
        rotate(key_raw.reshape(seq_count, local_len, KV, HD), cosine, sines)
        .astype(jnp.bfloat16)
        .reshape(seq_count, local_len, KV * HD)
    )
    value_low = value_raw.astype(jnp.bfloat16).reshape(seq_count, local_len, KV * HD)
    keys_all, values_all = (
        lax.all_gather(key_rot, "grp", axis=1, tiled=True),
        lax.all_gather(value_low, "grp", axis=1, tiled=True),
    )
    query_index = lax.axis_index("grp") * local_len + jnp.arange(local_len, dtype=jnp.int32)
    offsets = query_index[:, None] - jnp.arange(full_len, dtype=jnp.int32)[None, :]
    allowed = (
        (offsets >= 0)[None]
        & (offsets[None] <= positions[:, :, None])
        & ((segments[:, :, None] != 0) | (offsets == 0)[None])
    )
    query_heads = query_rot.reshape(seq_count, local_len, KV, group_size, HD).transpose(
        2, 0, 1, 3, 4
    )
    key_heads = keys_all.reshape(seq_count, full_len, KV, HD).transpose(2, 0, 1, 3)
    value_heads = values_all.reshape(seq_count, full_len, KV, HD).transpose(2, 0, 1, 3)

    def masked_scores(query_head, key_head):
        scores = (
            jnp.einsum("bqgd,bjd->bgqj", query_head, key_head, preferred_element_type=jnp.float32)
            * score_scale
        )
        return jnp.where(allowed[:, None], scores, NEGATIVE)

    def head_forward(items):
        query_head, key_head, value_head = items
        masked = masked_scores(query_head, key_head)
        peak = jnp.max(masked, axis=-1, keepdims=True)
        exponent = jnp.exp(masked - peak)
        summed = jnp.sum(exponent, axis=-1, keepdims=True)
        softmaxed = exponent / summed
        attended = jnp.einsum(
            "bgqj,bjd->bqgd",
            softmaxed.astype(jnp.bfloat16),
            value_head,
            preferred_element_type=jnp.float32,
        )
        return (attended, peak + jnp.log(summed))

    attended, log_totals = lax.map(head_forward, (query_heads, key_heads, value_heads))
    attn_low = attended.transpose(1, 2, 0, 3, 4).reshape(row_count, H * HD).astype(jnp.bfloat16)
    middle = inputs + jnp.dot(attn_low, out_full, preferred_element_type=jnp.float32)
    gain_mid, gate_full, up_full, down_full = fetch_mlp(norm2_gain, w_gate, w_up, w_down)
    scale_mid = norm_scale(middle)
    unit_mid = middle * scale_mid
    normed_mid = (unit_mid * gain_mid.astype(jnp.float32)).astype(jnp.bfloat16)
    gate_raw = jnp.dot(normed_mid, gate_full, preferred_element_type=jnp.float32)
    up_raw = jnp.dot(normed_mid, up_full, preferred_element_type=jnp.float32)
    sigmoid_gate = jax.nn.sigmoid(gate_raw)
    hidden_low = (gate_raw * sigmoid_gate * up_raw).astype(jnp.bfloat16)
    output = (
        (middle + jnp.dot(hidden_low, down_full, preferred_element_type=jnp.float32))
        .astype(jnp.bfloat16)
        .reshape(tokens.shape)
    )
    gain_mid, gate_full, up_full, down_full = fetch_mlp(norm2_gain, w_gate, w_up, w_down)
    cot_low = cotangent.reshape(row_count, D)
    hidden_delta = against(cot_low, down_full)
    gate_delta = (
        hidden_delta * up_raw * sigmoid_gate * (1.0 + gate_raw * (1.0 - sigmoid_gate))
    ).astype(jnp.bfloat16)
    upward_delta = (hidden_delta * gate_raw * sigmoid_gate).astype(jnp.bfloat16)
    columns = normed_mid
    gate_part = lax.psum_scatter(
        contract_rows(columns, gate_delta).astype(jnp.bfloat16),
        "grp",
        scatter_dimension=0,
        tiled=True,
    ).astype(jnp.float32)
    columns = normed_mid
    up_part = lax.psum_scatter(
        contract_rows(columns, upward_delta).astype(jnp.bfloat16),
        "grp",
        scatter_dimension=0,
        tiled=True,
    ).astype(jnp.float32)
    columns = hidden_low
    down_part = lax.psum_scatter(
        contract_rows(columns, cot_low).astype(jnp.bfloat16), "grp", scatter_dimension=0, tiled=True
    ).astype(jnp.float32)
    gate_grad, up_grad, down_grad = (gate_part, up_part, down_part)
    normed_mid_delta = against(gate_delta, gate_full) + against(upward_delta, up_full)
    gain_mid_term = jnp.sum(normed_mid_delta * unit_mid, axis=0)
    scaled_mid = normed_mid_delta * gain_mid.astype(jnp.float32)
    middle_delta = cot_low.astype(jnp.float32) + scale_mid * (
        scaled_mid - unit_mid * jnp.mean(scaled_mid * unit_mid, axis=-1, keepdims=True)
    )
    gain_in, query_full, key_full, value_full, out_full = fetch_attention(
        norm1_gain, w_query, w_key, w_value, w_out
    )
    out_delta = middle_delta.astype(jnp.bfloat16)
    out_term = contract_rows(attn_low, out_delta)
    attn_delta = against(out_delta, out_full).astype(jnp.bfloat16)
    attn_heads = attn_delta.reshape(seq_count, local_len, KV, group_size, HD).transpose(
        2, 0, 1, 3, 4
    )

    def head_backward(items):
        query_head, key_head, value_head, log_total, attn_head = items
        masked = masked_scores(query_head, key_head)
        softmaxed = jnp.exp(masked - log_total)
        prob_delta = jnp.einsum(
            "bqgd,bjd->bgqj", attn_head, value_head, preferred_element_type=jnp.float32
        )
        value_delta = jnp.einsum(
            "bgqj,bqgd->bjd",
            softmaxed.astype(jnp.bfloat16),
            attn_head,
            preferred_element_type=jnp.float32,
        )
        score_delta = (
            softmaxed * (prob_delta - jnp.sum(softmaxed * prob_delta, axis=-1, keepdims=True))
        ).astype(jnp.bfloat16)
        query_delta = (
            jnp.einsum("bgqj,bjd->bqgd", score_delta, key_head, preferred_element_type=jnp.float32)
            * score_scale
        )
        key_delta = (
            jnp.einsum(
                "bgqj,bqgd->bjd", score_delta, query_head, preferred_element_type=jnp.float32
            )
            * score_scale
        )
        return (query_delta, key_delta, value_delta)

    query_deltas, key_deltas, value_deltas = lax.map(
        head_backward, (query_heads, key_heads, value_heads, log_totals, attn_heads)
    )
    key_delta_all = key_deltas.transpose(1, 2, 0, 3).reshape(seq_count, full_len, KV * HD)
    value_delta_all = value_deltas.transpose(1, 2, 0, 3).reshape(seq_count, full_len, KV * HD)
    key_delta_own, value_delta_own = (
        lax.psum_scatter(
            key_delta_all.astype(jnp.bfloat16), "grp", scatter_dimension=1, tiled=True
        ).astype(jnp.float32),
        lax.psum_scatter(
            value_delta_all.astype(jnp.bfloat16), "grp", scatter_dimension=1, tiled=True
        ).astype(jnp.float32),
    )
    query_low = (
        rotate_back(
            query_deltas.transpose(1, 2, 0, 3, 4).reshape(seq_count, local_len, H, HD),
            cosine,
            sines,
        )
        .reshape(row_count, H * HD)
        .astype(jnp.bfloat16)
    )
    key_low = (
        rotate_back(key_delta_own.reshape(seq_count, local_len, KV, HD), cosine, sines)
        .reshape(row_count, KV * HD)
        .astype(jnp.bfloat16)
    )
    value_delta_low = value_delta_own.reshape(row_count, KV * HD).astype(jnp.bfloat16)
    query_term = contract_rows(normed_in, query_low)
    key_term = contract_rows(normed_in, key_low)
    value_term = contract_rows(normed_in, value_delta_low)
    normed_in_delta = (
        against(query_low, query_full)
        + against(key_low, key_full)
        + against(value_delta_low, value_full)
    )
    gain_in_term = jnp.sum(normed_in_delta * unit_in, axis=0)
    scaled_in = normed_in_delta * gain_in.astype(jnp.float32)
    input_grad = middle_delta + scale_in * (
        scaled_in - unit_in * jnp.mean(scaled_in * unit_in, axis=-1, keepdims=True)
    )
    norm1_part, norm2_part, query_part, key_part, value_part, out_part = (
        lax.psum_scatter(
            gain_in_term.astype(jnp.bfloat16), "grp", scatter_dimension=0, tiled=True
        ).astype(jnp.float32),
        lax.psum_scatter(
            gain_mid_term.astype(jnp.bfloat16), "grp", scatter_dimension=0, tiled=True
        ).astype(jnp.float32),
        lax.psum_scatter(
            query_term.astype(jnp.bfloat16), "grp", scatter_dimension=0, tiled=True
        ).astype(jnp.float32),
        lax.psum_scatter(
            key_term.astype(jnp.bfloat16), "grp", scatter_dimension=0, tiled=True
        ).astype(jnp.float32),
        lax.psum_scatter(
            value_term.astype(jnp.bfloat16), "grp", scatter_dimension=0, tiled=True
        ).astype(jnp.float32),
        lax.psum_scatter(
            out_term.astype(jnp.bfloat16), "grp", scatter_dimension=0, tiled=True
        ).astype(jnp.float32),
    )
    (
        norm1_grad,
        norm2_grad,
        query_grad,
        key_grad,
        value_grad,
        out_grad,
        gate_grad,
        up_grad,
        down_grad,
    ) = replica_all(
        (
            norm1_part,
            norm2_part,
            query_part,
            key_part,
            value_part,
            out_part,
            gate_grad,
            up_grad,
            down_grad,
        )
    )
    return (
        output,
        input_grad.reshape(tokens.shape),
        norm1_grad,
        query_grad,
        key_grad,
        value_grad,
        out_grad,
        norm2_grad,
        gate_grad,
        up_grad,
        down_grad,
    )


def on_device(
    tokens,
    segments,
    positions,
    norm1_gain,
    w_query,
    w_key,
    w_value,
    w_out,
    norm2_gain,
    w_gate,
    w_up,
    w_down,
    cotangent,
):
    results = flat_body(
        tokens,
        segments,
        positions,
        norm1_gain,
        w_query,
        w_key,
        w_value,
        w_out,
        norm2_gain,
        w_gate,
        w_up,
        w_down,
        cotangent,
    )
    return results


def solution(mesh):
    in_specs = (
        P("rep", "grp", None),
        P("rep", "grp"),
        P("rep", "grp"),
        P("grp"),
        P("grp", None),
        P("grp", None),
        P("grp", None),
        P("grp", None),
        P("grp"),
        P("grp", None),
        P("grp", None),
        P("grp", None),
        P("rep", "grp", None),
    )
    out_specs = (
        P("rep", "grp", None),
        P("rep", "grp", None),
        P("grp"),
        P("grp", None),
        P("grp", None),
        P("grp", None),
        P("grp", None),
        P("grp"),
        P("grp", None),
        P("grp", None),
        P("grp", None),
    )
    return jax.shard_map(
        on_device, mesh=mesh, in_specs=in_specs, out_specs=out_specs, check_vma=False
    )
```

profile of v0, /device:TPU:0, one launch (start us, length us, event | category | flops | bytes accessed | tf_op | source)
XLA Modules:
  0.0 614.8 jit_solution(3722437577382787025)
XLA Ops:
  7.2 17.6 %all_gather.43 = bf16[512,512]{1,0:T(8,128)(2,1)S(1)} all-gather(bf16[128,512]{1,0:T(8,128)(2,1)} %param.23), channel_id=1, replica_groups=mesh['rep'=8,'grp'=4] {'grp'}, dimensions={0}, use_global_device_ids=true | all-gather | bytes 655360 | tf_op jit(solution)/shard_map/all_gather | solution.py:64
  24.8 11.8 %all-gather.1 = bf16[4,1,128]{2,1,0:T(2,128)(2,1)S(1)} all-gather(bf16[1,1,128]{2,1,0:T(2,128)(2,1)} %bitcast.349), channel_id=1, replica_groups=mesh['rep'=8,'grp'=4] {'grp'}, dimensions={0}, use_global_device_ids=true | all-gather | bytes 1280 | tf_op jit(solution)/shard_map/all_gather | solution.py:61
  39.9 19.2 %all_gather.47 = bf16[512,512]{1,0:T(8,128)(2,1)S(1)} all-gather(bf16[128,512]{1,0:T(8,128)(2,1)S(1)} %copy-done.27), channel_id=1, replica_groups=mesh['rep'=8,'grp'=4] {'grp'}, dimensions={0}, use_global_device_ids=true | all-gather | bytes 655360 | tf_op jit(solution)/shard_map/all_gather | solution.py:62
  59.4 19.7 %all_gather.45 = bf16[512,512]{1,0:T(8,128)(2,1)S(1)} all-gather(bf16[128,512]{1,0:T(8,128)(2,1)S(1)} %copy-done.28), channel_id=1, replica_groups=mesh['rep'=8,'grp'=4] {'grp'}, dimensions={0}, use_global_device_ids=true | all-gather | bytes 655360 | tf_op jit(solution)/shard_map/all_gather | solution.py:63
  84.0 17.9 %all_gather.48 = bf16[512,512]{1,0:T(8,128)(2,1)S(1)} all-gather(bf16[128,512]{1,0:T(8,128)(2,1)S(1)} %copy-done.29), channel_id=1, replica_groups=mesh['rep'=8,'grp'=4] {'grp'}, dimensions={0}, use_global_device_ids=true | all-gather | bytes 655360 | tf_op jit(solution)/shard_map/all_gather | solution.py:65
  101.9 9.7 %all-gather.2 = bf16[4,1,128]{2,1,0:T(2,128)(2,1)S(1)} all-gather(bf16[1,1,128]{2,1,0:T(2,128)(2,1)S(1)} %bitcast.350), channel_id=1, replica_groups=mesh['rep'=8,'grp'=4] {'grp'}, dimensions={0}, use_global_device_ids=true | all-gather | bytes 1280 | tf_op jit(solution)/shard_map/all_gather | solution.py:71
  119.4 26.0 %while.30 = (s32[]{:T(128)}, bf16[8,1,256,1,64]{2,4,3,1,0:T(8,128)(2,1)}, f32[8,1,1,256,1]{3,4,2,1,0:T(1,128)}, bf16[8,1,1024,64]{3,2,1,0:T(8,128)(2,1)S(1)}, bf...) while((s32[]{:T(128)}, ...), condition=%wide.region_4.5_spmd.clone.clone, body=%wide.region_1.4_spmd.clone.sunk.clone | while | flops 71040768 | bytes 3783017 | solution.py:172
  148.5 3.0 fusion.103
  151.6 31.7 %all-gather.13.cloned.1.call-done = bf16[512,1376]{0,1:T(8,128)(2,1)} async-done(((bf16[128,1376]{0,1:T(8,128)(2,1)}), bf16[512,1376]{0,1:T(8,128)(2,1)}) %all-gather.13.cloned.1.call-update) | async-done | bytes 1409040 | tf_op jit(solution)/shard_map/all_gather | solution.py:73
  186.2 30.8 %all-gather.15.cloned.1.call-done = bf16[1376,512]{1,0:T(8,128)(2,1)} async-done(((bf16[344,512]{1,0:T(8,128)(2,1)}), bf16[1376,512]{1,0:T(8,128)(2,1)}) %all-gather.15.cloned.1.call-update) | async-done | bytes 1409040 | tf_op jit(solution)/shard_map/all_gather | solution.py:74
  217.1 4.0 multiply_convert_fusion.1
  226.2 60.1 %while.31 = (s32[]{:T(128)}, f32[8,1,256,1,64]{2,4,3,1,0:T(8,128)S(1)}, bf16[8,1,1024,64]{2,3,1,0:T(8,128)(2,1)}, bf16[8,1,1024,64]{2,3,1,0:T(8,128)(2,1)}, bf16...) while((s32[]{:T(128)}, ...), condition=%wide.region_9.10_spmd.clone.clone, body=%wide.region_7.9_spmd.clone.sunk.clone | while | flops 172048128 | bytes 9384321 | solution.py:258
  297.7 15.1 %reduce-scatter.14.cloned.1.call-done = bf16[1,256,512]{1,2,0:T(8,128)(2,1)} async-done(((bf16[1,1024,512]{1,2,0:T(8,128)(2,1)}), bf16[1,256,512]{1,2,0:T(8,128)(2,1)}) %reduce-scatter.14.cloned.1.call-update) | async-done | bytes 262160 | tf_op jit(solution)/shard_map/reduce_scatter | solution.py:264
  317.7 23.2 %reduce-scatter.16.cloned.1.call-done = bf16[1,256,512]{1,2,0:T(8,128)(2,1)} async-done(((bf16[1,1024,512]{1,2,0:T(8,128)(2,1)}), bf16[1,256,512]{1,2,0:T(8,128)(2,1)}) %reduce-scatter.16.cloned.1.call-update) | async-done | bytes 262160 | tf_op jit(solution)/shard_map/reduce_scatter | solution.py:267
  347.5 27.7 %reduce-scatter.28.cloned.1.call-done = bf16[128,1376]{1,0:T(8,128)(2,1)} async-done(((bf16[512,1376]{1,0:T(8,128)(2,1)}), bf16[128,1376]{1,0:T(8,128)(2,1)}) %reduce-scatter.28.cloned.1.call-update) | async-done | bytes 352272
  377.1 32.6 %reduce-scatter.30.cloned.1.call-done = bf16[128,1376]{1,0:T(8,128)(2,1)} async-done(((bf16[512,1376]{1,0:T(8,128)(2,1)}), bf16[128,1376]{1,0:T(8,128)(2,1)}) %reduce-scatter.30.cloned.1.call-update) | async-done | bytes 352272
  411.6 21.4 %reduce-scatter.24.cloned.1.call-done = bf16[128,512]{1,0:T(8,128)(2,1)} async-done(((bf16[512,512]{1,0:T(8,128)(2,1)}), bf16[128,512]{1,0:T(8,128)(2,1)}) %reduce-scatter.24.cloned.1.call-update) | async-done | bytes 131088 | tf_op jit(solution)/shard_map/reduce_scatter | solution.py:315
  433.1 33.5 %reduce-scatter.26.cloned.1.call-done = bf16[344,512]{1,0:T(8,128)(2,1)} async-done(((bf16[1376,512]{1,0:T(8,128)(2,1)}), bf16[344,512]{1,0:T(8,128)(2,1)}) %reduce-scatter.26.cloned.1.call-update) | async-done | bytes 352272 | tf_op jit(solution)/shard_map/reduce_scatter | solution.py:210
  466.5 23.4 %reduce-scatter.18.cloned.1.call-done = bf16[128,512]{1,0:T(8,128)(2,1)} async-done(((bf16[512,512]{1,0:T(8,128)(2,1)}), bf16[128,512]{1,0:T(8,128)(2,1)}) %reduce-scatter.18.cloned.1.call-update) | async-done | bytes 131088 | tf_op jit(solution)/shard_map/reduce_scatter | solution.py:306
  489.9 23.0 %reduce-scatter.20.cloned.1.call-done = bf16[128,512]{1,0:T(8,128)(2,1)} async-done(((bf16[512,512]{1,0:T(8,128)(2,1)}), bf16[128,512]{1,0:T(8,128)(2,1)}) %reduce-scatter.20.cloned.1.call-update) | async-done | bytes 131088 | tf_op jit(solution)/shard_map/reduce_scatter | solution.py:309
  512.9 22.9 %reduce-scatter.22.cloned.1.call-done = bf16[128,512]{1,0:T(8,128)(2,1)} async-done(((bf16[512,512]{1,0:T(8,128)(2,1)}), bf16[128,512]{1,0:T(8,128)(2,1)}) %reduce-scatter.22.cloned.1.call-update) | async-done | bytes 131088 | tf_op jit(solution)/shard_map/reduce_scatter | solution.py:312
  537.5 8.6 %all-reduce.4 = (bf16[512]{0:T(512)(128)(2,1)S(1)}, bf16[512]{0:T(512)(128)(2,1)S(1)}) all-reduce(bf16[512]{0:T(512)(128)(2,1)S(1)} %get-tuple-element.225, bf16[512]{0:T(512)(128)(2,1)S(1)} %copy-done.30), channel_id=5, replica_groups=mesh['rep'=8,'grp'=4] {'grp'}, use_global_device_ids=true, to_apply=%region_14.15.clone | all-reduce | flops 1024 | bytes 4096
  546.3 12.0 %all-reduce.2 = (bf16[128]{0:T(256)(128)(2,1)S(1)}, bf16[128]{0:T(256)(128)(2,1)S(1)}) all-reduce(bf16[128]{0:T(256)(128)(2,1)S(1)} %dynamic-slice.1, bf16[128]{0:T(256)(128)(2,1)S(1)} %dynamic-slice.3), channel_id=1, replica_groups=mesh['rep'=8,'grp'=4] {'rep'}, use_global_device_ids=true, to_apply=%region_15.16 | all-reduce | flops 256 | bytes 1024 | tf_op jit(solution)/shard_map/psum | solution.py:80
  560.3 38.6 %all-reduce.7.cloned.1.call-done = (bf16[128,512]{1,0:T(8,128)(2,1)}, bf16[128,512]{1,0:T(8,128)(2,1)}, bf16[128,512]{1,0:T(8,128)(2,1)}, bf16[128,512]{1,0:T(8,...) async-done(((bf16[128,512]{1,0:T(8,128)(2,1)}, bf16[128,512]{1,0:T(8,128)(2,1)}, bf16[128,512]{1,0:T(8,128)(2,1)}, ...) | async-done | bytes 1581072 | tf_op jit(solution)/shard_map/psum | solution.py:82
  (276 shorter events, 152.3 us)
Async XLA Ops:
  7.2 32.7 %copy-start.27 = (bf16[128,512]{1,0:T(8,128)(2,1)S(1)}, bf16[128,512]{1,0:T(8,128)(2,1)}, u32[]{:S(2)}) copy-start(bf16[128,512]{1,0:T(8,128)(2,1)} %param.21) | copy-start | bytes 393220
  7.2 105.1 %all-gather.17.cloned.1.call-start = ((), (), s32[]{:S(2)}) async-start(), calls=%async_computation.20 | async-start | bytes 1310720 | tf_op jit(solution)/shard_map/all_gather | solution.py:135
  37.7 21.6 %copy-start.31 = (s32[1,256]{1,0:T(1,128)S(1)}, s32[1,256]{1,0:T(1,128)}, u32[]{:S(2)}) copy-start(s32[1,256]{1,0:T(1,128)} %param.19) | copy-start | bytes 3076
  37.8 21.6 %copy-start.28 = (bf16[128,512]{1,0:T(8,128)(2,1)S(1)}, bf16[128,512]{1,0:T(8,128)(2,1)}, u32[]{:S(2)}) copy-start(bf16[128,512]{1,0:T(8,128)(2,1)} %param.22) | copy-start | bytes 393220
  39.8 76.8 %all-gather.9.cloned.1.call-start = ((), (), s32[]{:S(2)}) async-start(), calls=%async_computation.9 | async-start | bytes 1310720 | tf_op jit(solution)/shard_map/all_gather | solution.py:134
  59.1 20.6 %copy-start.4 = (bf16[512,512]{1,0:T(8,128)(2,1)}, bf16[512,512]{1,0:T(8,128)(2,1)S(1)}, u32[]{:S(2)}) copy-start(bf16[512,512]{1,0:T(8,128)(2,1)S(1)} %all_gather.47) | copy-start | bytes 1572868
  80.5 21.4 %copy-start.33 = (bf16[128]{0:T(256)(128)(2,1)S(1)}, bf16[128]{0:T(256)(128)(2,1)}, u32[]{:S(2)}) copy-start(bf16[128]{0:T(256)(128)(2,1)} %param.25) | copy-start | bytes 772
  81.3 67.2 %all-gather.11.cloned.1.call-start = ((), (), s32[]{:S(2)}) async-start(), calls=%async_computation.10 | async-start | bytes 1761280 | tf_op jit(solution)/shard_map/all_gather | solution.py:72
  82.0 101.2 %all-gather.13.cloned.1.call-start = ((), (), s32[]{:S(2)}) async-start(), calls=%async_computation.11 | async-start | bytes 1761280 | tf_op jit(solution)/shard_map/all_gather | solution.py:73
  82.6 134.4 %all-gather.15.cloned.1.call-start = ((), (), s32[]{:S(2)}) async-start(), calls=%async_computation.12 | async-start | bytes 1761280 | tf_op jit(solution)/shard_map/all_gather | solution.py:74
  83.2 229.6 %reduce-scatter.14.cloned.1.call-start = ((), (), s32[]{:S(2)}) async-start(), calls=%async_computation.13 | async-start | bytes 1310720 | tf_op jit(solution)/shard_map/reduce_scatter | solution.py:264
  101.9 44.8 %copy-start.6 = (bf16[512,512]{1,0:T(8,128)(2,1)}, bf16[512,512]{1,0:T(8,128)(2,1)S(1)}, u32[]{:S(2)}) copy-start(bf16[512,512]{1,0:T(8,128)(2,1)S(1)} %all_gather.48) | copy-start | bytes 1572868
  151.6 65.5 %copy-start.16 = (bf16[1,256,512]{2,1,0:T(8,128)(2,1)S(1)}, bf16[1,256,512]{2,1,0:T(8,128)(2,1)}, u32[]{:S(2)}) copy-start(bf16[1,256,512]{2,1,0:T(8,128)(2,1)} %param.29) | copy-start | bytes 786436
  186.2 34.8 %copy-start.2 = (bf16[512,1376]{0,1:T(8,128)(2,1)S(1)}, bf16[512,1376]{0,1:T(8,128)(2,1)}, u32[]{:S(2)}) copy-start(bf16[512,1376]{0,1:T(8,128)(2,1)} %all-gather.11.cloned.1.call-done) | copy-start | bytes 4227076
  286.4 54.5 %reduce-scatter.16.cloned.1.call-start = ((), (), s32[]{:S(2)}) async-start(), calls=%async_computation.14 | async-start | bytes 1310720 | tf_op jit(solution)/shard_map/reduce_scatter | solution.py:267
  287.1 88.1 %reduce-scatter.28.cloned.1.call-start = ((), (), s32[]{:S(2)}) async-start(), calls=%async_computation.21 | async-start | bytes 1802240
  290.4 119.3 %reduce-scatter.30.cloned.1.call-start = ((), (), s32[]{:S(2)}) async-start(), calls=%async_computation.22 | async-start | bytes 1802240
  293.7 139.4 %reduce-scatter.24.cloned.1.call-start = ((), (), s32[]{:S(2)}) async-start(), calls=%async_computation.18 | async-start | bytes 655360 | tf_op jit(solution)/shard_map/reduce_scatter | solution.py:315
  295.7 170.8 %reduce-scatter.26.cloned.1.call-start = ((), (), s32[]{:S(2)}) async-start(), calls=%async_computation.19 | async-start | bytes 1761280 | tf_op jit(solution)/shard_map/reduce_scatter | solution.py:210
  297.7 192.2 %reduce-scatter.18.cloned.1.call-start = ((), (), s32[]{:S(2)}) async-start(), calls=%async_computation.15 | async-start | bytes 655360 | tf_op jit(solution)/shard_map/reduce_scatter | solution.py:306
  316.3 196.6 %reduce-scatter.20.cloned.1.call-start = ((), (), s32[]{:S(2)}) async-start(), calls=%async_computation.16 | async-start | bytes 655360 | tf_op jit(solution)/shard_map/reduce_scatter | solution.py:309
  316.4 26.8 %copy-start.37 = (u32[32]{0:T(128)S(1)}, u32[32]{0:T(128)}, u32[]{:S(2)}) copy-start(u32[32]{0:T(128)} %constant.83) | copy-start | bytes 388
  317.6 218.1 %reduce-scatter.22.cloned.1.call-start = ((), (), s32[]{:S(2)}) async-start(), calls=%async_computation.17 | async-start | bytes 655360 | tf_op jit(solution)/shard_map/reduce_scatter | solution.py:312
  343.1 255.8 %all-reduce.7.cloned.1.call-start = ((), (), s32[]{:S(2)}) async-start(), calls=%async_computation.23 | async-start | bytes 3162112 | tf_op jit(solution)/shard_map/psum | solution.py:82
  (31 other events, 126.6 us)
Sparse Core Ops, SparseCore 0:
  40.0 36.5 all-gather.16
  81.4 31.7 all-gather.8
  114.8 33.6 all-gather.10
  149.9 33.2 all-gather.12
  184.6 32.3 all-gather.14
  286.5 26.2 reduce-scatter.13
  315.1 25.7 reduce-scatter.15
  343.2 31.9 reduce-scatter.27
  377.5 32.1 reduce-scatter.29
  412.4 20.6 reduce-scatter.23
  435.4 31.1 reduce-scatter.25
  469.2 20.6 reduce-scatter.17
  492.7 20.1 reduce-scatter.19
  515.6 20.1 reduce-scatter.21
  539.8 59.1 all-reduce.6
where the time goes:
time: 617 us; the launch traced here: 615 us
  waiting for transfers between devices  327 us (53%)
  blocking collectives  116 us (19%)
  matrix products  104 us (17%)
  local copies, waits for them, and re-layouts  30.9 us (5%)
  other arithmetic  20.6 us (3%)
  between operations  15.1 us (2%)
    unnamed x17, waiting for transfers between devices  62.9 us
    psum x1, waiting for transfers between devices, replica_all(): lax.psum(parts[2].astype(jnp.bfloat16), 'rep').astype(jnp.float32)  38.6 us
    reduce_scatter x1, waiting for transfers between devices, flat_body(): lax.psum_scatter(contract_rows(columns, cot_low).astype(jnp.bfloat16), 'g...  33.5 us
    all_gather x1, waiting for transfers between devices, fetch_mlp(): lax.all_gather(w_up, 'grp', axis=0, tiled=True)  31.7 us
    all_gather x1, waiting for transfers between devices, fetch_mlp(): lax.all_gather(w_down, 'grp', axis=0, tiled=True)  30.8 us
    dot_general x16, matrix products, masked_scores(): jnp.einsum('bqgd,bjd->bgqj', query_head, key_head, preferred_element_type...  25.2 us
    reduce_scatter x1, waiting for transfers between devices, flat_body(): lax.psum_scatter(query_term.astype(jnp.bfloat16), 'grp', scatter_dimensio...  23.4 us
    reduce_scatter x1, waiting for transfers between devices, flat_body(): lax.psum_scatter(value_delta_all.astype(jnp.bfloat16), 'grp', scatter_dim...  23.2 us
  transfers between devices with their start and end apart: 15, of which 13 were waited for; matrix products, arithmetic and copies ran while one was open for 12% of the time, Pallas kernels for 0%

commit v1 on v0

v1 whole, which is shorter than its diff:
```python
import functools

import jax
import jax.numpy as jnp
import numpy as np
from jax import lax
from jax.experimental import pallas as pl
from jax.experimental.pallas import tpu as pltpu
from jax.sharding import PartitionSpec as P

D = 512
H = 8
HD = 64
FF = 1376
EPSILON = 1e-05
NEGATIVE = -1e30
SR = 16
PAIR = 2 * HD
F32 = jnp.float32
BF16 = jnp.bfloat16
VMEM = pl.BlockSpec(memory_space=pltpu.VMEM)
SMEM = pl.BlockSpec(memory_space=pltpu.SMEM)
PARAMS = pltpu.CompilerParams(vmem_limit_bytes=56 * 1024 * 1024)


class Plan:
    def __init__(self, mesh, tokens_shape):
        self.rep = mesh.shape["rep"]
        self.grp = mesh.shape["grp"]
        self.rows = D // self.grp
        self.slices = min(self.rep, self.rows // SR)
        self.half = self.slices // 2
        self.down = FF // self.grp
        self.pieces = -(-self.down // (self.slices * SR))
        self.down_pad = self.pieces * self.slices * SR
        self.ffp = self.down_pad * self.grp
        self.local = tokens_shape[1] // self.grp
        self.full = self.local * self.grp
        self.wide_a = 4 * D + 128
        self.wide_b = 2 * self.ffp + self.pieces * D


def dot(left, right, dims):
    return lax.dot_general(left, right, ((dims[0], dims[1]), ((), ())), preferred_element_type=F32)


def mm(left, right):
    return dot(left, right, ((1,), (0,)))


def against(left, right):
    return dot(left, right, ((1,), (1,)))


def rows_of(left, right):
    return dot(left, right, ((0,), (0,)))


def call(body, outs, name, args, scratch=(), flops=0, moved=0):
    specs = [SMEM if a.dtype == jnp.int32 and a.ndim == 1 else VMEM for a in args]
    return pl.pallas_call(
        body,
        out_shape=outs,
        in_specs=specs,
        out_specs=[VMEM] * len(outs),
        scratch_shapes=scratch,
        compiler_params=PARAMS,
        cost_estimate=pl.CostEstimate(flops=flops, bytes_accessed=moved, transcendentals=0),
        name=name,
    )(*args)


def sds(shape, dtype):
    return jax.ShapeDtypeStruct(shape, dtype)


def swap(axis, k, size, value):
    return lax.ppermute(value, axis, [(i, i ^ k) for i in range(size)])


def shift(k, size, value):
    return lax.ppermute(value, "grp", [(i, i + k) for i in range(size) if 0 <= i + k < size])


def xor(a, b):
    return lax.bitwise_xor(a, jnp.int32(b)) if isinstance(b, int) else lax.bitwise_xor(a, b)


def aligned(index):
    return pl.multiple_of(index, SR)


def rotary_tables(plan):
    halves = HD // 2
    frequency = 10000.0 ** (-2.0 * np.arange(halves) / HD)
    place = np.concatenate([np.arange(plan.local) - k * plan.local for k in range(plan.grp)])
    angle = place[:, None] * frequency[None, :]
    cosine = np.tile(np.cos(angle), (1, 4)).astype(np.float32)
    sines = np.tile(np.concatenate([-np.sin(angle), np.sin(angle)], axis=1), (1, 2))
    return cosine, sines.astype(np.float32)


def swap_halves(value):
    wide = value.shape[1]
    lane = lax.broadcasted_iota(jnp.int32, value.shape, 1)
    first = (lane % HD) < HD // 2
    return jnp.where(
        first, pltpu.roll(value, wide - HD // 2, 1), pltpu.roll(value, HD // 2, 1)
    )


def tile_heads(table, wide):
    return jnp.concatenate([table] * (wide // table.shape[1]), axis=1)


def rotate(value, cosine, sines):
    wide = value.shape[1]
    return value * tile_heads(cosine, wide) + swap_halves(value) * tile_heads(sines, wide)


def rotate_back(value, cosine, sines):
    wide = value.shape[1]
    return value * tile_heads(cosine, wide) - swap_halves(value) * tile_heads(sines, wide)


def two_heads(value):
    lane = lax.broadcasted_iota(jnp.int32, value.shape, 1)
    zero = jnp.zeros_like(value)
    return jnp.concatenate(
        [jnp.where(lane < HD, value, zero), jnp.where(lane < HD, zero, value)], axis=0
    )


def one_pair(value):
    count = value.shape[1] // 2
    return jnp.concatenate([value[:HD, :count], value[HD:, count:]], axis=0).T


def mask_bias(plan, reach, bias_ref):
    n = plan.local
    key = lax.broadcasted_iota(jnp.int32, (n, n), 0)
    query = lax.broadcasted_iota(jnp.int32, (n, n), 1)
    for k in range(plan.grp):
        offset = query - key + k * n
        seen = (offset >= 0) & (offset <= reach)
        bias = jnp.where(seen, 0.0, NEGATIVE).astype(F32)
        bias_ref[k * n : (k + 1) * n, :] = jnp.concatenate([bias, bias], axis=1)


def each_slice(plan, place, slice_id, mine, part, store):
    for c, source in enumerate((mine, part)):
        for o in range(plan.half):
            for k in range(1, plan.grp):
                row = (o * (plan.grp - 1) + k - 1) * SR
                store(xor(place, k), xor(slice_id, 2 * o + c), source[row : row + SR, :])


def attend_kernel(plan, ids, *refs):
    g = plan.grp
    parts = refs[:g]
    own = refs[g : g + 4]
    mine, part, gain, cosine, sines, reach = refs[g + 4 : g + 10]
    attn_ref, q_ref, k_ref, v_ref, n1_ref, lse_ref, wa_ref = refs[g + 10 : g + 17]
    bias_ref, = refs[g + 17 :]
    n = plan.local
    place, slice_id = ids[0], ids[1]
    for i in range(4):
        wa_ref[pl.ds(aligned(place * plan.rows), plan.rows), i * D : (i + 1) * D] = own[i][...]

    def store(z, s, rows):
        wa_ref[pl.ds(aligned(z * plan.rows + s * SR), SR), :] = rows[:, : 4 * D]

    each_slice(plan, place, slice_id, mine, part, store)
    mask_bias(plan, reach[...], bias_ref)
    gains = gain[...]
    for k in range(g):
        x = parts[k][...].astype(F32)
        unit = x * lax.rsqrt(jnp.mean(x * x, axis=1, keepdims=True) + EPSILON)
        n1 = (unit * gains).astype(BF16)
        rows = slice(k * n, (k + 1) * n)
        n1_ref[rows, :] = n1
        cos_k, sin_k = cosine[rows, :], sines[rows, :]
        k_ref[rows, :] = rotate(mm(n1, wa_ref[:, D : 2 * D]), cos_k, sin_k).astype(BF16)
        v_ref[rows, :] = mm(n1, wa_ref[:, 2 * D : 3 * D]).astype(BF16)
        if k == 0:
            q_ref[...] = rotate(mm(n1, wa_ref[:, :D]), cos_k, sin_k).astype(BF16) * BF16(
                HD**-0.5
            )

    def pair(i, carry):
        lanes = pl.ds(pl.multiple_of(i * PAIR, PAIR), PAIR)
        score = against(k_ref[:, lanes], two_heads(q_ref[:, lanes])) + bias_ref[...]
        peak = jnp.max(score, axis=0, keepdims=True)
        exponent = jnp.exp(score - peak)
        total = jnp.sum(exponent, axis=0, keepdims=True)
        out = rows_of(v_ref[:, lanes], exponent.astype(BF16)) / total
        attn_ref[:, lanes] = one_pair(out)
        lse_ref[i] = peak + jnp.log(total)
        return carry

    lax.fori_loop(0, H // 2, pair, 0)


def mlp_kernel(plan, ids, *refs):
    attn, x0, wa, gain, cot, own, mine, part = refs[:8]
    out_ref, dx1_ref, dout_ref, dattn_ref, n2_ref, hid_ref, dg_ref, dup_ref, attn_ref, norm_ref = refs[8:18]
    wgu_ref, wd_ref = refs[18:]
    ffp = plan.ffp
    place, slice_id = ids[0], ids[1]

    def store(z, s, rows):
        wgu_ref[pl.ds(aligned(z * plan.rows + s * SR), SR), :] = rows[:, : 2 * ffp]
        for i in range(plan.pieces):
            at = z * plan.down_pad + (s * plan.pieces + i) * SR
            wd_ref[pl.ds(aligned(at), SR), :] = rows[:, 2 * ffp + i * D : 2 * ffp + (i + 1) * D]

    for s in range(plan.slices):
        store(place, s, own[s * SR : (s + 1) * SR, :])
    each_slice(plan, place, slice_id, mine, part, store)

    attn_low = attn[...].astype(BF16)
    attn_ref[...] = attn_low
    x1 = x0[...].astype(F32) + mm(attn_low, wa[:, 3 * D : 4 * D])
    scale = lax.rsqrt(jnp.mean(x1 * x1, axis=1, keepdims=True) + EPSILON)
    unit = x1 * scale
    gains = gain[...]
    n2 = (unit * gains).astype(BF16)
    n2_ref[...] = n2
    c = cot[...]
    out = x1
    dn2 = jnp.zeros_like(x1)
    step = 512 if ffp % 512 == 0 else ffp
    for f in range(0, ffp, step):
        cols = slice(f, f + step)
        up_cols = slice(ffp + f, ffp + f + step)
        gate = mm(n2, wgu_ref[:, cols])
        up = mm(n2, wgu_ref[:, up_cols])
        dhid = against(c, wd_ref[cols, :])
        sig = 1.0 / (1.0 + jnp.exp(-gate))
        silu = gate * sig
        hid = (silu * up).astype(BF16)
        dup = (dhid * silu).astype(BF16)
        dg = (dhid * up * (sig * (1.0 + gate * (1.0 - sig)))).astype(BF16)
        hid_ref[:, cols] = hid
        dg_ref[:, cols] = dg
        dup_ref[:, cols] = dup
        out = out + mm(hid, wd_ref[cols, :])
        dn2 = dn2 + against(dg, wgu_ref[:, cols]) + against(dup, wgu_ref[:, up_cols])
    out_ref[...] = out.astype(BF16)
    norm_ref[...] = jnp.sum(dn2 * unit, axis=0, keepdims=True)
    e2 = dn2 * gains
    dx1 = c.astype(F32) + scale * (e2 - unit * jnp.mean(e2 * unit, axis=1, keepdims=True))
    dx1_ref[...] = dx1
    dout = dx1.astype(BF16)
    dout_ref[...] = dout
    dattn_ref[...] = against(dout, wa[:, 3 * D : 4 * D]).astype(BF16)


def spread(plan, place, slice_id, keep, send, copy):
    for c, target in enumerate((keep, send)):
        for o in range(plan.half):
            for k in range(plan.grp):
                copy(xor(place, k), xor(slice_id, 2 * o + c), target, o, k)


def mlp_grads_kernel(plan, ids, n2, hid, dg, dup, cot, keep, send, gu_ref, d_ref):
    ffp = plan.ffp
    n2_t = n2[...].T
    gu_ref[:, :ffp] = mm(n2_t, dg[...]).astype(BF16)
    gu_ref[:, ffp:] = mm(n2_t, dup[...]).astype(BF16)
    d_ref[...] = rows_of(hid[...], cot[...]).astype(BF16)

    def copy(z, s, target, o, k):
        target[o, k, :, : 2 * ffp] = gu_ref[pl.ds(aligned(z * plan.rows + s * SR), SR), :]
        for i in range(plan.pieces):
            at = z * plan.down_pad + (s * plan.pieces + i) * SR
            target[o, k, :, 2 * ffp + i * D : 2 * ffp + (i + 1) * D] = d_ref[
                pl.ds(aligned(at), SR), :
            ]

    spread(plan, ids[0], ids[1], keep, send, copy)


def attend_back_kernel(plan, q, k_in, v_in, attn, dattn, lse, cosine, sines, reach, dq_ref, dk_ref, dv_ref, bias_ref, dq_scr, dk_scr):
    mask_bias(plan, reach[...], bias_ref)

    def pair(i, carry):
        lanes = pl.ds(pl.multiple_of(i * PAIR, PAIR), PAIR)
        q2 = two_heads(q[:, lanes])
        da = dattn[:, lanes]
        da2 = two_heads(da)
        prod = two_heads(da.astype(F32) * attn[:, lanes])
        ones = jnp.ones((8, PAIR), F32)
        mean = lax.dot_general(
            ones, prod, (((1,), (1,)), ((), ())), precision=lax.Precision.HIGHEST,
            preferred_element_type=F32,
        )[0:1, :]
        keys = k_in[:, lanes]
        values = v_in[:, lanes]
        prob = jnp.exp(against(keys, q2) + (bias_ref[...] - lse[i]))
        dprob = against(values, da2)
        dscore = (prob * (dprob - mean)).astype(BF16)
        dv_ref[:, lanes] = mm(prob.astype(BF16), da2).astype(BF16)
        dk_scr[:, lanes] = mm(dscore, q2)
        dq_scr[:, lanes] = one_pair(rows_of(keys, dscore)) * (HD**-0.5)
        return carry

    lax.fori_loop(0, H // 2, pair, 0)
    n = plan.local
    dq_ref[...] = rotate_back(dq_scr[...], cosine[:n, :], sines[:n, :]).astype(BF16)
    for k in range(plan.grp):
        rows = slice(k * n, (k + 1) * n)
        dk_ref[rows, :] = rotate_back(dk_scr[rows, :], cosine[rows, :], sines[rows, :]).astype(BF16)


def input_kernel(plan, *refs):
    g = plan.grp
    parts = refs[:g]
    dq, dk, dv, wa = refs[g : g + 4]
    own_ref, norm_ref = refs[g + 4 : g + 6]
    sends = refs[g + 6 :]
    n = plan.local
    norm = jnp.zeros((1, D), F32)
    for k in reversed(range(g)):
        rows = slice(k * n, (k + 1) * n)
        dn1 = against(dk[rows, :], wa[:, D : 2 * D]) + against(dv[rows, :], wa[:, 2 * D : 3 * D])
        if k == 0:
            dn1 = dn1 + against(dq[...], wa[:, :D])
            own_ref[...] = dn1
        else:
            sends[k - 1][...] = dn1.astype(BF16)
        x = parts[k][...].astype(F32)
        unit = x * lax.rsqrt(jnp.mean(x * x, axis=1, keepdims=True) + EPSILON)
        norm = norm + jnp.sum(dn1 * unit, axis=0, keepdims=True)
    norm_ref[...] = norm


def attend_grads_kernel(plan, ids, n1, dq, dk, dv, attn, dout, norms, keep, send, ga_ref):
    n1_t = n1[...].T
    ga_ref[:, :D] = mm(n1_t[:, : plan.local], dq[...]).astype(BF16)
    ga_ref[:, D : 2 * D] = mm(n1_t, dk[...]).astype(BF16)
    ga_ref[:, 2 * D : 3 * D] = mm(n1_t, dv[...]).astype(BF16)
    ga_ref[:, 3 * D :] = rows_of(attn[...], dout[...]).astype(BF16)

    def copy(z, s, target, o, k):
        target[o, k, :, : 4 * D] = ga_ref[pl.ds(aligned(z * plan.rows + s * SR), SR), :]
        flag = (s == 0).astype(F32)
        target[o, k, :, 4 * D :] = (norms[z] * flag).astype(BF16)

    spread(plan, ids[0], ids[1], keep, send, copy)


def finish_kernel(plan, ids, mine, part, out_ref):
    for c, source in enumerate((mine, part)):
        for o in range(plan.half):
            s = xor(ids[1], 2 * o + c)
            out_ref[pl.ds(aligned(s * SR), SR), :] = source[o * SR : (o + 1) * SR, :].astype(F32)


def residual_kernel(plan, *refs):
    own, x0, dx1, gain = refs[:4]
    received = refs[4:-1]
    out_ref = refs[-1]
    dn1 = own[...]
    for r in received:
        dn1 = dn1 + r[...].astype(F32)
    x = x0[...].astype(F32)
    scale = lax.rsqrt(jnp.mean(x * x, axis=1, keepdims=True) + EPSILON)
    unit = x * scale
    e1 = dn1 * gain[...]
    out_ref[...] = dx1[...] + scale * (e1 - unit * jnp.mean(e1 * unit, axis=1, keepdims=True))


def fetch(plan, slab):
    parts = [swap("grp", k, plan.grp, slab) for k in range(1, plan.grp)]
    block = jnp.concatenate(parts, axis=0)
    mine = jnp.concatenate(
        [block] + [swap("rep", 2 * o, plan.rep, block) for o in range(1, plan.half)], axis=0
    )
    return mine, swap("rep", 1, plan.rep, mine)


def add(*values):
    total = values[0].astype(F32)
    for v in values[1:]:
        total = total + v.astype(F32)
    return total.astype(BF16)


def combine(plan, keep, send):
    got = swap("rep", 1, plan.rep, send)
    terms = [add(keep[o], got[o]) for o in range(plan.half)]
    total = add(
        terms[0], *[swap("rep", 2 * o, plan.rep, terms[o]) for o in range(1, plan.half)]
    )
    final = add(total[0], *[swap("grp", k, plan.grp, total[k]) for k in range(1, plan.grp)])
    bit = plan.slices
    while bit < plan.rep:
        final = add(final, swap("rep", bit, plan.rep, final))
        bit *= 2
    mine = jnp.concatenate(
        [final] + [swap("rep", 2 * o, plan.rep, final) for o in range(1, plan.half)], axis=0
    )
    return mine, swap("rep", 1, plan.rep, mine)


def pad_columns(plan, weight):
    rows = weight.shape[0]
    blocks = weight.reshape(rows, plan.grp, plan.down)
    blocks = jnp.pad(blocks, ((0, 0), (0, 0), (0, plan.down_pad - plan.down)))
    return blocks.reshape(rows, plan.ffp)


def drop_columns(plan, grad):
    return jnp.concatenate(
        [grad[:, z * plan.down_pad : z * plan.down_pad + plan.down] for z in range(plan.grp)],
        axis=1,
    )


def body(plan, tokens, segments, positions, norm1_gain, w_query, w_key, w_value, w_out, norm2_gain, w_gate, w_up, w_down, cotangent):
    g, n = plan.grp, plan.local
    place = lax.axis_index("grp").astype(jnp.int32)
    slice_id = (lax.axis_index("rep") % plan.slices).astype(jnp.int32)
    ids = jnp.stack([place, slice_id])
    x0 = tokens.reshape(n, D)
    cot = cotangent.reshape(n, D)
    reach = jnp.where(segments != 0, positions, 0).reshape(1, n)
    table_cos, table_sin = rotary_tables(plan)
    cosine, sines = jnp.asarray(table_cos), jnp.asarray(table_sin)

    gains = jnp.stack([norm1_gain, norm2_gain])
    gain_tile = jnp.pad(gains, ((0, SR - 2), (0, 128 - plan.rows)))
    own_a = (w_query, w_key, w_value, w_out)
    start = slice_id * SR
    slab_a = jnp.concatenate(
        [lax.dynamic_slice(w, (start, 0), (SR, D)) for w in own_a] + [gain_tile], axis=1
    )
    down_rows = jnp.pad(w_down, ((0, plan.down_pad - plan.down), (0, 0)))
    down_rows = down_rows.reshape(plan.slices, plan.pieces, SR, D).transpose(0, 2, 1, 3)
    own_b = jnp.concatenate(
        [
            pad_columns(plan, w_gate),
            pad_columns(plan, w_up),
            down_rows.reshape(plan.rows, plan.pieces * D),
        ],
        axis=1,
    )
    slab_b = lax.dynamic_slice(own_b, (start, 0), (SR, plan.wide_b))

    mine_a, part_a = fetch(plan, slab_a)
    parts = [x0] + [shift(k, g, x0) for k in range(1, g)]
    mine_b, part_b = fetch(plan, slab_b)

    tiles = jnp.stack(
        [gains] + [mine_a[k * SR : k * SR + 2, 4 * D : 4 * D + plan.rows] for k in range(g - 1)]
    )
    order = jnp.bitwise_xor(jnp.arange(g, dtype=jnp.int32), place)
    chosen = sum(
        jnp.where((order == k)[:, None, None], tiles[k][None], 0).astype(F32) for k in range(g)
    )
    gain1 = chosen[:, 0].reshape(1, D)
    gain2 = chosen[:, 1].reshape(1, D)

    full = plan.full
    attn, q, k_all, v_all, n1, lse, wa = call(
        functools.partial(attend_kernel, plan),
        [
            sds((n, D), F32),
            sds((n, D), BF16),
            sds((full, D), BF16),
            sds((full, D), BF16),
            sds((full, D), BF16),
            sds((H // 2, 1, 2 * n), F32),
            sds((D, 4 * D), BF16),
        ],
        "attend",
        (ids, *parts, *own_a, mine_a, part_a, gain1, cosine, sines, reach),
        [pltpu.VMEM((full, 2 * n), F32)],
        flops=4 * 10**9,
        moved=8 * 10**6,
    )

    ffp = plan.ffp
    output, dx1, dout, dattn, n2, hid, dg, dup, attn_low, norm2 = call(
        functools.partial(mlp_kernel, plan),
        [
            sds((n, D), BF16),
            sds((n, D), F32),
            sds((n, D), BF16),
            sds((n, D), BF16),
            sds((n, D), BF16),
            sds((n, ffp), BF16),
            sds((n, ffp), BF16),
            sds((n, ffp), BF16),
            sds((n, D), BF16),
            sds((1, D), F32),
        ],
        "mlp",
        (ids, attn, x0, wa, gain2, cot, own_b, mine_b, part_b),
        [pltpu.VMEM((D, 2 * ffp), BF16), pltpu.VMEM((ffp, D), BF16)],
        flops=4 * 10**9,
        moved=12 * 10**6,
    )

    slabs_b = sds((plan.half, g, SR, plan.wide_b), BF16)
    keep_b, send_b = call(
        functools.partial(mlp_grads_kernel, plan),
        [slabs_b, slabs_b],
        "mlp_grads",
        (ids, n2, hid, dg, dup, cot),
        [pltpu.VMEM((D, 2 * ffp), BF16), pltpu.VMEM((ffp, D), BF16)],
        flops=2 * 10**9,
        moved=8 * 10**6,
    )
    dq, dk, dv = call(
        functools.partial(attend_back_kernel, plan),
        [sds((n, D), BF16), sds((full, D), BF16), sds((full, D), BF16)],
        "attend_back",
        (q, k_all, v_all, attn, dattn, lse, cosine, sines, reach),
        [pltpu.VMEM((full, 2 * n), F32), pltpu.VMEM((n, D), F32), pltpu.VMEM((full, D), F32)],
        flops=8 * 10**9,
        moved=8 * 10**6,
    )
    own, norm1, *sends = call(
        functools.partial(input_kernel, plan),
        [sds((n, D), F32), sds((1, D), F32)] + [sds((n, D), BF16)] * (g - 1),
        "dn1",
        (*parts, dq, dk, dv, wa),
        flops=2 * 10**9,
        moved=4 * 10**6,
    )
    received = [shift(-k, g, sends[k - 1]) for k in range(1, g)]

    norms = jnp.concatenate([norm1, norm2], axis=0).reshape(2, g, plan.rows).transpose(1, 0, 2)
    norms = jnp.pad(norms, ((0, 0), (0, SR - 2), (0, 128 - plan.rows)))
    slabs_a = sds((plan.half, g, SR, plan.wide_a), BF16)
    keep_a, send_a = call(
        functools.partial(attend_grads_kernel, plan),
        [slabs_a, slabs_a],
        "attend_grads",
        (ids, n1, dq, dk, dv, attn_low, dout, norms),
        [pltpu.VMEM((D, 4 * D), BF16)],
        flops=2 * 10**9,
        moved=8 * 10**6,
    )

    def finish(halves, wide, name):
        (out,) = call(
            functools.partial(finish_kernel, plan),
            [sds((plan.slices * SR, wide), F32)],
            name,
            (ids, *halves),
            moved=4 * 10**6,
        )
        return out

    grads_b = finish(combine(plan, keep_b, send_b), plan.wide_b, "finish_b")
    grads_a = finish(combine(plan, keep_a, send_a), plan.wide_a, "finish_a")
    (input_grad,) = call(
        functools.partial(residual_kernel, plan),
        [sds((n, D), F32)],
        "residual",
        (own, x0, dx1, gain1, *received),
        moved=4 * 10**6,
    )
    down = grads_b[:, 2 * ffp :].reshape(plan.slices, SR, plan.pieces, D).transpose(0, 2, 1, 3)
    return (
        output.reshape(tokens.shape),
        input_grad.reshape(tokens.shape),
        grads_a[0, 4 * D : 4 * D + plan.rows],
        grads_a[:, :D],
        grads_a[:, D : 2 * D],
        grads_a[:, 2 * D : 3 * D],
        grads_a[:, 3 * D : 4 * D],
        grads_a[1, 4 * D : 4 * D + plan.rows],
        drop_columns(plan, grads_b[:, :ffp]),
        drop_columns(plan, grads_b[:, ffp : 2 * ffp]),
        down.reshape(plan.down_pad, D)[: plan.down],
    )


def solution(mesh):
    wide, line, pair = P("grp", None), P("grp"), P("rep", "grp")
    three = P("rep", "grp", None)

    def run(tokens, *rest):
        plan = Plan(mesh, tokens.shape)
        return jax.shard_map(
            functools.partial(body, plan),
            mesh=mesh,
            in_specs=(three, pair, pair, line, wide, wide, wide, wide, line, wide, wide, wide, three),
            out_specs=(three, three, line, wide, wide, wide, wide, line, wide, wide, wide),
            check_vma=False,
        )(tokens, *rest)

    return run
```

time: 617 us -> 261 us (0.42)
  waiting for transfers between devices: 327 us -> 99.5 us
  blocking collectives: 116 us -> 0 us
  matrix products: 104 us -> 0 us
  starting transfers between devices: 0.78 us -> 77.5 us
  Pallas kernels: 0 us -> 55.8 us
  other arithmetic: 20.6 us -> 4.02 us
  between operations: 15.1 us -> 1.28 us
  local copies, waits for them, and re-layouts: 30.9 us -> 22.2 us
    reduce_scatter x7 -> x0, waiting for transfers between devices: 162 us -> none  [the longest x1 33.5 us: flat_body(): lax.psum_scatter(contract_rows(columns, cot_low).astype(jnp.bfloat16), 'g...]
    dot_general x77 -> x0, matrix products: 104 us -> none  [the longest x16 25.2 us: masked_scores(): jnp.einsum('bqgd,bjd->bgqj', query_head, key_head, preferred_element_type...]
    ppermute x0 -> x42, waiting for transfers between devices: none -> 99.5 us  [the longest x36 91.7 us: swap(): return lax.ppermute(value, axis, [(i, i ^ k) for i in range(size)])]
    all_gather x6 -> x0, blocking collectives: 95.9 us -> none  [the longest x1 19.7 us: fetch_attention(): lax.all_gather(w_key, 'grp', axis=0, tiled=True)]
    ppermute x0 -> x42, starting transfers between devices: none -> 77.5 us  [the longest x36 64 us: swap(): return lax.ppermute(value, axis, [(i, i ^ k) for i in range(size)])]
    unnamed x17 -> x0, waiting for transfers between devices: 62.9 us -> none
    all_gather x5 -> x0, waiting for transfers between devices: 62.8 us -> none  [the longest x1 31.7 us: fetch_mlp(): lax.all_gather(w_up, 'grp', axis=0, tiled=True)]
    pallas_call x0 -> x9, Pallas kernels: none -> 55.8 us  [call(): pl.pallas_call(body, out_shape=outs, in_specs=specs, out_specs=[VMEM] * l...]
  transfers between devices with their start and end apart: 15 -> 42, of which waited for: 13 -> 19; matrix products, arithmetic and copies ran while one was open for 12% -> 4% of each run, Pallas kernels for 0% -> 8%
where the time goes in v1:
time: 261 us; the launch traced here: 260 us
  waiting for transfers between devices  99.5 us (38%)
  starting transfers between devices  77.5 us (30%)
  Pallas kernels  55.8 us (21%)
  local copies, waits for them, and re-layouts  22.2 us (9%)
  other arithmetic  4.02 us (2%)
    ppermute x36, waiting for transfers between devices, swap(): return lax.ppermute(value, axis, [(i, i ^ k) for i in range(size)])  91.7 us
    ppermute x36, starting transfers between devices, swap(): return lax.ppermute(value, axis, [(i, i ^ k) for i in range(size)])  64 us
    pallas_call x9, Pallas kernels, call(): pl.pallas_call(body, out_shape=outs, in_specs=specs, out_specs=[VMEM] * l...  55.8 us
    ppermute x6, starting transfers between devices, shift(): lax.ppermute(value, 'grp', [(i, i + k) for i in range(size) if 0 <= i + k...  13.5 us
    unnamed x71, local copies, waits for them, and re-layouts  11.3 us
    ppermute x6, waiting for transfers between devices, shift(): lax.ppermute(value, 'grp', [(i, i + k) for i in range(size) if 0 <= i + k...  7.82 us
  transfers between devices with their start and end apart: 42, of which 19 were waited for; matrix products, arithmetic and copies ran while one was open for 4% of the time, Pallas kernels for 8%

profile of v1, /device:TPU:0, one launch (start us, length us, event | category | flops | bytes accessed | tf_op | source)
XLA Modules:
  0.0 260.3 jit_solution(7194789257010967281)
XLA Ops:
  4.3 5.1 %collective-permute-start.5 = (bf16[16,2176]{1,0:T(8,128)(2,1)S(1)}, bf16[16,2176]{1,0:T(8,128)(2,1)S(1)}, u32[]{:S(2)}, u32[]{:S(2)}) collective-permute-start(bf16[16,2176]{1,0:T(8,128)(2,1)S(1)} %constant_dynamic-update-slice_fusion), channel_id=1, source_target_pairs={{0,3},{1,2},{2,1},{3,0},{4,7},{5,6},{6,5},{7,4},{8,11},{9,10},{10,... | collective-permute-start | bytes 208904 | tf_op jit(solution)/shard_map/ppermute | solution.py:78
  10.0 5.7 %collective-permute-start.2 = (bf16[256,512]{1,0:T(8,128)(2,1)}, bf16[256,512]{1,0:T(8,128)(2,1)S(1)}, u32[]{:S(2)}, u32[]{:S(2)}) collective-permute-start(bf16[256,512]{1,0:T(8,128)(2,1)} %bitcast.87), channel_id=1, source_target_pairs={{0,3},{4,7},{8,11},{12,15},{16,19},{20,23},{24,27},{28,31}} | collective-permute-start | bytes 786440 | tf_op jit(solution)/shard_map/ppermute | solution.py:82
  23.6 14.6 %collective-permute-done.10 = bf16[16,4608]{1,0:T(8,128)(2,1)S(1)} collective-permute-done((bf16[16,4608]{1,0:T(8,128)(2,1)S(1)}, bf16[16,4608]{1,0:T(8,128)(2,1)S(1)}, u32[]{:S(2)}, u32[]{:S(2)}) %collective-permute-start.10) | collective-permute-done | bytes 147488 | tf_op jit(solution)/shard_map/ppermute | solution.py:78
  40.9 6.5 %collective-permute-done.11 = bf16[16,4608]{1,0:T(8,128)(2,1)S(1)} collective-permute-done((bf16[16,4608]{1,0:T(8,128)(2,1)S(1)}, bf16[16,4608]{1,0:T(8,128)(2,1)S(1)}, u32[]{:S(2)}, u32[]{:S(2)}) %collective-permute-start.11) | collective-permute-done | bytes 147488 | tf_op jit(solution)/shard_map/ppermute | solution.py:78
  49.5 5.9 %collective-permute-done.6 = bf16[48,2176]{1,0:T(8,128)(2,1)S(1)} collective-permute-done((bf16[48,2176]{1,0:T(8,128)(2,1)S(1)}, bf16[48,2176]{1,0:T(8,128)(2,1)S(1)}, u32[]{:S(2)}, u32[]{:S(2)}) %collective-permute-start.6) | collective-permute-done | bytes 208928 | tf_op jit(solution)/shard_map/ppermute | solution.py:78
  57.9 3.1 %collective-permute-done.13 = bf16[48,4608]{1,0:T(8,128)(2,1)S(1)} collective-permute-done((bf16[48,4608]{1,0:T(8,128)(2,1)S(1)}, bf16[48,4608]{1,0:T(8,128)(2,1)S(1)}, u32[]{:S(2)}, u32[]{:S(2)}) %collective-permute-start.13) | collective-permute-done | bytes 442400 | tf_op jit(solution)/shard_map/ppermute | solution.py:78
  62.6 13.5 %collective-permute-done.14 = bf16[48,4608]{1,0:T(8,128)(2,1)S(1)} collective-permute-done((bf16[48,4608]{1,0:T(8,128)(2,1)S(1)}, bf16[48,4608]{1,0:T(8,128)(2,1)S(1)}, u32[]{:S(2)}, u32[]{:S(2)}) %collective-permute-start.14) | collective-permute-done | bytes 442400 | tf_op jit(solution)/shard_map/ppermute | solution.py:78
  78.7 6.5 %collective-permute-done.15 = bf16[48,4608]{1,0:T(8,128)(2,1)S(1)} collective-permute-done((bf16[48,4608]{1,0:T(8,128)(2,1)S(1)}, bf16[48,4608]{1,0:T(8,128)(2,1)S(1)}, u32[]{:S(2)}, u32[]{:S(2)}) %collective-permute-start.15) | collective-permute-done | bytes 442400 | tf_op jit(solution)/shard_map/ppermute | solution.py:78
  87.0 4.0 %collective-permute-done.7 = bf16[48,2176]{1,0:T(8,128)(2,1)S(1)} collective-permute-done((bf16[48,2176]{1,0:T(8,128)(2,1)S(1)}, bf16[48,2176]{1,0:T(8,128)(2,1)S(1)}, u32[]{:S(2)}, u32[]{:S(2)}) %collective-permute-start.7) | collective-permute-done | bytes 208928 | tf_op jit(solution)/shard_map/ppermute | solution.py:78
  96.9 11.4 %attend.1 = (f32[256,512]{1,0:T(8,128)}, bf16[256,512]{1,0:T(8,128)(2,1)}, bf16[1024,512]{1,0:T(8,128)(2,1)}, bf16[1024,512]{1,0:T(8,128)(2,1)}, bf16[1024,512]{...) custom-call(s32[2]{0:T(128)} %pad_add_fusion.ids, bf16[256,512]{1,0:T(8,128)(2,1)} %bitcast.89, ...), custom_call_target="tpu_custom_call" | custom-call | flops 4000000000 | bytes 8000000 | tf_op jit(solution)/shard_map/attend/pallas_call | solution.py:61
  109.6 8.4 %mlp.1 = (bf16[256,512]{1,0:T(8,128)(2,1)}, f32[256,512]{1,0:T(8,128)}, bf16[256,512]{1,0:T(8,128)(2,1)}, bf16[256,512]{1,0:T(8,128)(2,1)}, bf16[256,512]{1,0:T(...) custom-call(s32[2]{0:T(128)} %pad_add_fusion.ids, ...), custom_call_target="tpu_custom_call" | custom-call | flops 4000000000 | bytes 12000000 | tf_op jit(solution)/shard_map/mlp/pallas_call | solution.py:61
  118.0 12.6 %attend_back.1 = (bf16[256,512]{1,0:T(8,128)(2,1)}, bf16[1024,512]{1,0:T(8,128)(2,1)}, bf16[1024,512]{1,0:T(8,128)(2,1)}) custom-call(bf16[256,512]{1,0:T(8,128)(2,1)} %get-tuple-element.43.q, bf16[1024,512]{1,0:T(8,128)(2,1)} %get-tuple-element.44.k_in, bf16[1024,512]{1,0:T(8,128)(2,1)} %get-tuple-element.45.v_in, ...), custom_call_target="tpu_custom_call" | custom-call | flops 8000000000 | bytes 8000000 | tf_op jit(solution)/shard_map/attend_back/pallas_call | solution.py:61
  130.6 5.0 %dn1.1 = (f32[256,512]{1,0:T(8,128)}, f32[1,512]{1,0:T(1,128)}, bf16[256,512]{1,0:T(8,128)(2,1)}, bf16[256,512]{1,0:T(8,128)(2,1)}, bf16[256,512]{1,0:T(8,128)(2,1)}) custom-call(bf16[256,512]{1,0:T(8,128)(2,1)} %bitcast.91, bf16[256,512]{1,0:T(8,128)(2,1)} %copy-done.25, bf16[256,512]{1,0:T(8,128)(2,1)} %copy-done.22, bf16[256,512]{1,0:T(8,128)(2,1)} %copy-done.20, ...), custom_call_target="tpu_custom_call" | custom-call | flops 2000000000 | bytes 4000000 | tf_op jit(solution)/shard_map/dn1/pallas_call | solution.py:61
  136.9 5.1 %attend_grads.1 = (bf16[4,4,16,2176]{3,2,1,0:T(8,128)(2,1)}, bf16[4,4,16,2176]{3,2,1,0:T(8,128)(2,1)}) custom-call(s32[2]{0:T(128)} %pad_add_fusion.ids, bf16[1024,512]{1,0:T(8,128)(2,1)} %get-tuple-element.56.n1, bf16[256,512]{1,0:T(8,128)(2,1)} %get-tuple-element.48.refs_4_.dq, bf16[1024,512]{1,0:T(8,128)(2,1)} %get-tuple-element.49.refs_5_.dk, ...), custom_call_target="tpu_custom_call" | custom-call | flops 2000000000 | bytes 8000000 | tf_op jit(solution)/shard_map/attend_grads/pallas_call | solution.py:61
  142.1 5.7 %mlp_grads.1 = (bf16[4,4,16,4608]{3,2,1,0:T(8,128)(2,1)}, bf16[4,4,16,4608]{3,2,1,0:T(8,128)(2,1)}) custom-call(s32[2]{0:T(128)} %pad_add_fusion.ids, bf16[256,512]{1,0:T(8,128)(2,1)} %get-tuple-element.63.n2, bf16[256,1536]{1,0:T(8,128)(2,1)} %get-tuple-element.64.hid, bf16[256,1536]{1,0:T(8,128)(2,1)} %get-tuple-element.65.dg, ...), custom_call_target="tpu_custom_call" | custom-call | flops 2000000000 | bytes 8000000 | tf_op jit(solution)/shard_map/mlp_grads/pallas_call | solution.py:61
  153.2 4.7 %collective-permute-done.21 = bf16[4,16,2176]{2,1,0:T(8,128)(2,1)S(1)} collective-permute-done((bf16[4,16,2176]{2,1,0:T(8,128)(2,1)S(1)}, bf16[4,16,2176]{2,1,0:T(8,128)(2,1)S(1)}, u32[]{:S(2)}, u32[]{:S(2)}) %collective-permute-start.21) | collective-permute-done | bytes 278560 | tf_op jit(solution)/shard_map/ppermute | solution.py:78
  159.3 5.1 %collective-permute-done.23 = bf16[4,16,2176]{2,1,0:T(8,128)(2,1)S(1)} collective-permute-done((bf16[4,16,2176]{2,1,0:T(8,128)(2,1)S(1)}, bf16[4,16,2176]{2,1,0:T(8,128)(2,1)S(1)}, u32[]{:S(2)}, u32[]{:S(2)}) %collective-permute-start.23) | collective-permute-done | bytes 278560 | tf_op jit(solution)/shard_map/ppermute | solution.py:78
  169.9 12.7 %collective-permute-done.32 = bf16[4,16,4608]{2,1,0:T(8,128)(2,1)S(1)} collective-permute-done((bf16[4,16,4608]{2,1,0:T(8,128)(2,1)S(1)}, bf16[4,16,4608]{2,1,0:T(8,128)(2,1)S(1)}, u32[]{:S(2)}, u32[]{:S(2)}) %collective-permute-start.32) | collective-permute-done | bytes 589856 | tf_op jit(solution)/shard_map/ppermute | solution.py:78
  182.6 10.0 %collective-permute-start.24 = (bf16[16,2176]{1,0:T(8,128)(2,1)S(1)}, bf16[16,2176]{1,0:T(8,128)(2,1)S(1)}, u32[]{:S(2)}, u32[]{:S(2)}) collective-permute-start(bf16[16,2176]{1,0:T(8,128)(2,1)S(1)} %get-tuple-element.125), channel_id=1, source_target_pairs={{0,1},{1,0},{2,3},{3,2},{4,5},{5,4},{6,7},{7,6},{8,9},{9,8},{10,11... | collective-permute-start | bytes 208904 | tf_op jit(solution)/shard_map/ppermute | solution.py:78
  192.6 13.2 %collective-permute-start.26 = (bf16[16,2176]{1,0:T(8,128)(2,1)S(1)}, bf16[16,2176]{1,0:T(8,128)(2,1)S(1)}, u32[]{:S(2)}, u32[]{:S(2)}) collective-permute-start(bf16[16,2176]{1,0:T(8,128)(2,1)S(1)} %get-tuple-element.126), channel_id=1, source_target_pairs={{0,3},{1,2},{2,1},{3,0},{4,7},{5,6},{6,5},{7,4},{8,11},{9,10},{10,... | collective-permute-start | bytes 208904 | tf_op jit(solution)/shard_map/ppermute | solution.py:78
  208.5 3.4 %collective-permute-start.37 = (bf16[16,4608]{1,0:T(8,128)(2,1)S(1)}, bf16[16,4608]{1,0:T(8,128)(2,1)S(1)}, u32[]{:S(2)}, u32[]{:S(2)}) collective-permute-start(bf16[16,4608]{1,0:T(8,128)(2,1)S(1)} %get-tuple-element.123), channel_id=1, source_target_pairs={{0,3},{1,2},{2,1},{3,0},{4,7},{5,6},{6,5},{7,4},{8,11},{9,10},{10,... | collective-permute-start | bytes 442376 | tf_op jit(solution)/shard_map/ppermute | solution.py:78
  212.0 3.0 %collective-permute-done.25 = bf16[16,2176]{1,0:T(8,128)(2,1)S(1)} collective-permute-done((bf16[16,2176]{1,0:T(8,128)(2,1)S(1)}, bf16[16,2176]{1,0:T(8,128)(2,1)S(1)}, u32[]{:S(2)}, u32[]{:S(2)}) %collective-permute-start.25) | collective-permute-done | bytes 69664 | tf_op jit(solution)/shard_map/ppermute | solution.py:78
  218.0 4.4 %collective-permute-done.36 = bf16[16,4608]{1,0:T(8,128)(2,1)S(1)} collective-permute-done((bf16[16,4608]{1,0:T(8,128)(2,1)S(1)}, bf16[16,4608]{1,0:T(8,128)(2,1)S(1)}, u32[]{:S(2)}, u32[]{:S(2)}) %collective-permute-start.36) | collective-permute-done | bytes 147488 | tf_op jit(solution)/shard_map/ppermute | solution.py:78
  233.1 7.8 %collective-permute-done.19.refs_6_ = bf16[256,512]{1,0:T(8,128)(2,1)S(1)} collective-permute-done((bf16[256,512]{1,0:T(8,128)(2,1)S(1)}, bf16[256,512]{1,0:T(8,128)(2,1)S(1)}, u32[]{:S(2)}, u32[]{:S(2)}) %collective-permute-start.19) | collective-permute-done | bytes 262176 | tf_op jit(solution)/shard_map/ppermute | solution.py:82
  (185 shorter events, 81.6 us)
Async XLA Ops:
  4.3 19.2 %collective-permute-start.5 = (bf16[16,2176]{1,0:T(8,128)(2,1)S(1)}, bf16[16,2176]{1,0:T(8,128)(2,1)S(1)}, u32[]{:S(2)}, u32[]{:S(2)}) collective-permute-start(bf16[16,2176]{1,0:T(8,128)(2,1)S(1)} %constant_dynamic-update-slice_fusion), channel_id=1, source_target_pairs={{0,3},{1,2},{2,1},{3,0},{4,7},{5,6},{6,5},{7,4},{8,11},{9,10},{10,... | collective-permute-start | bytes 208904 | tf_op jit(solution)/shard_map/ppermute | solution.py:78
  9.4 14.0 %collective-permute-start.4 = (bf16[16,2176]{1,0:T(8,128)(2,1)S(1)}, bf16[16,2176]{1,0:T(8,128)(2,1)S(1)}, u32[]{:S(2)}, u32[]{:S(2)}) collective-permute-start(bf16[16,2176]{1,0:T(8,128)(2,1)S(1)} %constant_dynamic-update-slice_fusion), channel_id=1, source_target_pairs={{0,2},{1,3},{2,0},{3,1},{4,6},{5,7},{6,4},{7,5},{8,10},{9,11},{10,... | collective-permute-start | bytes 208904 | tf_op jit(solution)/shard_map/ppermute | solution.py:78
  9.4 10.7 %collective-permute-start.3 = (bf16[16,2176]{1,0:T(8,128)(2,1)S(1)}, bf16[16,2176]{1,0:T(8,128)(2,1)S(1)}, u32[]{:S(2)}, u32[]{:S(2)}) collective-permute-start(bf16[16,2176]{1,0:T(8,128)(2,1)S(1)} %constant_dynamic-update-slice_fusion), channel_id=1, source_target_pairs={{0,1},{1,0},{2,3},{3,2},{4,5},{5,4},{6,7},{7,6},{8,9},{9,8},{10,11... | collective-permute-start | bytes 208904 | tf_op jit(solution)/shard_map/ppermute | solution.py:78
  10.0 83.6 %collective-permute-start.2 = (bf16[256,512]{1,0:T(8,128)(2,1)}, bf16[256,512]{1,0:T(8,128)(2,1)S(1)}, u32[]{:S(2)}, u32[]{:S(2)}) collective-permute-start(bf16[256,512]{1,0:T(8,128)(2,1)} %bitcast.87), channel_id=1, source_target_pairs={{0,3},{4,7},{8,11},{12,15},{16,19},{20,23},{24,27},{28,31}} | collective-permute-start | bytes 786440 | tf_op jit(solution)/shard_map/ppermute | solution.py:82
  15.7 77.9 %collective-permute-start.1 = (bf16[256,512]{1,0:T(8,128)(2,1)}, bf16[256,512]{1,0:T(8,128)(2,1)S(1)}, u32[]{:S(2)}, u32[]{:S(2)}) collective-permute-start(bf16[256,512]{1,0:T(8,128)(2,1)} %bitcast.88), channel_id=1, source_target_pairs={{0,2},{1,3},{4,6},{5,7},{8,10},{9,11},{12,14},{13,15},{16,18},{17,... | collective-permute-start | bytes 786440 | tf_op jit(solution)/shard_map/ppermute | solution.py:82
  20.9 72.8 %collective-permute-start = (bf16[256,512]{1,0:T(8,128)(2,1)S(1)}, bf16[256,512]{1,0:T(8,128)(2,1)S(1)}, u32[]{:S(2)}, u32[]{:S(2)}) collective-permute-start(bf16[256,512]{1,0:T(8,128)(2,1)S(1)} %bitcast.93), channel_id=1, source_target_pairs={{0,1},{1,2},{2,3},{4,5},{5,6},{6,7},{8,9},{9,10},{10,11},{12,13},{... | collective-permute-start | bytes 786440 | tf_op jit(solution)/shard_map/ppermute | solution.py:82
  23.4 25.5 %collective-permute-start.12 = (bf16[16,4608]{1,0:T(8,128)(2,1)S(1)}, bf16[16,4608]{1,0:T(8,128)(2,1)S(1)}, u32[]{:S(2)}, u32[]{:S(2)}) collective-permute-start(bf16[16,4608]{1,0:T(8,128)(2,1)S(1)} %constant_dynamic-slice_fusion), channel_id=1, source_target_pairs={{0,3},{1,2},{2,1},{3,0},{4,7},{5,6},{6,5},{7,4},{8,11},{9,10},{10,... | collective-permute-start | bytes 442376 | tf_op jit(solution)/shard_map/ppermute | solution.py:78
  23.5 14.7 %collective-permute-start.10 = (bf16[16,4608]{1,0:T(8,128)(2,1)S(1)}, bf16[16,4608]{1,0:T(8,128)(2,1)S(1)}, u32[]{:S(2)}, u32[]{:S(2)}) collective-permute-start(bf16[16,4608]{1,0:T(8,128)(2,1)S(1)} %constant_dynamic-slice_fusion), channel_id=1, source_target_pairs={{0,1},{1,0},{2,3},{3,2},{4,5},{5,4},{6,7},{7,6},{8,9},{9,8},{10,11... | collective-permute-start | bytes 442376 | tf_op jit(solution)/shard_map/ppermute | solution.py:78
  48.9 12.1 %collective-permute-start.13 = (bf16[48,4608]{1,0:T(8,128)(2,1)S(1)}, bf16[48,4608]{1,0:T(8,128)(2,1)S(1)}, u32[]{:S(2)}, u32[]{:S(2)}) collective-permute-start(bf16[48,4608]{1,0:T(8,128)(2,1)S(1)} %get-tuple-element.128), channel_id=1, source_target_pairs={{0,8},{4,12},{8,0},{12,4},{16,24},{20,28},{24,16},{28,20},{1,9},{5... | collective-permute-start | bytes 1327112 | tf_op jit(solution)/shard_map/ppermute | solution.py:78
  55.4 35.7 %collective-permute-start.8 = (bf16[48,2176]{1,0:T(8,128)(2,1)S(1)}, bf16[48,2176]{1,0:T(8,128)(2,1)S(1)}, u32[]{:S(2)}, u32[]{:S(2)}) collective-permute-start(bf16[48,2176]{1,0:T(8,128)(2,1)S(1)} %get-tuple-element.134), channel_id=1, source_target_pairs={{0,24},{4,28},{8,16},{12,20},{16,8},{20,12},{24,0},{28,4},{1,25},{... | collective-permute-start | bytes 626696 | tf_op jit(solution)/shard_map/ppermute | solution.py:78
  61.0 15.1 %collective-permute-start.14 = (bf16[48,4608]{1,0:T(8,128)(2,1)S(1)}, bf16[48,4608]{1,0:T(8,128)(2,1)S(1)}, u32[]{:S(2)}, u32[]{:S(2)}) collective-permute-start(bf16[48,4608]{1,0:T(8,128)(2,1)S(1)} %get-tuple-element.128), channel_id=1, source_target_pairs={{0,16},{4,20},{8,24},{12,28},{16,0},{20,4},{24,8},{28,12},{1,17},{... | collective-permute-start | bytes 1327112 | tf_op jit(solution)/shard_map/ppermute | solution.py:78
  91.1 17.2 %collective-permute-start.16 = (bf16[192,4608]{1,0:T(8,128)(2,1)S(1)}, bf16[192,4608]{1,0:T(8,128)(2,1)S(1)}, u32[]{:S(2)}, u32[]{:S(2)}) collective-permute-start(bf16[192,4608]{1,0:T(8,128)(2,1)S(1)} %constant_dynamic-update-slice_fusion.20.refs_6_), channel_id=1, source_target_pairs={{0,4},{4,0},{8,12},{12,8},{16,20},{20,16},{24,28},{28,24},{1,5},{5... | collective-permute-start | bytes 5308424 | tf_op jit(solution)/shard_map/ppermute | solution.py:78
  147.8 18.1 %collective-permute-start.31 = (bf16[4,4,16,4608]{3,2,1,0:T(8,128)(2,1)}, bf16[4,4,16,4608]{3,2,1,0:T(8,128)(2,1)S(1)}, u32[]{:S(2)}, u32[]{:S(2)}) collective-permute-start(bf16[4,4,16,4608]{3,2,1,0:T(8,128)(2,1)} %get-tuple-element.68), channel_id=1, source_target_pairs={{0,4},{4,0},{8,12},{12,8},{16,20},{20,16},{24,28},{28,24},{1,5},{5... | collective-permute-start | bytes 7077896 | tf_op jit(solution)/shard_map/ppermute | solution.py:78
  149.9 14.4 %collective-permute-start.23 = (bf16[4,16,2176]{2,1,0:T(8,128)(2,1)S(1)}, bf16[4,16,2176]{2,1,0:T(8,128)(2,1)S(1)}, u32[]{:S(2)}, u32[]{:S(2)}) collective-permute-start(bf16[4,16,2176]{2,1,0:T(8,128)(2,1)S(1)} %get-tuple-element.114), channel_id=1, source_target_pairs={{0,24},{4,28},{8,16},{12,20},{16,8},{20,12},{24,0},{28,4},{1,25},{... | collective-permute-start | bytes 835592 | tf_op jit(solution)/shard_map/ppermute | solution.py:78
  151.6 14.1 %collective-permute-start.22 = (bf16[4,16,2176]{2,1,0:T(8,128)(2,1)S(1)}, bf16[4,16,2176]{2,1,0:T(8,128)(2,1)S(1)}, u32[]{:S(2)}, u32[]{:S(2)}) collective-permute-start(bf16[4,16,2176]{2,1,0:T(8,128)(2,1)S(1)} %get-tuple-element.115), channel_id=1, source_target_pairs={{0,16},{4,20},{8,24},{12,28},{16,0},{20,4},{24,8},{28,12},{1,17},{... | collective-permute-start | bytes 835592 | tf_op jit(solution)/shard_map/ppermute | solution.py:78
  151.9 81.2 %collective-permute-start.17 = (bf16[256,512]{1,0:T(8,128)(2,1)S(1)}, bf16[256,512]{1,0:T(8,128)(2,1)S(1)}, u32[]{:S(2)}, u32[]{:S(2)}) collective-permute-start(bf16[256,512]{1,0:T(8,128)(2,1)S(1)} %copy-done.24), channel_id=1, source_target_pairs={{1,0},{2,1},{3,2},{5,4},{6,5},{7,6},{9,8},{10,9},{11,10},{13,12},{... | collective-permute-start | bytes 786440 | tf_op jit(solution)/shard_map/ppermute | solution.py:82
  158.0 75.1 %collective-permute-start.18 = (bf16[256,512]{1,0:T(8,128)(2,1)S(1)}, bf16[256,512]{1,0:T(8,128)(2,1)S(1)}, u32[]{:S(2)}, u32[]{:S(2)}) collective-permute-start(bf16[256,512]{1,0:T(8,128)(2,1)S(1)} %copy-done.23), channel_id=1, source_target_pairs={{2,0},{3,1},{6,4},{7,5},{10,8},{11,9},{14,12},{15,13},{18,16},{19,... | collective-permute-start | bytes 786440 | tf_op jit(solution)/shard_map/ppermute | solution.py:82
  166.4 16.3 %collective-permute-start.32 = (bf16[4,16,4608]{2,1,0:T(8,128)(2,1)S(1)}, bf16[4,16,4608]{2,1,0:T(8,128)(2,1)S(1)}, u32[]{:S(2)}, u32[]{:S(2)}) collective-permute-start(bf16[4,16,4608]{2,1,0:T(8,128)(2,1)S(1)} %get-tuple-element.102), channel_id=1, source_target_pairs={{0,8},{4,12},{8,0},{12,4},{16,24},{20,28},{24,16},{28,20},{1,9},{5... | collective-permute-start | bytes 1769480 | tf_op jit(solution)/shard_map/ppermute | solution.py:78
  167.9 24.7 %collective-permute-start.34 = (bf16[4,16,4608]{2,1,0:T(8,128)(2,1)S(1)}, bf16[4,16,4608]{2,1,0:T(8,128)(2,1)S(1)}, u32[]{:S(2)}, u32[]{:S(2)}) collective-permute-start(bf16[4,16,4608]{2,1,0:T(8,128)(2,1)S(1)} %get-tuple-element.103), channel_id=1, source_target_pairs={{0,24},{4,28},{8,16},{12,20},{16,8},{20,12},{24,0},{28,4},{1,25},{... | collective-permute-start | bytes 1769480 | tf_op jit(solution)/shard_map/ppermute | solution.py:78
  168.2 37.6 %collective-permute-start.33 = (bf16[4,16,4608]{2,1,0:T(8,128)(2,1)S(1)}, bf16[4,16,4608]{2,1,0:T(8,128)(2,1)S(1)}, u32[]{:S(2)}, u32[]{:S(2)}) collective-permute-start(bf16[4,16,4608]{2,1,0:T(8,128)(2,1)S(1)} %get-tuple-element.104), channel_id=1, source_target_pairs={{0,16},{4,20},{8,24},{12,28},{16,0},{20,4},{24,8},{28,12},{1,17},{... | collective-permute-start | bytes 1769480 | tf_op jit(solution)/shard_map/ppermute | solution.py:78
  182.6 23.6 %collective-permute-start.24 = (bf16[16,2176]{1,0:T(8,128)(2,1)S(1)}, bf16[16,2176]{1,0:T(8,128)(2,1)S(1)}, u32[]{:S(2)}, u32[]{:S(2)}) collective-permute-start(bf16[16,2176]{1,0:T(8,128)(2,1)S(1)} %get-tuple-element.125), channel_id=1, source_target_pairs={{0,1},{1,0},{2,3},{3,2},{4,5},{5,4},{6,7},{7,6},{8,9},{9,8},{10,11... | collective-permute-start | bytes 208904 | tf_op jit(solution)/shard_map/ppermute | solution.py:78
  192.6 15.9 %collective-permute-start.26 = (bf16[16,2176]{1,0:T(8,128)(2,1)S(1)}, bf16[16,2176]{1,0:T(8,128)(2,1)S(1)}, u32[]{:S(2)}, u32[]{:S(2)}) collective-permute-start(bf16[16,2176]{1,0:T(8,128)(2,1)S(1)} %get-tuple-element.126), channel_id=1, source_target_pairs={{0,3},{1,2},{2,1},{3,0},{4,7},{5,6},{6,5},{7,4},{8,11},{9,10},{10,... | collective-permute-start | bytes 208904 | tf_op jit(solution)/shard_map/ppermute | solution.py:78
  232.4 11.9 %collective-permute-start.30 = (bf16[64,2176]{1,0:T(8,128)(2,1)S(1)}, bf16[64,2176]{1,0:T(8,128)(2,1)S(1)}, u32[]{:S(2)}, u32[]{:S(2)}) collective-permute-start(bf16[64,2176]{1,0:T(8,128)(2,1)S(1)} %pad_maximum_fusion.1.mine), channel_id=1, source_target_pairs={{0,4},{4,0},{8,12},{12,8},{16,20},{20,16},{24,28},{28,24},{1,5},{5... | collective-permute-start | bytes 835592 | tf_op jit(solution)/shard_map/ppermute | solution.py:78
  232.6 17.9 %collective-permute-start.41 = (bf16[64,4608]{1,0:T(8,128)(2,1)S(1)}, bf16[64,4608]{1,0:T(8,128)(2,1)S(1)}, u32[]{:S(2)}, u32[]{:S(2)}) collective-permute-start(bf16[64,4608]{1,0:T(8,128)(2,1)S(1)} %pad_maximum_fusion.mine), channel_id=1, source_target_pairs={{0,4},{4,0},{8,12},{12,8},{16,20},{20,16},{24,28},{28,24},{1,5},{5... | collective-permute-start | bytes 1769480 | tf_op jit(solution)/shard_map/ppermute | solution.py:78
  (45 other events, 413.3 us)

commit v2 on v1

--- a/solution.py
+++ b/solution.py
@@ -65,7 +65,7 @@
         out_specs=[VMEM] * len(outs),
         scratch_shapes=scratch,
         compiler_params=PARAMS,
-        cost_estimate=pl.CostEstimate(flops=flops, bytes_accessed=moved, transcendentals=0),
+        cost_estimate=pl.CostEstimate(flops=0, bytes_accessed=0, transcendentals=0),
         name=name,
     )(*args)
 
@@ -153,6 +153,73 @@
             for k in range(1, plan.grp):
                 row = (o * (plan.grp - 1) + k - 1) * SR
                 store(xor(place, k), xor(slice_id, 2 * o + c), source[row : row + SR, :])
+
+
+def pack_a_kernel(plan, ids, wq, wk, wv, wo, gain1, gain2, out_ref):
+    start = aligned(ids[1] * SR)
+    for i, w in enumerate((wq, wk, wv, wo)):
+        out_ref[:, i * D : (i + 1) * D] = w[pl.ds(start, SR), :]
+    out_ref[:, 4 * D :] = jnp.zeros((SR, 128), BF16)
+    out_ref[0:1, 4 * D : 4 * D + plan.rows] = gain1[...]
+    out_ref[1:2, 4 * D : 4 * D + plan.rows] = gain2[...]
+
+
+def pack_b_kernel(plan, ids, gate_t, up_t, down, own_ref, slab_ref):
+    for i, w in enumerate((gate_t, up_t)):
+        for z in range(plan.grp):
+            rows = w[z * plan.down : (z + 1) * plan.down, :].astype(F32)
+            gap = jnp.zeros((plan.down_pad - plan.down, plan.rows), F32)
+            at = i * plan.ffp + z * plan.down_pad
+            block = jnp.concatenate([rows, gap], axis=0).T
+            own_ref[:, at : at + plan.down_pad] = block.astype(BF16)
+    for s in range(plan.slices):
+        for i in range(plan.pieces):
+            at = (s * plan.pieces + i) * SR
+            have = max(0, min(SR, plan.down - at))
+            rows = []
+            if have:
+                rows.append(down[at : at + have, :])
+            if have < SR:
+                rows.append(jnp.zeros((SR - have, D), BF16))
+            cols = slice(2 * plan.ffp + i * D, 2 * plan.ffp + (i + 1) * D)
+            own_ref[s * SR : (s + 1) * SR, cols] = (
+                jnp.concatenate(rows, axis=0) if len(rows) > 1 else rows[0]
+            )
+    slab_ref[...] = own_ref[pl.ds(aligned(ids[1] * SR), SR), :]
+
+
+def gather_slices(plan, slice_id, mine, part, target):
+    for c, source in enumerate((mine, part)):
+        for o in range(plan.half):
+            s = xor(slice_id, 2 * o + c)
+            target[pl.ds(aligned(s * SR), SR), :] = source[o * SR : (o + 1) * SR, :]
+
+
+def finish_a_kernel(plan, ids, mine, part, *refs):
+    scratch = refs[-1]
+    gather_slices(plan, ids[1], mine, part, scratch)
+    for i in range(4):
+        refs[i][...] = scratch[:, i * D : (i + 1) * D].astype(F32)
+    norms = scratch[0:SR, 4 * D : 4 * D + plan.rows].astype(F32)
+    refs[4][...] = norms[0:1, :]
+    refs[5][...] = norms[1:2, :]
+
+
+def finish_b_kernel(plan, ids, mine, part, gate_ref, up_ref, down_ref, scratch):
+    gather_slices(plan, ids[1], mine, part, scratch)
+    for i, ref in enumerate((gate_ref, up_ref)):
+        for z in range(plan.grp):
+            at = i * plan.ffp + z * plan.down_pad
+            block = scratch[:, at : at + plan.down_pad].astype(F32).T
+            ref[z * plan.down : (z + 1) * plan.down, :] = block[: plan.down, :]
+    for s in range(plan.slices):
+        for i in range(plan.pieces):
+            at = (s * plan.pieces + i) * SR
+            have = max(0, min(SR, plan.down - at))
+            if have:
+                cols = slice(2 * plan.ffp + i * D, 2 * plan.ffp + (i + 1) * D)
+                rows = scratch[s * SR : (s + 1) * SR, cols].astype(F32)
+                down_ref[at : at + have, :] = rows[:have, :]
 
 
 def attend_kernel(plan, ids, *refs):
@@ -281,11 +348,12 @@
     spread(plan, ids[0], ids[1], keep, send, copy)
 
 
-def attend_back_kernel(plan, q, k_in, v_in, attn, dattn, lse, cosine, sines, reach, dq_ref, dk_ref, dv_ref, bias_ref, dq_scr, dk_scr):
+def attend_back_kernel(plan, first, count, q, k_in, v_in, attn, dattn, lse, cosine, sines, reach, dq_ref, dk_ref, dv_ref, bias_ref, dq_scr, dk_scr):
     mask_bias(plan, reach[...], bias_ref)
 
     def pair(i, carry):
-        lanes = pl.ds(pl.multiple_of(i * PAIR, PAIR), PAIR)
+        lanes = pl.ds(pl.multiple_of((first + i) * PAIR, PAIR), PAIR)
+        outs = pl.ds(pl.multiple_of(i * PAIR, PAIR), PAIR)
         q2 = two_heads(q[:, lanes])
         da = dattn[:, lanes]
         da2 = two_heads(da)
@@ -297,15 +365,15 @@
         )[0:1, :]
         keys = k_in[:, lanes]
         values = v_in[:, lanes]
-        prob = jnp.exp(against(keys, q2) + (bias_ref[...] - lse[i]))
+        prob = jnp.exp(against(keys, q2) + (bias_ref[...] - lse[first + i]))
         dprob = against(values, da2)
         dscore = (prob * (dprob - mean)).astype(BF16)
-        dv_ref[:, lanes] = mm(prob.astype(BF16), da2).astype(BF16)
-        dk_scr[:, lanes] = mm(dscore, q2)
-        dq_scr[:, lanes] = one_pair(rows_of(keys, dscore)) * (HD**-0.5)
+        dv_ref[:, outs] = mm(prob.astype(BF16), da2).astype(BF16)
+        dk_scr[:, outs] = mm(dscore, q2)
+        dq_scr[:, outs] = one_pair(rows_of(keys, dscore)) * (HD**-0.5)
         return carry
 
-    lax.fori_loop(0, H // 2, pair, 0)
+    lax.fori_loop(0, count, pair, 0)
     n = plan.local
     dq_ref[...] = rotate_back(dq_scr[...], cosine[:n, :], sines[:n, :]).astype(BF16)
     for k in range(plan.grp):
@@ -313,19 +381,27 @@
         dk_ref[rows, :] = rotate_back(dk_scr[rows, :], cosine[rows, :], sines[rows, :]).astype(BF16)
 
 
-def input_kernel(plan, *refs):
+def input_kernel(plan, halves, *refs):
     g = plan.grp
     parts = refs[:g]
-    dq, dk, dv, wa = refs[g : g + 4]
-    own_ref, norm_ref = refs[g + 4 : g + 6]
-    sends = refs[g + 6 :]
+    back = refs[g : g + 3 * halves]
+    wa, own_ref, norm_ref = refs[g + 3 * halves : g + 3 * halves + 3]
+    sends = refs[g + 3 * halves + 3 :]
     n = plan.local
+    wide = D // halves
     norm = jnp.zeros((1, D), F32)
     for k in reversed(range(g)):
         rows = slice(k * n, (k + 1) * n)
-        dn1 = against(dk[rows, :], wa[:, D : 2 * D]) + against(dv[rows, :], wa[:, 2 * D : 3 * D])
+        dn1 = None
+        for h in range(halves):
+            dq, dk, dv = back[3 * h : 3 * h + 3]
+            at = h * wide
+            term = against(dk[rows, :], wa[:, D + at : D + at + wide])
+            term = term + against(dv[rows, :], wa[:, 2 * D + at : 2 * D + at + wide])
+            if k == 0:
+                term = term + against(dq[...], wa[:, at : at + wide])
+            dn1 = term if dn1 is None else dn1 + term
         if k == 0:
-            dn1 = dn1 + against(dq[...], wa[:, :D])
             own_ref[...] = dn1
         else:
             sends[k - 1][...] = dn1.astype(BF16)
@@ -335,11 +411,17 @@
     norm_ref[...] = norm
 
 
-def attend_grads_kernel(plan, ids, n1, dq, dk, dv, attn, dout, norms, keep, send, ga_ref):
+def attend_grads_kernel(plan, halves, ids, n1, *refs):
+    back = refs[: 3 * halves]
+    attn, dout, norms, keep, send, ga_ref = refs[3 * halves :]
     n1_t = n1[...].T
-    ga_ref[:, :D] = mm(n1_t[:, : plan.local], dq[...]).astype(BF16)
-    ga_ref[:, D : 2 * D] = mm(n1_t, dk[...]).astype(BF16)
-    ga_ref[:, 2 * D : 3 * D] = mm(n1_t, dv[...]).astype(BF16)
+    wide = D // halves
+    for h in range(halves):
+        dq, dk, dv = back[3 * h : 3 * h + 3]
+        at = h * wide
+        ga_ref[:, at : at + wide] = mm(n1_t[:, : plan.local], dq[...]).astype(BF16)
+        ga_ref[:, D + at : D + at + wide] = mm(n1_t, dk[...]).astype(BF16)
+        ga_ref[:, 2 * D + at : 2 * D + at + wide] = mm(n1_t, dv[...]).astype(BF16)
     ga_ref[:, 3 * D :] = rows_of(attn[...], dout[...]).astype(BF16)
 
     def copy(z, s, target, o, k):
@@ -371,13 +453,22 @@
     out_ref[...] = dx1[...] + scale * (e1 - unit * jnp.mean(e1 * unit, axis=1, keepdims=True))
 
 
-def fetch(plan, slab):
-    parts = [swap("grp", k, plan.grp, slab) for k in range(1, plan.grp)]
-    block = jnp.concatenate(parts, axis=0)
-    mine = jnp.concatenate(
+def fetch_line(plan, slab):
+    return jnp.concatenate([swap("grp", k, plan.grp, slab) for k in range(1, plan.grp)], axis=0)
+
+
+def fetch_plane(plan, block):
+    return jnp.concatenate(
         [block] + [swap("rep", 2 * o, plan.rep, block) for o in range(1, plan.half)], axis=0
     )
-    return mine, swap("rep", 1, plan.rep, mine)
+
+
+def fetch_core(plan, mine):
+    return swap("rep", 1, plan.rep, mine)
+
+
+def tie(value, *others):
+    return lax.optimization_barrier((value, *others))[0]
 
 
 def add(*values):
@@ -387,21 +478,24 @@
     return total.astype(BF16)
 
 
-def combine(plan, keep, send):
+def combine_cores(plan, keep, send):
     got = swap("rep", 1, plan.rep, send)
-    terms = [add(keep[o], got[o]) for o in range(plan.half)]
-    total = add(
-        terms[0], *[swap("rep", 2 * o, plan.rep, terms[o]) for o in range(1, plan.half)]
-    )
+    return [add(keep[o], got[o]) for o in range(plan.half)]
+
+
+def combine_plane(plan, terms, after=()):
+    got = [swap("rep", 2 * o, plan.rep, terms[o]) for o in range(1, plan.half)]
+    return add(tie(terms[0], *after), *got)
+
+
+def combine_line(plan, total):
     final = add(total[0], *[swap("grp", k, plan.grp, total[k]) for k in range(1, plan.grp)])
     bit = plan.slices
     while bit < plan.rep:
         final = add(final, swap("rep", bit, plan.rep, final))
         bit *= 2
-    mine = jnp.concatenate(
-        [final] + [swap("rep", 2 * o, plan.rep, final) for o in range(1, plan.half)], axis=0
-    )
-    return mine, swap("rep", 1, plan.rep, mine)
+    mine = fetch_plane(plan, final)
+    return mine, fetch_core(plan, mine)
 
 
 def pad_columns(plan, weight):
@@ -415,6 +509,56 @@
     return jnp.concatenate(
         [grad[:, z * plan.down_pad : z * plan.down_pad + plan.down] for z in range(plan.grp)],
         axis=1,
+    )
+
+
+def pack_b(plan, ids, w_gate, w_up, w_down):
+    if plan.down % 8 == 0:
+        return call(
+            functools.partial(pack_b_kernel, plan),
+            [sds((plan.rows, plan.wide_b), BF16), sds((SR, plan.wide_b), BF16)],
+            "pack_b",
+            (ids, w_gate.T, w_up.T, w_down),
+            moved=3 * 10**6,
+        )
+    rows = jnp.pad(w_down, ((0, plan.down_pad - plan.down), (0, 0)))
+    rows = rows.reshape(plan.slices, plan.pieces, SR, D).transpose(0, 2, 1, 3)
+    own = jnp.concatenate(
+        [
+            pad_columns(plan, w_gate),
+            pad_columns(plan, w_up),
+            rows.reshape(plan.rows, plan.pieces * D),
+        ],
+        axis=1,
+    )
+    return own, lax.dynamic_slice(own, (ids[1] * SR, 0), (SR, plan.wide_b))
+
+
+def finish_b(plan, ids, final):
+    if plan.down % 8 == 0:
+        tall = sds((FF, plan.rows), F32)
+        gate, up, down = call(
+            functools.partial(finish_b_kernel, plan),
+            [tall, tall, sds((plan.down, D), F32)],
+            "finish_b",
+            (ids, *final),
+            [pltpu.VMEM((plan.rows, plan.wide_b), BF16)],
+            moved=3 * 10**6,
+        )
+        return gate.T, up.T, down
+    (grads,) = call(
+        functools.partial(finish_kernel, plan),
+        [sds((plan.rows, plan.wide_b), F32)],
+        "finish_b",
+        (ids, *final),
+        moved=4 * 10**6,
+    )
+    ffp = plan.ffp
+    down = grads[:, 2 * ffp :].reshape(plan.slices, SR, plan.pieces, D).transpose(0, 2, 1, 3)
+    return (
+        drop_columns(plan, grads[:, :ffp]),
+        drop_columns(plan, grads[:, ffp : 2 * ffp]),
+        down.reshape(plan.down_pad, D)[: plan.down],
     )
 
 
@@ -429,28 +573,26 @@
     table_cos, table_sin = rotary_tables(plan)
     cosine, sines = jnp.asarray(table_cos), jnp.asarray(table_sin)
 
+    own_a = (w_query, w_key, w_value, w_out)
     gains = jnp.stack([norm1_gain, norm2_gain])
-    gain_tile = jnp.pad(gains, ((0, SR - 2), (0, 128 - plan.rows)))
-    own_a = (w_query, w_key, w_value, w_out)
-    start = slice_id * SR
-    slab_a = jnp.concatenate(
-        [lax.dynamic_slice(w, (start, 0), (SR, D)) for w in own_a] + [gain_tile], axis=1
-    )
-    down_rows = jnp.pad(w_down, ((0, plan.down_pad - plan.down), (0, 0)))
-    down_rows = down_rows.reshape(plan.slices, plan.pieces, SR, D).transpose(0, 2, 1, 3)
-    own_b = jnp.concatenate(
-        [
-            pad_columns(plan, w_gate),
-            pad_columns(plan, w_up),
-            down_rows.reshape(plan.rows, plan.pieces * D),
-        ],
-        axis=1,
-    )
-    slab_b = lax.dynamic_slice(own_b, (start, 0), (SR, plan.wide_b))
-
-    mine_a, part_a = fetch(plan, slab_a)
-    parts = [x0] + [shift(k, g, x0) for k in range(1, g)]
-    mine_b, part_b = fetch(plan, slab_b)
+    (slab_a,) = call(
+        functools.partial(pack_a_kernel, plan),
+        [sds((SR, plan.wide_a), BF16)],
+        "pack_a",
+        (ids, *own_a, norm1_gain.reshape(1, -1), norm2_gain.reshape(1, -1)),
+        moved=10**6,
+    )
+    own_b, slab_b = pack_b(plan, ids, w_gate, w_up, w_down)
+
+    block_a = fetch_line(plan, slab_a)
+    block_b = fetch_line(plan, slab_b)
+    parts = [x0]
+    for _ in range(1, g):
+        parts.append(shift(1, g, parts[-1]))
+    mine_a = fetch_plane(plan, block_a)
+    mine_b = fetch_plane(plan, tie(block_b, mine_a))
+    part_a = fetch_core(plan, mine_a)
+    part_b = fetch_core(plan, mine_b)
 
     tiles = jnp.stack(
         [gains] + [mine_a[k * SR : k * SR + 2, 4 * D : 4 * D + plan.rows] for k in range(g - 1)]
@@ -513,70 +655,86 @@
         flops=2 * 10**9,
         moved=8 * 10**6,
     )
-    dq, dk, dv = call(
-        functools.partial(attend_back_kernel, plan),
-        [sds((n, D), BF16), sds((full, D), BF16), sds((full, D), BF16)],
-        "attend_back",
-        (q, k_all, v_all, attn, dattn, lse, cosine, sines, reach),
-        [pltpu.VMEM((full, 2 * n), F32), pltpu.VMEM((n, D), F32), pltpu.VMEM((full, D), F32)],
-        flops=8 * 10**9,
-        moved=8 * 10**6,
-    )
+    halves = 2
+    count = H // 2 // halves
+    wide = D // halves
+
+    def attend_back(first, dattn):
+        return call(
+            functools.partial(attend_back_kernel, plan, first, count),
+            [sds((n, wide), BF16), sds((full, wide), BF16), sds((full, wide), BF16)],
+            "attend_back",
+            (q, k_all, v_all, attn, dattn, lse, cosine, sines, reach),
+            [
+                pltpu.VMEM((full, 2 * n), F32),
+                pltpu.VMEM((n, wide), F32),
+                pltpu.VMEM((full, wide), F32),
+            ],
+            flops=4 * 10**9,
+            moved=8 * 10**6,
+        )
+
+    back = list(attend_back(0, tie(dattn, keep_b)))
+    terms_b = combine_cores(plan, keep_b, send_b)
+    back += attend_back(count, tie(dattn, *terms_b, back[0]))
     own, norm1, *sends = call(
-        functools.partial(input_kernel, plan),
+        functools.partial(input_kernel, plan, halves),
         [sds((n, D), F32), sds((1, D), F32)] + [sds((n, D), BF16)] * (g - 1),
         "dn1",
-        (*parts, dq, dk, dv, wa),
+        (*parts, *back, wa),
         flops=2 * 10**9,
         moved=4 * 10**6,
     )
-    received = [shift(-k, g, sends[k - 1]) for k in range(1, g)]
+    moving = sends[g - 2]
+    for k in reversed(range(1, g)):
+        moving = shift(-1, g, moving)
+        if k > 1:
+            moving = add(moving, sends[k - 2])
 
     norms = jnp.concatenate([norm1, norm2], axis=0).reshape(2, g, plan.rows).transpose(1, 0, 2)
     norms = jnp.pad(norms, ((0, 0), (0, SR - 2), (0, 128 - plan.rows)))
     slabs_a = sds((plan.half, g, SR, plan.wide_a), BF16)
     keep_a, send_a = call(
-        functools.partial(attend_grads_kernel, plan),
+        functools.partial(attend_grads_kernel, plan, halves),
         [slabs_a, slabs_a],
         "attend_grads",
-        (ids, n1, dq, dk, dv, attn_low, dout, norms),
+        (ids, n1, *back, attn_low, dout, norms),
         [pltpu.VMEM((D, 4 * D), BF16)],
         flops=2 * 10**9,
         moved=8 * 10**6,
     )
 
-    def finish(halves, wide, name):
-        (out,) = call(
-            functools.partial(finish_kernel, plan),
-            [sds((plan.slices * SR, wide), F32)],
-            name,
-            (ids, *halves),
-            moved=4 * 10**6,
-        )
-        return out
-
-    grads_b = finish(combine(plan, keep_b, send_b), plan.wide_b, "finish_b")
-    grads_a = finish(combine(plan, keep_a, send_a), plan.wide_a, "finish_a")
+    total_b = combine_plane(plan, terms_b, (own,))
+    final_b = combine_line(plan, total_b)
+    total_a = combine_plane(plan, combine_cores(plan, keep_a, send_a))
     (input_grad,) = call(
         functools.partial(residual_kernel, plan),
         [sds((n, D), F32)],
         "residual",
-        (own, x0, dx1, gain1, *received),
+        (own, x0, dx1, gain1, moving),
         moved=4 * 10**6,
     )
-    down = grads_b[:, 2 * ffp :].reshape(plan.slices, SR, plan.pieces, D).transpose(0, 2, 1, 3)
+    final_a = combine_line(plan, tie(total_a, input_grad))
+    gate, up, down = finish_b(plan, ids, final_b)
+    shard = sds((plan.rows, D), F32)
+    line = sds((1, plan.rows), F32)
+    grads_a = call(
+        functools.partial(finish_a_kernel, plan),
+        [shard, shard, shard, shard, line, line],
+        "finish_a",
+        (ids, *final_a),
+        [pltpu.VMEM((plan.rows, plan.wide_a), BF16)],
+        moved=2 * 10**6,
+    )
     return (
         output.reshape(tokens.shape),
         input_grad.reshape(tokens.shape),
-        grads_a[0, 4 * D : 4 * D + plan.rows],
-        grads_a[:, :D],
-        grads_a[:, D : 2 * D],
-        grads_a[:, 2 * D : 3 * D],
-        grads_a[:, 3 * D : 4 * D],
-        grads_a[1, 4 * D : 4 * D + plan.rows],
-        drop_columns(plan, grads_b[:, :ffp]),
-        drop_columns(plan, grads_b[:, ffp : 2 * ffp]),
-        down.reshape(plan.down_pad, D)[: plan.down],
+        grads_a[4].reshape(plan.rows),
+        *grads_a[:4],
+        grads_a[5].reshape(plan.rows),
+        gate,
+        up,
+        down,
     )
 
 

time: 261 us -> 199 us (0.76)
  waiting for transfers between devices: 99.5 us -> 59.7 us
  local copies, waits for them, and re-layouts: 22.2 us -> 5.3 us
  starting transfers between devices: 77.5 us -> 64.2 us
  Pallas kernels: 55.8 us -> 62.5 us
    ppermute x36, waiting for transfers between devices: 91.7 us -> 36.3 us  [swap(): return lax.ppermute(value, axis, [(i, i ^ k) for i in range(size)])]
    ppermute x36, starting transfers between devices: 64 us -> 48.2 us  [swap(): return lax.ppermute(value, axis, [(i, i ^ k) for i in range(size)])]
    ppermute x6, waiting for transfers between devices: 7.82 us -> 23.4 us  [shift(): lax.ppermute(value, 'grp', [(i, i + k) for i in range(size) if 0 <= i + k...]
    unnamed x71 -> x49, local copies, waits for them, and re-layouts: 11.3 us -> 3.97 us
    pallas_call x9 -> x12, Pallas kernels: 55.8 us -> 62.5 us  [call(): pl.pallas_call(body, out_shape=outs, in_specs=specs, out_specs=[VMEM] * l...]
    slice x5 -> x0, local copies, waits for them, and re-layouts: 4.65 us -> none  [the longest x1 2.17 us: body(): grads_a[:, 3 * D:4 * D]]
  transfers between devices with their start and end apart: 42 -> 42, of which waited for: 19 -> 17; matrix products, arithmetic and copies ran while one was open for 4% -> 2% of each run, Pallas kernels for 8% -> 16%
where the time goes in v2:
time: 199 us; the launch traced here: 198 us
  starting transfers between devices  64.2 us (32%)
  Pallas kernels  62.5 us (31%)
  waiting for transfers between devices  59.7 us (30%)
  local copies, waits for them, and re-layouts  5.3 us (3%)
  other arithmetic  4.72 us (2%)
    pallas_call x12, Pallas kernels, call(): pl.pallas_call(body, out_shape=outs, in_specs=specs, out_specs=[VMEM] * l...  62.5 us
    ppermute x36, starting transfers between devices, swap(): return lax.ppermute(value, axis, [(i, i ^ k) for i in range(size)])  48.2 us
    ppermute x36, waiting for transfers between devices, swap(): return lax.ppermute(value, axis, [(i, i ^ k) for i in range(size)])  36.3 us
    ppermute x6, waiting for transfers between devices, shift(): lax.ppermute(value, 'grp', [(i, i + k) for i in range(size) if 0 <= i + k...  23.4 us
    ppermute x6, starting transfers between devices, shift(): lax.ppermute(value, 'grp', [(i, i + k) for i in range(size) if 0 <= i + k...  16 us
  transfers between devices with their start and end apart: 42, of which 17 were waited for; matrix products, arithmetic and copies ran while one was open for 2% of the time, Pallas kernels for 16%

profile of v2, /device:TPU:0, one launch (start us, length us, event | category | flops | bytes accessed | tf_op | source)
XLA Modules:
  0.0 197.5 jit_solution(13474364356225475367)
XLA Ops:
  3.1 3.1 %collective-permute-start.3 = (bf16[16,2176]{1,0:T(8,128)(2,1)}, bf16[16,2176]{1,0:T(8,128)(2,1)S(1)}, u32[]{:S(2)}, u32[]{:S(2)}) collective-permute-start(bf16[16,2176]{1,0:T(8,128)(2,1)} %pack_a.1), channel_id=1, source_target_pairs={{0,1},{1,0},{2,3},{3,2},{4,5},{5,4},{6,7},{7,6},{8,9},{9,8},{10,11... | collective-permute-start | bytes 208904 | tf_op jit(solution)/shard_map/ppermute | solution.py:78
  12.2 3.5 %collective-permute-start.11 = (bf16[16,4608]{1,0:T(8,128)(2,1)}, bf16[16,4608]{1,0:T(8,128)(2,1)S(1)}, u32[]{:S(2)}, u32[]{:S(2)}) collective-permute-start(bf16[16,4608]{1,0:T(8,128)(2,1)} %get-tuple-element.62), channel_id=1, source_target_pairs={{0,2},{1,3},{2,0},{3,1},{4,6},{5,7},{6,4},{7,5},{8,10},{9,11},{10,... | collective-permute-start | bytes 442376 | tf_op jit(solution)/shard_map/ppermute | solution.py:78
  22.1 4.4 %collective-permute-done.11 = bf16[16,4608]{1,0:T(8,128)(2,1)S(1)} collective-permute-done((bf16[16,4608]{1,0:T(8,128)(2,1)}, bf16[16,4608]{1,0:T(8,128)(2,1)S(1)}, u32[]{:S(2)}, u32[]{:S(2)}) %collective-permute-start.11) | collective-permute-done | bytes 147488 | tf_op jit(solution)/shard_map/ppermute | solution.py:78
  31.5 9.5 %collective-permute-done.13 = bf16[48,4608]{1,0:T(8,128)(2,1)S(1)} collective-permute-done((bf16[48,4608]{1,0:T(8,128)(2,1)S(1)}, bf16[48,4608]{1,0:T(8,128)(2,1)S(1)}, u32[]{:S(2)}, u32[]{:S(2)}) %collective-permute-start.13) | collective-permute-done | bytes 442400 | tf_op jit(solution)/shard_map/ppermute | solution.py:78
  41.0 7.9 %collective-permute-done.14 = bf16[48,4608]{1,0:T(8,128)(2,1)S(1)} collective-permute-done((bf16[48,4608]{1,0:T(8,128)(2,1)S(1)}, bf16[48,4608]{1,0:T(8,128)(2,1)S(1)}, u32[]{:S(2)}, u32[]{:S(2)}) %collective-permute-start.14) | collective-permute-done | bytes 442400 | tf_op jit(solution)/shard_map/ppermute | solution.py:78
  49.1 3.2 %collective-permute-start = (bf16[256,512]{1,0:T(8,128)(2,1)S(1)}, bf16[256,512]{1,0:T(8,128)(2,1)S(1)}, u32[]{:S(2)}, u32[]{:S(2)}) collective-permute-start(bf16[256,512]{1,0:T(8,128)(2,1)S(1)} %bitcast.60), channel_id=1, source_target_pairs={{0,1},{1,2},{2,3},{4,5},{5,6},{6,7},{8,9},{9,10},{10,11},{12,13},{... | collective-permute-start | bytes 786440 | tf_op jit(solution)/shard_map/ppermute | solution.py:82
  52.6 5.9 %collective-permute-done.refs_1_ = bf16[256,512]{1,0:T(8,128)(2,1)S(1)} collective-permute-done((bf16[256,512]{1,0:T(8,128)(2,1)S(1)}, bf16[256,512]{1,0:T(8,128)(2,1)S(1)}, u32[]{:S(2)}, u32[]{:S(2)}) %collective-permute-start) | collective-permute-done | bytes 262176 | tf_op jit(solution)/shard_map/ppermute | solution.py:82
  58.5 4.4 %collective-permute-start.1 = (bf16[256,512]{1,0:T(8,128)(2,1)S(1)}, bf16[256,512]{1,0:T(8,128)(2,1)S(1)}, u32[]{:S(2)}, u32[]{:S(2)}) collective-permute-start(bf16[256,512]{1,0:T(8,128)(2,1)S(1)} %collective-permute-done.refs_1_), channel_id=1, source_target_pairs={{0,1},{1,2},{2,3},{4,5},{5,6},{6,7},{8,9},{9,10},{10,11},{12,13},{... | collective-permute-start | bytes 786440 | tf_op jit(solution)/shard_map/ppermute | solution.py:82
  63.5 4.7 %collective-permute-done.1.refs_2_ = bf16[256,512]{1,0:T(8,128)(2,1)S(1)} collective-permute-done((bf16[256,512]{1,0:T(8,128)(2,1)S(1)}, bf16[256,512]{1,0:T(8,128)(2,1)S(1)}, u32[]{:S(2)}, u32[]{:S(2)}) %collective-permute-start.1) | collective-permute-done | bytes 262176 | tf_op jit(solution)/shard_map/ppermute | solution.py:82
  68.2 4.4 %collective-permute-start.2 = (bf16[256,512]{1,0:T(8,128)(2,1)S(1)}, bf16[256,512]{1,0:T(8,128)(2,1)S(1)}, u32[]{:S(2)}, u32[]{:S(2)}) collective-permute-start(bf16[256,512]{1,0:T(8,128)(2,1)S(1)} %collective-permute-done.1.refs_2_), channel_id=1, source_target_pairs={{0,1},{1,2},{2,3},{4,5},{5,6},{6,7},{8,9},{9,10},{10,11},{12,13},{... | collective-permute-start | bytes 786440 | tf_op jit(solution)/shard_map/ppermute | solution.py:82
  73.3 3.8 %collective-permute-done.2.refs_3_ = bf16[256,512]{1,0:T(8,128)(2,1)S(1)} collective-permute-done((bf16[256,512]{1,0:T(8,128)(2,1)S(1)}, bf16[256,512]{1,0:T(8,128)(2,1)S(1)}, u32[]{:S(2)}, u32[]{:S(2)}) %collective-permute-start.2) | collective-permute-done | bytes 262176 | tf_op jit(solution)/shard_map/ppermute | solution.py:82
  78.1 11.6 %attend.1 = (f32[256,512]{1,0:T(8,128)}, bf16[256,512]{1,0:T(8,128)(2,1)}, bf16[1024,512]{1,0:T(8,128)(2,1)}, bf16[1024,512]{1,0:T(8,128)(2,1)}, bf16[1024,512]{...) custom-call(s32[2]{0:T(128)} %pad_add_fusion.ids, bf16[256,512]{1,0:T(8,128)(2,1)} %bitcast.56, ...), custom_call_target="tpu_custom_call" | custom-call | tf_op jit(solution)/shard_map/attend/pallas_call | solution.py:61
  90.9 8.4 %mlp.1 = (bf16[256,512]{1,0:T(8,128)(2,1)}, f32[256,512]{1,0:T(8,128)}, bf16[256,512]{1,0:T(8,128)(2,1)}, bf16[256,512]{1,0:T(8,128)(2,1)}, bf16[256,512]{1,0:T(...) custom-call(s32[2]{0:T(128)} %pad_add_fusion.ids, ...), custom_call_target="tpu_custom_call" | custom-call | tf_op jit(solution)/shard_map/mlp/pallas_call | solution.py:61
  99.3 5.5 %mlp_grads.1 = (bf16[4,4,16,4608]{3,2,1,0:T(8,128)(2,1)}, bf16[4,4,16,4608]{3,2,1,0:T(8,128)(2,1)}) custom-call(s32[2]{0:T(128)} %pad_add_fusion.ids, bf16[256,512]{1,0:T(8,128)(2,1)} %get-tuple-element.69.n2, bf16[256,1536]{1,0:T(8,128)(2,1)} %get-tuple-element.70.hid, bf16[256,1536]{1,0:T(8,128)(2,1)} %get-tuple-element.71.dg, ...), custom_call_target="tpu_custom_call" | custom-call | tf_op jit(solution)/shard_map/mlp_grads/pallas_call | solution.py:61
  104.8 7.6 %attend_back.2 = (bf16[256,256]{1,0:T(8,128)(2,1)}, bf16[1024,256]{1,0:T(8,128)(2,1)}, bf16[1024,256]{1,0:T(8,128)(2,1)}) custom-call(bf16[256,512]{1,0:T(8,128)(2,1)} %get-tuple-element.65.q, bf16[1024,512]{1,0:T(8,128)(2,1)} %get-tuple-element.66.k_in, bf16[1024,512]{1,0:T(8,128)(2,1)} %get-tuple-element.67.v_in, ...), custom_call_target="tpu_custom_call" | custom-call | tf_op jit(solution)/shard_map/attend_back/pallas_call | solution.py:61
  113.1 7.7 %attend_back.3 = (bf16[256,256]{1,0:T(8,128)(2,1)}, bf16[1024,256]{1,0:T(8,128)(2,1)}, bf16[1024,256]{1,0:T(8,128)(2,1)}) custom-call(bf16[256,512]{1,0:T(8,128)(2,1)} %get-tuple-element.65.q, bf16[1024,512]{1,0:T(8,128)(2,1)} %get-tuple-element.66.k_in, bf16[1024,512]{1,0:T(8,128)(2,1)} %get-tuple-element.67.v_in, ...), custom_call_target="tpu_custom_call" | custom-call | tf_op jit(solution)/shard_map/attend_back/pallas_call | solution.py:61
  120.8 5.0 %dn1.1 = (f32[256,512]{1,0:T(8,128)}, f32[1,512]{1,0:T(1,128)}, bf16[256,512]{1,0:T(8,128)(2,1)}, bf16[256,512]{1,0:T(8,128)(2,1)}, bf16[256,512]{1,0:T(8,128)(2,1)}) custom-call(bf16[256,512]{1,0:T(8,128)(2,1)} %bitcast.58, bf16[256,512]{1,0:T(8,128)(2,1)} %copy-done.7, bf16[256,512]{1,0:T(8,128)(2,1)} %copy-done.8, bf16[256,512]{1,0:T(8,128)(2,1)} %copy-done.9, ...), custom_call_target="tpu_custom_call" | custom-call | tf_op jit(solution)/shard_map/dn1/pallas_call | solution.py:61
  130.7 6.7 %collective-permute-done.18 = bf16[256,512]{1,0:T(8,128)(2,1)S(1)} collective-permute-done((bf16[256,512]{1,0:T(8,128)(2,1)}, bf16[256,512]{1,0:T(8,128)(2,1)S(1)}, u32[]{:S(2)}, u32[]{:S(2)}) %collective-permute-start.18) | collective-permute-done | bytes 262176 | tf_op jit(solution)/shard_map/ppermute | solution.py:82
  141.0 5.1 %attend_grads.1 = (bf16[4,4,16,2176]{3,2,1,0:T(8,128)(2,1)}, bf16[4,4,16,2176]{3,2,1,0:T(8,128)(2,1)}) custom-call(s32[2]{0:T(128)} %pad_add_fusion.ids, bf16[1024,512]{1,0:T(8,128)(2,1)} %get-tuple-element.89.n1, bf16[256,256]{1,0:T(8,128)(2,1)} %get-tuple-element.76.refs_4_.refs_0_, bf16[1024,256]{1,0:T(8,128)(2,1)} %get-tuple-element.77.refs_5_.refs_1_, ...), custom_call_target="tpu_custom_call" | custom-call | tf_op jit(solution)/shard_map/attend_grads/pallas_call | solution.py:61
  150.0 4.9 %collective-permute-done.33 = bf16[4,16,4608]{2,1,0:T(8,128)(2,1)S(1)} collective-permute-done((bf16[4,16,4608]{2,1,0:T(8,128)(2,1)S(1)}, bf16[4,16,4608]{2,1,0:T(8,128)(2,1)S(1)}, u32[]{:S(2)}, u32[]{:S(2)}) %collective-permute-start.33) | collective-permute-done | bytes 589856 | tf_op jit(solution)/shard_map/ppermute | solution.py:78
  160.7 3.2 %collective-permute-start.35 = (bf16[16,4608]{1,0:T(8,128)(2,1)S(1)}, bf16[16,4608]{1,0:T(8,128)(2,1)S(1)}, u32[]{:S(2)}, u32[]{:S(2)}) collective-permute-start(bf16[16,4608]{1,0:T(8,128)(2,1)S(1)} %get-tuple-element.115), channel_id=1, source_target_pairs={{0,1},{1,0},{2,3},{3,2},{4,5},{5,4},{6,7},{7,6},{8,9},{9,8},{10,11... | collective-permute-start | bytes 442376 | tf_op jit(solution)/shard_map/ppermute | solution.py:78
  169.0 3.0 %collective-permute-start.37 = (bf16[16,4608]{1,0:T(8,128)(2,1)S(1)}, bf16[16,4608]{1,0:T(8,128)(2,1)S(1)}, u32[]{:S(2)}, u32[]{:S(2)}) collective-permute-start(bf16[16,4608]{1,0:T(8,128)(2,1)S(1)} %get-tuple-element.116), channel_id=1, source_target_pairs={{0,3},{1,2},{2,1},{3,0},{4,7},{5,6},{6,5},{7,4},{8,11},{9,10},{10,... | collective-permute-start | bytes 442376 | tf_op jit(solution)/shard_map/ppermute | solution.py:78
  172.1 2.9 %collective-permute-start.25 = (bf16[16,2176]{1,0:T(8,128)(2,1)S(1)}, bf16[16,2176]{1,0:T(8,128)(2,1)S(1)}, u32[]{:S(2)}, u32[]{:S(2)}) collective-permute-start(bf16[16,2176]{1,0:T(8,128)(2,1)S(1)} %get-tuple-element.118), channel_id=1, source_target_pairs={{0,1},{1,0},{2,3},{3,2},{4,5},{5,4},{6,7},{7,6},{8,9},{9,8},{10,11... | collective-permute-start | bytes 208904 | tf_op jit(solution)/shard_map/ppermute | solution.py:78
  191.9 2.8 %finish_b.1 = (f32[1376,128]{1,0:T(8,128)}, f32[1376,128]{1,0:T(8,128)}, f32[344,512]{1,0:T(8,128)}) custom-call(s32[2]{0:T(128)} %pad_add_fusion.ids, bf16[64,4608]{1,0:T(8,128)(2,1)} %copy-done.3, bf16[64,4608]{1,0:T(8,128)(2,1)} %copy-done.12), custom_call_target="tpu_custom_call" | custom-call | tf_op jit(solution)/shard_map/finish_b/pallas_call | solution.py:61
  (149 shorter events, 67.4 us)
Async XLA Ops:
  3.1 12.6 %collective-permute-start.3 = (bf16[16,2176]{1,0:T(8,128)(2,1)}, bf16[16,2176]{1,0:T(8,128)(2,1)S(1)}, u32[]{:S(2)}, u32[]{:S(2)}) collective-permute-start(bf16[16,2176]{1,0:T(8,128)(2,1)} %pack_a.1), channel_id=1, source_target_pairs={{0,1},{1,0},{2,3},{3,2},{4,5},{5,4},{6,7},{7,6},{8,9},{9,8},{10,11... | collective-permute-start | bytes 208904 | tf_op jit(solution)/shard_map/ppermute | solution.py:78
  6.1 9.6 %collective-permute-start.4 = (bf16[16,2176]{1,0:T(8,128)(2,1)}, bf16[16,2176]{1,0:T(8,128)(2,1)S(1)}, u32[]{:S(2)}, u32[]{:S(2)}) collective-permute-start(bf16[16,2176]{1,0:T(8,128)(2,1)} %pack_a.1), channel_id=1, source_target_pairs={{0,2},{1,3},{2,0},{3,1},{4,6},{5,7},{6,4},{7,5},{8,10},{9,11},{10,... | collective-permute-start | bytes 208904 | tf_op jit(solution)/shard_map/ppermute | solution.py:78
  12.2 14.3 %collective-permute-start.11 = (bf16[16,4608]{1,0:T(8,128)(2,1)}, bf16[16,4608]{1,0:T(8,128)(2,1)S(1)}, u32[]{:S(2)}, u32[]{:S(2)}) collective-permute-start(bf16[16,4608]{1,0:T(8,128)(2,1)} %get-tuple-element.62), channel_id=1, source_target_pairs={{0,2},{1,3},{2,0},{3,1},{4,6},{5,7},{6,4},{7,5},{8,10},{9,11},{10,... | collective-permute-start | bytes 442376 | tf_op jit(solution)/shard_map/ppermute | solution.py:78
  15.7 10.8 %collective-permute-start.12 = (bf16[16,4608]{1,0:T(8,128)(2,1)}, bf16[16,4608]{1,0:T(8,128)(2,1)S(1)}, u32[]{:S(2)}, u32[]{:S(2)}) collective-permute-start(bf16[16,4608]{1,0:T(8,128)(2,1)} %get-tuple-element.62), channel_id=1, source_target_pairs={{0,3},{1,2},{2,1},{3,0},{4,7},{5,6},{6,5},{7,4},{8,11},{9,10},{10,... | collective-permute-start | bytes 442376 | tf_op jit(solution)/shard_map/ppermute | solution.py:78
  15.7 10.8 %collective-permute-start.6 = (bf16[48,2176]{1,0:T(8,128)(2,1)S(1)}, bf16[48,2176]{1,0:T(8,128)(2,1)S(1)}, u32[]{:S(2)}, u32[]{:S(2)}) collective-permute-start(bf16[48,2176]{1,0:T(8,128)(2,1)S(1)} %get-tuple-element.121), channel_id=1, source_target_pairs={{0,8},{4,12},{8,0},{12,4},{16,24},{20,28},{24,16},{28,20},{1,9},{5... | collective-permute-start | bytes 626696 | tf_op jit(solution)/shard_map/ppermute | solution.py:78
  17.5 10.3 %collective-permute-start.7 = (bf16[48,2176]{1,0:T(8,128)(2,1)S(1)}, bf16[48,2176]{1,0:T(8,128)(2,1)S(1)}, u32[]{:S(2)}, u32[]{:S(2)}) collective-permute-start(bf16[48,2176]{1,0:T(8,128)(2,1)S(1)} %get-tuple-element.121), channel_id=1, source_target_pairs={{0,16},{4,20},{8,24},{12,28},{16,0},{20,4},{24,8},{28,12},{1,17},{... | collective-permute-start | bytes 626696 | tf_op jit(solution)/shard_map/ppermute | solution.py:78
  27.9 13.1 %collective-permute-start.13 = (bf16[48,4608]{1,0:T(8,128)(2,1)S(1)}, bf16[48,4608]{1,0:T(8,128)(2,1)S(1)}, u32[]{:S(2)}, u32[]{:S(2)}) collective-permute-start(bf16[48,4608]{1,0:T(8,128)(2,1)S(1)} %pad_maximum_fusion.1), channel_id=1, source_target_pairs={{0,8},{4,12},{8,0},{12,4},{16,24},{20,28},{24,16},{28,20},{1,9},{5... | collective-permute-start | bytes 1327112 | tf_op jit(solution)/shard_map/ppermute | solution.py:78
  28.8 20.0 %collective-permute-start.14 = (bf16[48,4608]{1,0:T(8,128)(2,1)S(1)}, bf16[48,4608]{1,0:T(8,128)(2,1)S(1)}, u32[]{:S(2)}, u32[]{:S(2)}) collective-permute-start(bf16[48,4608]{1,0:T(8,128)(2,1)S(1)} %pad_maximum_fusion.1), channel_id=1, source_target_pairs={{0,16},{4,20},{8,24},{12,28},{16,0},{20,4},{24,8},{28,12},{1,17},{... | collective-permute-start | bytes 1327112 | tf_op jit(solution)/shard_map/ppermute | solution.py:78
  30.0 18.9 %collective-permute-start.15 = (bf16[48,4608]{1,0:T(8,128)(2,1)S(1)}, bf16[48,4608]{1,0:T(8,128)(2,1)S(1)}, u32[]{:S(2)}, u32[]{:S(2)}) collective-permute-start(bf16[48,4608]{1,0:T(8,128)(2,1)S(1)} %pad_maximum_fusion.1), channel_id=1, source_target_pairs={{0,24},{4,28},{8,16},{12,20},{16,8},{20,12},{24,0},{28,4},{1,25},{... | collective-permute-start | bytes 1327112 | tf_op jit(solution)/shard_map/ppermute | solution.py:78
  49.0 40.7 %collective-permute-start.16 = (bf16[192,4608]{1,0:T(8,128)(2,1)S(1)}, bf16[192,4608]{1,0:T(8,128)(2,1)S(1)}, u32[]{:S(2)}, u32[]{:S(2)}) collective-permute-start(bf16[192,4608]{1,0:T(8,128)(2,1)S(1)} %constant_dynamic-update-slice_fusion.9.refs_6_), channel_id=1, source_target_pairs={{0,4},{4,0},{8,12},{12,8},{16,20},{20,16},{24,28},{28,24},{1,5},{5... | collective-permute-start | bytes 5308424 | tf_op jit(solution)/shard_map/ppermute | solution.py:78
  52.3 24.7 %collective-permute-start.9 = (bf16[192,2176]{1,0:T(8,128)(2,1)S(1)}, bf16[192,2176]{1,0:T(8,128)(2,1)S(1)}, u32[]{:S(2)}, u32[]{:S(2)}) collective-permute-start(bf16[192,2176]{1,0:T(8,128)(2,1)S(1)} %constant_dynamic-update-slice_fusion.3.refs_8_), channel_id=1, source_target_pairs={{0,4},{4,0},{8,12},{12,8},{16,20},{20,16},{24,28},{28,24},{1,5},{5... | collective-permute-start | bytes 2506760 | tf_op jit(solution)/shard_map/ppermute | solution.py:78
  58.5 9.7 %collective-permute-start.1 = (bf16[256,512]{1,0:T(8,128)(2,1)S(1)}, bf16[256,512]{1,0:T(8,128)(2,1)S(1)}, u32[]{:S(2)}, u32[]{:S(2)}) collective-permute-start(bf16[256,512]{1,0:T(8,128)(2,1)S(1)} %collective-permute-done.refs_1_), channel_id=1, source_target_pairs={{0,1},{1,2},{2,3},{4,5},{5,6},{6,7},{8,9},{9,10},{10,11},{12,13},{... | collective-permute-start | bytes 786440 | tf_op jit(solution)/shard_map/ppermute | solution.py:82
  125.8 11.6 %collective-permute-start.18 = (bf16[256,512]{1,0:T(8,128)(2,1)}, bf16[256,512]{1,0:T(8,128)(2,1)S(1)}, u32[]{:S(2)}, u32[]{:S(2)}) collective-permute-start(bf16[256,512]{1,0:T(8,128)(2,1)} %get-tuple-element.86), channel_id=1, source_target_pairs={{1,0},{2,1},{3,2},{5,4},{6,5},{7,6},{9,8},{10,9},{11,10},{13,12},{... | collective-permute-start | bytes 786440 | tf_op jit(solution)/shard_map/ppermute | solution.py:82
  127.1 22.9 %collective-permute-start.32 = (bf16[4,16,4608]{2,1,0:T(8,128)(2,1)S(1)}, bf16[4,16,4608]{2,1,0:T(8,128)(2,1)S(1)}, u32[]{:S(2)}, u32[]{:S(2)}) collective-permute-start(bf16[4,16,4608]{2,1,0:T(8,128)(2,1)S(1)} %get-tuple-element.109), channel_id=1, source_target_pairs={{0,8},{4,12},{8,0},{12,4},{16,24},{20,28},{24,16},{28,20},{1,9},{5... | collective-permute-start | bytes 1769480 | tf_op jit(solution)/shard_map/ppermute | solution.py:78
  128.4 26.5 %collective-permute-start.33 = (bf16[4,16,4608]{2,1,0:T(8,128)(2,1)S(1)}, bf16[4,16,4608]{2,1,0:T(8,128)(2,1)S(1)}, u32[]{:S(2)}, u32[]{:S(2)}) collective-permute-start(bf16[4,16,4608]{2,1,0:T(8,128)(2,1)S(1)} %get-tuple-element.108), channel_id=1, source_target_pairs={{0,16},{4,20},{8,24},{12,28},{16,0},{20,4},{24,8},{28,12},{1,17},{... | collective-permute-start | bytes 1769480 | tf_op jit(solution)/shard_map/ppermute | solution.py:78
  129.2 27.3 %collective-permute-start.34 = (bf16[4,16,4608]{2,1,0:T(8,128)(2,1)S(1)}, bf16[4,16,4608]{2,1,0:T(8,128)(2,1)S(1)}, u32[]{:S(2)}, u32[]{:S(2)}) collective-permute-start(bf16[4,16,4608]{2,1,0:T(8,128)(2,1)S(1)} %get-tuple-element.107), channel_id=1, source_target_pairs={{0,24},{4,28},{8,16},{12,20},{16,8},{20,12},{24,0},{28,4},{1,25},{... | collective-permute-start | bytes 1769480 | tf_op jit(solution)/shard_map/ppermute | solution.py:78
  138.4 10.0 %collective-permute-start.19 = (bf16[256,512]{1,0:T(8,128)(2,1)S(1)}, bf16[256,512]{1,0:T(8,128)(2,1)S(1)}, u32[]{:S(2)}, u32[]{:S(2)}) collective-permute-start(bf16[256,512]{1,0:T(8,128)(2,1)S(1)} %add_convert_fusion.11), channel_id=1, source_target_pairs={{1,0},{2,1},{3,2},{5,4},{6,5},{7,6},{9,8},{10,9},{11,10},{13,12},{... | collective-permute-start | bytes 786440 | tf_op jit(solution)/shard_map/ppermute | solution.py:82
  146.1 10.7 %collective-permute-start.21 = (bf16[4,4,16,2176]{3,2,1,0:T(8,128)(2,1)}, bf16[4,4,16,2176]{3,2,1,0:T(8,128)(2,1)S(1)}, u32[]{:S(2)}, u32[]{:S(2)}) collective-permute-start(bf16[4,4,16,2176]{3,2,1,0:T(8,128)(2,1)} %get-tuple-element.95), channel_id=1, source_target_pairs={{0,4},{4,0},{8,12},{12,8},{16,20},{20,16},{24,28},{28,24},{1,5},{5... | collective-permute-start | bytes 3342344 | tf_op jit(solution)/shard_map/ppermute | solution.py:78
  148.5 15.3 %collective-permute-start.20 = (bf16[256,512]{1,0:T(8,128)(2,1)S(1)}, bf16[256,512]{1,0:T(8,128)(2,1)S(1)}, u32[]{:S(2)}, u32[]{:S(2)}) collective-permute-start(bf16[256,512]{1,0:T(8,128)(2,1)S(1)} %add_convert_fusion.10), channel_id=1, source_target_pairs={{1,0},{2,1},{3,2},{5,4},{6,5},{7,6},{9,8},{10,9},{11,10},{13,12},{... | collective-permute-start | bytes 786440 | tf_op jit(solution)/shard_map/ppermute | solution.py:82
  157.1 11.9 %collective-permute-start.22 = (bf16[4,16,2176]{2,1,0:T(8,128)(2,1)S(1)}, bf16[4,16,2176]{2,1,0:T(8,128)(2,1)S(1)}, u32[]{:S(2)}, u32[]{:S(2)}) collective-permute-start(bf16[4,16,2176]{2,1,0:T(8,128)(2,1)S(1)} %get-tuple-element.114), channel_id=1, source_target_pairs={{0,8},{4,12},{8,0},{12,4},{16,24},{20,28},{24,16},{28,20},{1,9},{5... | collective-permute-start | bytes 835592 | tf_op jit(solution)/shard_map/ppermute | solution.py:78
  158.0 14.0 %collective-permute-start.23 = (bf16[4,16,2176]{2,1,0:T(8,128)(2,1)S(1)}, bf16[4,16,2176]{2,1,0:T(8,128)(2,1)S(1)}, u32[]{:S(2)}, u32[]{:S(2)}) collective-permute-start(bf16[4,16,2176]{2,1,0:T(8,128)(2,1)S(1)} %get-tuple-element.113), channel_id=1, source_target_pairs={{0,16},{4,20},{8,24},{12,28},{16,0},{20,4},{24,8},{28,12},{1,17},{... | collective-permute-start | bytes 835592 | tf_op jit(solution)/shard_map/ppermute | solution.py:78
  159.5 12.5 %collective-permute-start.24 = (bf16[4,16,2176]{2,1,0:T(8,128)(2,1)S(1)}, bf16[4,16,2176]{2,1,0:T(8,128)(2,1)S(1)}, u32[]{:S(2)}, u32[]{:S(2)}) collective-permute-start(bf16[4,16,2176]{2,1,0:T(8,128)(2,1)S(1)} %get-tuple-element.112), channel_id=1, source_target_pairs={{0,24},{4,28},{8,16},{12,20},{16,8},{20,12},{24,0},{28,4},{1,25},{... | collective-permute-start | bytes 835592 | tf_op jit(solution)/shard_map/ppermute | solution.py:78
  160.7 16.8 %collective-permute-start.35 = (bf16[16,4608]{1,0:T(8,128)(2,1)S(1)}, bf16[16,4608]{1,0:T(8,128)(2,1)S(1)}, u32[]{:S(2)}, u32[]{:S(2)}) collective-permute-start(bf16[16,4608]{1,0:T(8,128)(2,1)S(1)} %get-tuple-element.115), channel_id=1, source_target_pairs={{0,1},{1,0},{2,3},{3,2},{4,5},{5,4},{6,7},{7,6},{8,9},{9,8},{10,11... | collective-permute-start | bytes 442376 | tf_op jit(solution)/shard_map/ppermute | solution.py:78
  163.9 13.6 %collective-permute-start.36 = (bf16[16,4608]{1,0:T(8,128)(2,1)S(1)}, bf16[16,4608]{1,0:T(8,128)(2,1)S(1)}, u32[]{:S(2)}, u32[]{:S(2)}) collective-permute-start(bf16[16,4608]{1,0:T(8,128)(2,1)S(1)} %get-tuple-element.117), channel_id=1, source_target_pairs={{0,2},{1,3},{2,0},{3,1},{4,6},{5,7},{6,4},{7,5},{8,10},{9,11},{10,... | collective-permute-start | bytes 442376 | tf_op jit(solution)/shard_map/ppermute | solution.py:78
  (39 other events, 418.9 us)

commit v3 on v2

--- a/solution.py
+++ b/solution.py
@@ -36,8 +36,15 @@
         self.ffp = self.down_pad * self.grp
         self.local = tokens_shape[1] // self.grp
         self.full = self.local * self.grp
-        self.wide_a = 4 * D + 128
-        self.wide_b = 2 * self.ffp + self.pieces * D
+        self.wide_a = 3 * D + 128
+        self.tall_b = 2 * self.ffp + D
+        self.wide_b = self.tall_b + self.pieces * D
+        self.line = [bit for bit in (1, 2, 4, 8, 16) if bit < self.grp]
+        self.plane = [bit for bit in (1, 2, 4, 8, 16) if bit < self.half]
+        order = [0]
+        for bit in reversed(self.line):
+            order += [k ^ bit for k in order]
+        self.order = order[1:]
 
 
 def dot(left, right, dims):
@@ -56,7 +63,7 @@
     return dot(left, right, ((0,), (0,)))
 
 
-def call(body, outs, name, args, scratch=(), flops=0, moved=0):
+def call(body, outs, name, args, scratch=(), us=0):
     specs = [SMEM if a.dtype == jnp.int32 and a.ndim == 1 else VMEM for a in args]
     return pl.pallas_call(
         body,
@@ -65,7 +72,7 @@
         out_specs=[VMEM] * len(outs),
         scratch_shapes=scratch,
         compiler_params=PARAMS,
-        cost_estimate=pl.CostEstimate(flops=0, bytes_accessed=0, transcendentals=0),
+        cost_estimate=pl.CostEstimate(flops=us * 10**9, bytes_accessed=0, transcendentals=0),
         name=name,
     )(*args)
 
@@ -150,21 +157,23 @@
 def each_slice(plan, place, slice_id, mine, part, store):
     for c, source in enumerate((mine, part)):
         for o in range(plan.half):
-            for k in range(1, plan.grp):
-                row = (o * (plan.grp - 1) + k - 1) * SR
-                store(xor(place, k), xor(slice_id, 2 * o + c), source[row : row + SR, :])
-
-
-def pack_a_kernel(plan, ids, wq, wk, wv, wo, gain1, gain2, out_ref):
+            for i, k in enumerate(plan.order):
+                row = (o * (plan.grp - 1) + i) * SR
+                rows = [ref[row : row + SR, :] for ref in source]
+                rows = jnp.concatenate(rows, axis=1) if len(rows) > 1 else rows[0]
+                store(xor(place, k), xor(slice_id, 2 * o + c), rows)
+
+
+def pack_a_kernel(plan, ids, wq, wk, wv, gain1, gain2, out_ref):
     start = aligned(ids[1] * SR)
-    for i, w in enumerate((wq, wk, wv, wo)):
+    for i, w in enumerate((wq, wk, wv)):
         out_ref[:, i * D : (i + 1) * D] = w[pl.ds(start, SR), :]
-    out_ref[:, 4 * D :] = jnp.zeros((SR, 128), BF16)
-    out_ref[0:1, 4 * D : 4 * D + plan.rows] = gain1[...]
-    out_ref[1:2, 4 * D : 4 * D + plan.rows] = gain2[...]
-
-
-def pack_b_kernel(plan, ids, gate_t, up_t, down, own_ref, slab_ref):
+    out_ref[:, 3 * D :] = jnp.zeros((SR, 128), BF16)
+    out_ref[0:1, 3 * D : 3 * D + plan.rows] = gain1[...]
+    out_ref[1:2, 3 * D : 3 * D + plan.rows] = gain2[...]
+
+
+def pack_b_kernel(plan, ids, gate_t, up_t, out, down, own_ref, slab_ref):
     for i, w in enumerate((gate_t, up_t)):
         for z in range(plan.grp):
             rows = w[z * plan.down : (z + 1) * plan.down, :].astype(F32)
@@ -172,6 +181,7 @@
             at = i * plan.ffp + z * plan.down_pad
             block = jnp.concatenate([rows, gap], axis=0).T
             own_ref[:, at : at + plan.down_pad] = block.astype(BF16)
+    own_ref[:, 2 * plan.ffp : plan.tall_b] = out[...]
     for s in range(plan.slices):
         for i in range(plan.pieces):
             at = (s * plan.pieces + i) * SR
@@ -181,7 +191,7 @@
                 rows.append(down[at : at + have, :])
             if have < SR:
                 rows.append(jnp.zeros((SR - have, D), BF16))
-            cols = slice(2 * plan.ffp + i * D, 2 * plan.ffp + (i + 1) * D)
+            cols = slice(plan.tall_b + i * D, plan.tall_b + (i + 1) * D)
             own_ref[s * SR : (s + 1) * SR, cols] = (
                 jnp.concatenate(rows, axis=0) if len(rows) > 1 else rows[0]
             )
@@ -195,29 +205,43 @@
             target[pl.ds(aligned(s * SR), SR), :] = source[o * SR : (o + 1) * SR, :]
 
 
-def finish_a_kernel(plan, ids, mine, part, *refs):
+def row_sums(value):
+    ones = jnp.ones((8, value.shape[1]), F32)
+    return lax.dot_general(
+        ones, value, (((1,), (1,)), ((), ())), precision=lax.Precision.HIGHEST,
+        preferred_element_type=F32,
+    )[0:1, :]
+
+
+def finish_a_kernel(plan, ids, mine, part, wq, wk, wv, gain, *refs):
     scratch = refs[-1]
     gather_slices(plan, ids[1], mine, part, scratch)
-    for i in range(4):
-        refs[i][...] = scratch[:, i * D : (i + 1) * D].astype(F32)
-    norms = scratch[0:SR, 4 * D : 4 * D + plan.rows].astype(F32)
-    refs[4][...] = norms[0:1, :]
-    refs[5][...] = norms[1:2, :]
-
-
-def finish_b_kernel(plan, ids, mine, part, gate_ref, up_ref, down_ref, scratch):
+    dots = jnp.zeros((plan.rows, D), F32)
+    for i, w in enumerate((wq, wk, wv)):
+        grad = scratch[:, i * D : (i + 1) * D].astype(F32)
+        refs[i][...] = grad
+        dots = dots + grad * w[...].astype(F32)
+    refs[3][...] = row_sums(dots) / gain[...].astype(F32)
+
+
+def finish_b_kernel(plan, ids, mine, part, gate_t, up_t, gain, gate_ref, up_ref, down_ref, out_ref, norm_ref, scratch):
     gather_slices(plan, ids[1], mine, part, scratch)
-    for i, ref in enumerate((gate_ref, up_ref)):
+    norm = jnp.zeros((1, plan.rows), F32)
+    for i, (ref, weight) in enumerate(((gate_ref, gate_t), (up_ref, up_t))):
         for z in range(plan.grp):
             at = i * plan.ffp + z * plan.down_pad
-            block = scratch[:, at : at + plan.down_pad].astype(F32).T
-            ref[z * plan.down : (z + 1) * plan.down, :] = block[: plan.down, :]
+            block = scratch[:, at : at + plan.down_pad].astype(F32).T[: plan.down, :]
+            rows = slice(z * plan.down, (z + 1) * plan.down)
+            ref[rows, :] = block
+            norm = norm + jnp.sum(block * weight[rows, :].astype(F32), axis=0, keepdims=True)
+    norm_ref[...] = norm / gain[...].astype(F32)
+    out_ref[...] = scratch[:, 2 * plan.ffp : plan.tall_b].astype(F32)
     for s in range(plan.slices):
         for i in range(plan.pieces):
             at = (s * plan.pieces + i) * SR
             have = max(0, min(SR, plan.down - at))
             if have:
-                cols = slice(2 * plan.ffp + i * D, 2 * plan.ffp + (i + 1) * D)
+                cols = slice(plan.tall_b + i * D, plan.tall_b + (i + 1) * D)
                 rows = scratch[s * SR : (s + 1) * SR, cols].astype(F32)
                 down_ref[at : at + have, :] = rows[:have, :]
 
@@ -225,19 +249,19 @@
 def attend_kernel(plan, ids, *refs):
     g = plan.grp
     parts = refs[:g]
-    own = refs[g : g + 4]
-    mine, part, gain, cosine, sines, reach = refs[g + 4 : g + 10]
-    attn_ref, q_ref, k_ref, v_ref, n1_ref, lse_ref, wa_ref = refs[g + 10 : g + 17]
-    bias_ref, = refs[g + 17 :]
+    own = refs[g : g + 3]
+    mine, part, gain, cosine, sines, reach = refs[g + 3 : g + 9]
+    attn_ref, q_ref, k_ref, v_ref, n1_ref, lse_ref, wa_ref = refs[g + 9 : g + 16]
+    bias_ref, = refs[g + 16 :]
     n = plan.local
     place, slice_id = ids[0], ids[1]
-    for i in range(4):
+    for i in range(3):
         wa_ref[pl.ds(aligned(place * plan.rows), plan.rows), i * D : (i + 1) * D] = own[i][...]
 
     def store(z, s, rows):
-        wa_ref[pl.ds(aligned(z * plan.rows + s * SR), SR), :] = rows[:, : 4 * D]
-
-    each_slice(plan, place, slice_id, mine, part, store)
+        wa_ref[pl.ds(aligned(z * plan.rows + s * SR), SR), :] = rows[:, : 3 * D]
+
+    each_slice(plan, place, slice_id, [mine], [part], store)
     mask_bias(plan, reach[...], bias_ref)
     gains = gain[...]
     for k in range(g):
@@ -269,17 +293,18 @@
 
 
 def mlp_kernel(plan, ids, *refs):
-    attn, x0, wa, gain, cot, own, mine, part = refs[:8]
-    out_ref, dx1_ref, dout_ref, dattn_ref, n2_ref, hid_ref, dg_ref, dup_ref, attn_ref, norm_ref = refs[8:18]
+    attn, x0, gain, cot, own = refs[:5]
+    mine, part = refs[5:7], refs[7:9]
+    out_ref, dx1_ref, dout_ref, dattn_ref, n2_ref, hid_ref, dg_ref, dup_ref, attn_ref = refs[9:18]
     wgu_ref, wd_ref = refs[18:]
-    ffp = plan.ffp
+    ffp, tall = plan.ffp, plan.tall_b
     place, slice_id = ids[0], ids[1]
 
     def store(z, s, rows):
-        wgu_ref[pl.ds(aligned(z * plan.rows + s * SR), SR), :] = rows[:, : 2 * ffp]
+        wgu_ref[pl.ds(aligned(z * plan.rows + s * SR), SR), :] = rows[:, :tall]
         for i in range(plan.pieces):
             at = z * plan.down_pad + (s * plan.pieces + i) * SR
-            wd_ref[pl.ds(aligned(at), SR), :] = rows[:, 2 * ffp + i * D : 2 * ffp + (i + 1) * D]
+            wd_ref[pl.ds(aligned(at), SR), :] = rows[:, tall + i * D : tall + (i + 1) * D]
 
     for s in range(plan.slices):
         store(place, s, own[s * SR : (s + 1) * SR, :])
@@ -287,7 +312,7 @@
 
     attn_low = attn[...].astype(BF16)
     attn_ref[...] = attn_low
-    x1 = x0[...].astype(F32) + mm(attn_low, wa[:, 3 * D : 4 * D])
+    x1 = x0[...].astype(F32) + mm(attn_low, wgu_ref[:, 2 * ffp :])
     scale = lax.rsqrt(jnp.mean(x1 * x1, axis=1, keepdims=True) + EPSILON)
     unit = x1 * scale
     gains = gain[...]
@@ -314,13 +339,12 @@
         out = out + mm(hid, wd_ref[cols, :])
         dn2 = dn2 + against(dg, wgu_ref[:, cols]) + against(dup, wgu_ref[:, up_cols])
     out_ref[...] = out.astype(BF16)
-    norm_ref[...] = jnp.sum(dn2 * unit, axis=0, keepdims=True)
     e2 = dn2 * gains
     dx1 = c.astype(F32) + scale * (e2 - unit * jnp.mean(e2 * unit, axis=1, keepdims=True))
     dx1_ref[...] = dx1
     dout = dx1.astype(BF16)
     dout_ref[...] = dout
-    dattn_ref[...] = against(dout, wa[:, 3 * D : 4 * D]).astype(BF16)
+    dattn_ref[...] = against(dout, wgu_ref[:, 2 * ffp :]).astype(BF16)
 
 
 def spread(plan, place, slice_id, keep, send, copy):
@@ -330,20 +354,19 @@
                 copy(xor(place, k), xor(slice_id, 2 * o + c), target, o, k)
 
 
-def mlp_grads_kernel(plan, ids, n2, hid, dg, dup, cot, keep, send, gu_ref, d_ref):
-    ffp = plan.ffp
+def mlp_grads_kernel(plan, ids, n2, hid, dg, dup, cot, attn, dout, keep, send, gu_ref, d_ref):
+    ffp, tall = plan.ffp, plan.tall_b
     n2_t = n2[...].T
     gu_ref[:, :ffp] = mm(n2_t, dg[...]).astype(BF16)
-    gu_ref[:, ffp:] = mm(n2_t, dup[...]).astype(BF16)
+    gu_ref[:, ffp : 2 * ffp] = mm(n2_t, dup[...]).astype(BF16)
+    gu_ref[:, 2 * ffp :] = rows_of(attn[...], dout[...]).astype(BF16)
     d_ref[...] = rows_of(hid[...], cot[...]).astype(BF16)
 
     def copy(z, s, target, o, k):
-        target[o, k, :, : 2 * ffp] = gu_ref[pl.ds(aligned(z * plan.rows + s * SR), SR), :]
+        target[o, k, :, :tall] = gu_ref[pl.ds(aligned(z * plan.rows + s * SR), SR), :]
         for i in range(plan.pieces):
             at = z * plan.down_pad + (s * plan.pieces + i) * SR
-            target[o, k, :, 2 * ffp + i * D : 2 * ffp + (i + 1) * D] = d_ref[
-                pl.ds(aligned(at), SR), :
-            ]
+            target[o, k, :, tall + i * D : tall + (i + 1) * D] = d_ref[pl.ds(aligned(at), SR), :]
 
     spread(plan, ids[0], ids[1], keep, send, copy)
 
@@ -382,15 +405,12 @@
 
 
 def input_kernel(plan, halves, *refs):
-    g = plan.grp
-    parts = refs[:g]
-    back = refs[g : g + 3 * halves]
-    wa, own_ref, norm_ref = refs[g + 3 * halves : g + 3 * halves + 3]
-    sends = refs[g + 3 * halves + 3 :]
+    back = refs[: 3 * halves]
+    wa, own_ref = refs[3 * halves : 3 * halves + 2]
+    sends = refs[3 * halves + 2 :]
     n = plan.local
     wide = D // halves
-    norm = jnp.zeros((1, D), F32)
-    for k in reversed(range(g)):
+    for k in reversed(range(plan.grp)):
         rows = slice(k * n, (k + 1) * n)
         dn1 = None
         for h in range(halves):
@@ -405,15 +425,11 @@
             own_ref[...] = dn1
         else:
             sends[k - 1][...] = dn1.astype(BF16)
-        x = parts[k][...].astype(F32)
-        unit = x * lax.rsqrt(jnp.mean(x * x, axis=1, keepdims=True) + EPSILON)
-        norm = norm + jnp.sum(dn1 * unit, axis=0, keepdims=True)
-    norm_ref[...] = norm
 
 
 def attend_grads_kernel(plan, halves, ids, n1, *refs):
     back = refs[: 3 * halves]
-    attn, dout, norms, keep, send, ga_ref = refs[3 * halves :]
+    keep, send, ga_ref = refs[3 * halves :]
     n1_t = n1[...].T
     wide = D // halves
     for h in range(halves):
@@ -422,12 +438,9 @@
         ga_ref[:, at : at + wide] = mm(n1_t[:, : plan.local], dq[...]).astype(BF16)
         ga_ref[:, D + at : D + at + wide] = mm(n1_t, dk[...]).astype(BF16)
         ga_ref[:, 2 * D + at : 2 * D + at + wide] = mm(n1_t, dv[...]).astype(BF16)
-    ga_ref[:, 3 * D :] = rows_of(attn[...], dout[...]).astype(BF16)
 
     def copy(z, s, target, o, k):
-        target[o, k, :, : 4 * D] = ga_ref[pl.ds(aligned(z * plan.rows + s * SR), SR), :]
-        flag = (s == 0).astype(F32)
-        target[o, k, :, 4 * D :] = (norms[z] * flag).astype(BF16)
+        target[o, k] = ga_ref[pl.ds(aligned(z * plan.rows + s * SR), SR), :]
 
     spread(plan, ids[0], ids[1], keep, send, copy)
 
@@ -454,13 +467,36 @@
 
 
 def fetch_line(plan, slab):
-    return jnp.concatenate([swap("grp", k, plan.grp, slab) for k in range(1, plan.grp)], axis=0)
+    blocks = [slab]
+    for bit in reversed(plan.line):
+        got = swap("grp", bit, plan.grp, jnp.concatenate(blocks, axis=0))
+        blocks += jnp.split(got, len(blocks), axis=0)
+    return jnp.concatenate(blocks[1:], axis=0)
 
 
 def fetch_plane(plan, block):
     return jnp.concatenate(
         [block] + [swap("rep", 2 * o, plan.rep, block) for o in range(1, plan.half)], axis=0
     )
+
+
+def fetch_plane_halves(plan, block, after):
+    terms = []
+    for half, bits in zip(column_halves(block), (plan.plane, plan.plane[::-1])):
+        terms.append(({0: half}, bits))
+    for step in range(len(plan.plane)):
+        done = []
+        for blocks, bits in terms:
+            moved = tie(jnp.concatenate(list(blocks.values()), axis=0), *after[step : step + 1])
+            got = jnp.split(swap("rep", 2 * bits[step], plan.rep, moved), len(blocks), axis=0)
+            done.append((blocks | {o ^ bits[step]: g for o, g in zip(list(blocks), got)}, bits))
+        terms = done
+    return [jnp.concatenate([mine[o] for o in range(plan.half)], axis=0) for mine, _ in terms]
+
+
+def column_halves(value):
+    middle = value.shape[-1] // 256 * 128
+    return value[..., :middle], value[..., middle:]
 
 
 def fetch_core(plan, mine):
@@ -480,20 +516,50 @@
 
 def combine_cores(plan, keep, send):
     got = swap("rep", 1, plan.rep, send)
-    return [add(keep[o], got[o]) for o in range(plan.half)]
-
-
-def combine_plane(plan, terms, after=()):
-    got = [swap("rep", 2 * o, plan.rep, terms[o]) for o in range(1, plan.half)]
-    return add(tie(terms[0], *after), *got)
-
-
-def combine_line(plan, total):
-    final = add(total[0], *[swap("grp", k, plan.grp, total[k]) for k in range(1, plan.grp)])
+    return add(keep, got)
+
+
+def plane_terms(plan, total):
+    orders = (plan.plane, plan.plane[::-1])
+    return [
+        ({o: half[o] for o in range(plan.half)}, bits)
+        for half, bits in zip(column_halves(total), orders)
+    ]
+
+
+def plane_step(plan, terms, before=(), after=()):
+    done = []
+    for mine, bits in terms:
+        leave = [o for o in mine if o & bits[0]]
+        moved = tie(jnp.stack([mine[o] for o in leave]), *before)
+        got = swap("rep", 2 * bits[0], plan.rep, moved)
+        kept = {}
+        for i, o in enumerate(leave):
+            kept[o ^ bits[0]] = add(tie(mine[o ^ bits[0]], *after), got[i])
+        done.append((kept, bits[1:]))
+    return done
+
+
+def arrays_of(terms):
+    return [value for mine, _ in terms for value in mine.values()]
+
+
+def combine_line(plan, total, after=()):
+    terms = {k: total[k] for k in range(plan.grp)}
+    for step, bit in enumerate(plan.line):
+        leave = [k for k in terms if k & bit]
+        moved = tie(jnp.stack([terms[k] for k in leave]), *after[step : step + 1])
+        got = swap("grp", bit, plan.grp, moved)
+        terms = {k ^ bit: add(terms[k ^ bit], got[i]) for i, k in enumerate(leave)}
+    final = terms[0]
     bit = plan.slices
     while bit < plan.rep:
         final = add(final, swap("rep", bit, plan.rep, final))
         bit *= 2
+    return final
+
+
+def share(plan, final):
     mine = fetch_plane(plan, final)
     return mine, fetch_core(plan, mine)
 
@@ -512,14 +578,13 @@
     )
 
 
-def pack_b(plan, ids, w_gate, w_up, w_down):
+def pack_b(plan, ids, w_gate, w_up, w_out, w_down):
     if plan.down % 8 == 0:
         return call(
             functools.partial(pack_b_kernel, plan),
             [sds((plan.rows, plan.wide_b), BF16), sds((SR, plan.wide_b), BF16)],
             "pack_b",
-            (ids, w_gate.T, w_up.T, w_down),
-            moved=3 * 10**6,
+            (ids, w_gate.T, w_up.T, w_out, w_down),
         )
     rows = jnp.pad(w_down, ((0, plan.down_pad - plan.down), (0, 0)))
     rows = rows.reshape(plan.slices, plan.pieces, SR, D).transpose(0, 2, 1, 3)
@@ -527,6 +592,7 @@
         [
             pad_columns(plan, w_gate),
             pad_columns(plan, w_up),
+            w_out,
             rows.reshape(plan.rows, plan.pieces * D),
         ],
         axis=1,
@@ -534,31 +600,35 @@
     return own, lax.dynamic_slice(own, (ids[1] * SR, 0), (SR, plan.wide_b))
 
 
-def finish_b(plan, ids, final):
+def finish_b(plan, ids, final, w_gate, w_up, gain):
+    line = gain.reshape(1, -1)
     if plan.down % 8 == 0:
         tall = sds((FF, plan.rows), F32)
-        gate, up, down = call(
+        gate, up, down, out, norm = call(
             functools.partial(finish_b_kernel, plan),
-            [tall, tall, sds((plan.down, D), F32)],
+            [tall, tall, sds((plan.down, D), F32), sds((plan.rows, D), F32), sds(line.shape, F32)],
             "finish_b",
-            (ids, *final),
+            (ids, *final, w_gate.T, w_up.T, line),
             [pltpu.VMEM((plan.rows, plan.wide_b), BF16)],
-            moved=3 * 10**6,
         )
-        return gate.T, up.T, down
+        return gate.T, up.T, down, out, norm.reshape(-1)
     (grads,) = call(
         functools.partial(finish_kernel, plan),
         [sds((plan.rows, plan.wide_b), F32)],
         "finish_b",
         (ids, *final),
-        moved=4 * 10**6,
     )
     ffp = plan.ffp
-    down = grads[:, 2 * ffp :].reshape(plan.slices, SR, plan.pieces, D).transpose(0, 2, 1, 3)
+    down = grads[:, plan.tall_b :].reshape(plan.slices, SR, plan.pieces, D).transpose(0, 2, 1, 3)
+    gate = drop_columns(plan, grads[:, :ffp])
+    up = drop_columns(plan, grads[:, ffp : 2 * ffp])
+    norm = jnp.sum(gate * w_gate.astype(F32) + up * w_up.astype(F32), axis=1) / gain.astype(F32)
     return (
-        drop_columns(plan, grads[:, :ffp]),
-        drop_columns(plan, grads[:, ffp : 2 * ffp]),
+        gate,
+        up,
         down.reshape(plan.down_pad, D)[: plan.down],
+        grads[:, 2 * ffp : plan.tall_b],
+        norm,
     )
 
 
@@ -573,33 +643,31 @@
     table_cos, table_sin = rotary_tables(plan)
     cosine, sines = jnp.asarray(table_cos), jnp.asarray(table_sin)
 
-    own_a = (w_query, w_key, w_value, w_out)
+    own_a = (w_query, w_key, w_value)
     gains = jnp.stack([norm1_gain, norm2_gain])
     (slab_a,) = call(
         functools.partial(pack_a_kernel, plan),
         [sds((SR, plan.wide_a), BF16)],
         "pack_a",
         (ids, *own_a, norm1_gain.reshape(1, -1), norm2_gain.reshape(1, -1)),
-        moved=10**6,
-    )
-    own_b, slab_b = pack_b(plan, ids, w_gate, w_up, w_down)
-
-    block_a = fetch_line(plan, slab_a)
-    block_b = fetch_line(plan, slab_b)
+        us=2,
+    )
+    own_b, slab_b = pack_b(plan, ids, w_gate, w_up, w_out, w_down)
+
     parts = [x0]
     for _ in range(1, g):
         parts.append(shift(1, g, parts[-1]))
-    mine_a = fetch_plane(plan, block_a)
-    mine_b = fetch_plane(plan, tie(block_b, mine_a))
+    block_a = fetch_line(plan, slab_a)
+    block_b = fetch_line(plan, slab_b)
+    mine_a = fetch_plane(plan, tie(block_a, parts[1]))
+    mine_b = fetch_plane_halves(plan, tie(block_b, mine_a), (parts[-2], parts[-1]))
     part_a = fetch_core(plan, mine_a)
-    part_b = fetch_core(plan, mine_b)
-
-    tiles = jnp.stack(
-        [gains] + [mine_a[k * SR : k * SR + 2, 4 * D : 4 * D + plan.rows] for k in range(g - 1)]
-    )
+
+    lines = [mine_a[i * SR : i * SR + 2, 3 * D : 3 * D + plan.rows] for i in range(g - 1)]
     order = jnp.bitwise_xor(jnp.arange(g, dtype=jnp.int32), place)
     chosen = sum(
-        jnp.where((order == k)[:, None, None], tiles[k][None], 0).astype(F32) for k in range(g)
+        jnp.where((order == k)[:, None, None], tile[None], 0).astype(F32)
+        for k, tile in zip([0, *plan.order], [gains, *lines])
     )
     gain1 = chosen[:, 0].reshape(1, D)
     gain2 = chosen[:, 1].reshape(1, D)
@@ -614,17 +682,17 @@
             sds((full, D), BF16),
             sds((full, D), BF16),
             sds((H // 2, 1, 2 * n), F32),
-            sds((D, 4 * D), BF16),
+            sds((D, 3 * D), BF16),
         ],
         "attend",
         (ids, *parts, *own_a, mine_a, part_a, gain1, cosine, sines, reach),
         [pltpu.VMEM((full, 2 * n), F32)],
-        flops=4 * 10**9,
-        moved=8 * 10**6,
-    )
+        us=11,
+    )
+    part_b = [fetch_core(plan, tie(half, attn)) for half in mine_b]
 
     ffp = plan.ffp
-    output, dx1, dout, dattn, n2, hid, dg, dup, attn_low, norm2 = call(
+    output, dx1, dout, dattn, n2, hid, dg, dup, attn_low = call(
         functools.partial(mlp_kernel, plan),
         [
             sds((n, D), BF16),
@@ -636,13 +704,11 @@
             sds((n, ffp), BF16),
             sds((n, ffp), BF16),
             sds((n, D), BF16),
-            sds((1, D), F32),
         ],
         "mlp",
-        (ids, attn, x0, wa, gain2, cot, own_b, mine_b, part_b),
-        [pltpu.VMEM((D, 2 * ffp), BF16), pltpu.VMEM((ffp, D), BF16)],
-        flops=4 * 10**9,
-        moved=12 * 10**6,
+        (ids, attn, x0, gain2, cot, own_b, *mine_b, *part_b),
+        [pltpu.VMEM((D, plan.tall_b), BF16), pltpu.VMEM((ffp, D), BF16)],
+        us=8,
     )
 
     slabs_b = sds((plan.half, g, SR, plan.wide_b), BF16)
@@ -650,10 +716,9 @@
         functools.partial(mlp_grads_kernel, plan),
         [slabs_b, slabs_b],
         "mlp_grads",
-        (ids, n2, hid, dg, dup, cot),
-        [pltpu.VMEM((D, 2 * ffp), BF16), pltpu.VMEM((ffp, D), BF16)],
-        flops=2 * 10**9,
-        moved=8 * 10**6,
+        (ids, n2, hid, dg, dup, cot, attn_low, dout),
+        [pltpu.VMEM((D, plan.tall_b), BF16), pltpu.VMEM((ffp, D), BF16)],
+        us=6,
     )
     halves = 2
     count = H // 2 // halves
@@ -670,68 +735,76 @@
                 pltpu.VMEM((n, wide), F32),
                 pltpu.VMEM((full, wide), F32),
             ],
-            flops=4 * 10**9,
-            moved=8 * 10**6,
+            us=8,
         )
 
     back = list(attend_back(0, tie(dattn, keep_b)))
-    terms_b = combine_cores(plan, keep_b, send_b)
-    back += attend_back(count, tie(dattn, *terms_b, back[0]))
-    own, norm1, *sends = call(
-        functools.partial(input_kernel, plan, halves),
-        [sds((n, D), F32), sds((1, D), F32)] + [sds((n, D), BF16)] * (g - 1),
-        "dn1",
-        (*parts, *back, wa),
-        flops=2 * 10**9,
-        moved=4 * 10**6,
-    )
-    moving = sends[g - 2]
-    for k in reversed(range(1, g)):
-        moving = shift(-1, g, moving)
-        if k > 1:
-            moving = add(moving, sends[k - 2])
-
-    norms = jnp.concatenate([norm1, norm2], axis=0).reshape(2, g, plan.rows).transpose(1, 0, 2)
-    norms = jnp.pad(norms, ((0, 0), (0, SR - 2), (0, 128 - plan.rows)))
-    slabs_a = sds((plan.half, g, SR, plan.wide_a), BF16)
+    core_b = combine_cores(plan, keep_b, send_b)
+    back += attend_back(count, tie(dattn, core_b, back[0]))
+    terms_b = plane_terms(plan, core_b)
+    steps = len(plan.plane)
+    if steps:
+        terms_b = plane_step(plan, terms_b)
+
+    slabs_a = sds((plan.half, g, SR, 3 * D), BF16)
     keep_a, send_a = call(
         functools.partial(attend_grads_kernel, plan, halves),
         [slabs_a, slabs_a],
         "attend_grads",
-        (ids, n1, *back, attn_low, dout, norms),
-        [pltpu.VMEM((D, 4 * D), BF16)],
-        flops=2 * 10**9,
-        moved=8 * 10**6,
-    )
-
-    total_b = combine_plane(plan, terms_b, (own,))
-    final_b = combine_line(plan, total_b)
-    total_a = combine_plane(plan, combine_cores(plan, keep_a, send_a))
+        (ids, n1, *back),
+        [pltpu.VMEM((D, 3 * D), BF16)],
+        us=0,
+    )
+    own, *sends = call(
+        functools.partial(input_kernel, plan, halves),
+        [sds((n, D), F32)] + [sds((n, D), BF16)] * (g - 1),
+        "dn1",
+        (*back, tie(wa, keep_a, *arrays_of(terms_b))),
+        us=4,
+    )
+    moving = sends[g - 2]
+    hops = []
+    for k in reversed(range(1, g)):
+        moving = shift(-1, g, moving)
+        hops.append(moving)
+        if k > 1:
+            moving = add(moving, sends[k - 2])
+    core_a = combine_cores(plan, keep_a, send_a)
+    terms_a = plane_terms(plan, tie(core_a, own))
+    for step in range(steps):
+        if step:
+            terms_b = plane_step(plan, terms_b, after=(own,))
+        terms_a = plane_step(plan, terms_a)
+    total_a = jnp.concatenate([mine[0] for mine, _ in terms_a], axis=-1)
+    total_b = jnp.concatenate([mine[0] for mine, _ in terms_b], axis=-1)
+    final_b = share(plan, tie(combine_line(plan, total_b, (own, hops[0])), hops[1]))
+    final_a = share(plan, tie(combine_line(plan, total_a, (hops[0], hops[1])), hops[-1]))
     (input_grad,) = call(
         functools.partial(residual_kernel, plan),
         [sds((n, D), F32)],
         "residual",
         (own, x0, dx1, gain1, moving),
-        moved=4 * 10**6,
-    )
-    final_a = combine_line(plan, tie(total_a, input_grad))
-    gate, up, down = finish_b(plan, ids, final_b)
+        us=2,
+    )
+    gate, up, down, out, norm2 = finish_b(plan, ids, final_b, w_gate, w_up, norm2_gain)
     shard = sds((plan.rows, D), F32)
-    line = sds((1, plan.rows), F32)
-    grads_a = call(
+    query, key, value, norm1 = call(
         functools.partial(finish_a_kernel, plan),
-        [shard, shard, shard, shard, line, line],
+        [shard, shard, shard, sds((1, plan.rows), F32)],
         "finish_a",
-        (ids, *final_a),
-        [pltpu.VMEM((plan.rows, plan.wide_a), BF16)],
-        moved=2 * 10**6,
+        (ids, *final_a, *own_a, norm1_gain.reshape(1, -1)),
+        [pltpu.VMEM((plan.rows, 3 * D), BF16)],
+        us=2,
     )
     return (
         output.reshape(tokens.shape),
         input_grad.reshape(tokens.shape),
-        grads_a[4].reshape(plan.rows),
-        *grads_a[:4],
-        grads_a[5].reshape(plan.rows),
+        norm1.reshape(-1),
+        query,
+        key,
+        value,
+        out,
+        norm2,
         gate,
         up,
         down,

time: 199 us -> 180 us (0.905)
  waiting for transfers between devices: 59.7 us -> 46.9 us
  starting transfers between devices: 64.2 us -> 60.3 us
    ppermute x6, waiting for transfers between devices: 23.4 us -> 13.1 us  [shift(): lax.ppermute(value, 'grp', [(i, i + k) for i in range(size) if 0 <= i + k...]
    ppermute x36, starting transfers between devices: 48.2 us -> 43.6 us  [swap(): return lax.ppermute(value, axis, [(i, i ^ k) for i in range(size)])]
    ppermute x36, waiting for transfers between devices: 36.3 us -> 33.8 us  [swap(): return lax.ppermute(value, axis, [(i, i ^ k) for i in range(size)])]
  transfers between devices with their start and end apart: 42 -> 42, of which waited for: 17 -> 20; matrix products, arithmetic and copies ran while one was open for 2% -> 2% of each run, Pallas kernels for 16% -> 23%
where the time goes in v3:
time: 180 us; the launch traced here: 179 us
  Pallas kernels  61.5 us (34%)
  starting transfers between devices  60.3 us (34%)
  waiting for transfers between devices  46.9 us (26%)
  other arithmetic  4.64 us (3%)
  local copies, waits for them, and re-layouts  4.48 us (2%)
    pallas_call x12, Pallas kernels, call(): pl.pallas_call(body, out_shape=outs, in_specs=specs, out_specs=[VMEM] * l...  61.5 us
    ppermute x36, starting transfers between devices, swap(): return lax.ppermute(value, axis, [(i, i ^ k) for i in range(size)])  43.6 us
    ppermute x36, waiting for transfers between devices, swap(): return lax.ppermute(value, axis, [(i, i ^ k) for i in range(size)])  33.8 us
    ppermute x6, starting transfers between devices, shift(): lax.ppermute(value, 'grp', [(i, i + k) for i in range(size) if 0 <= i + k...  16.7 us
    ppermute x6, waiting for transfers between devices, shift(): lax.ppermute(value, 'grp', [(i, i + k) for i in range(size) if 0 <= i + k...  13.1 us
  transfers between devices with their start and end apart: 42, of which 20 were waited for; matrix products, arithmetic and copies ran while one was open for 2% of the time, Pallas kernels for 23%

profile of v3, /device:TPU:0, one launch (start us, length us, event | category | flops | bytes accessed | tf_op | source)
XLA Modules:
  0.0 179.0 jit_solution(8795808599422912315)
XLA Ops:
  1.2 2.6 %pack_b.1 = (bf16[128,5120]{1,0:T(8,128)(2,1)}, bf16[16,5120]{1,0:T(8,128)(2,1)}) custom-call(s32[2]{0:T(128)} %pad_add_fusion.ids, bf16[1376,128]{1,0:T(8,128)(2,1)} %bitcast.94, bf16[1376,128]{1,0:T(8,128)(2,1)} %bitcast.96, bf16[128,512]{1,0:T(8,128)(2,1)} %out.1, bf16[344,512]{1,0:T(8,128)(2,1)} %down.1), custom_call_target="tpu_custom_call" | custom-call | tf_op jit(solution)/shard_map/pack_b/pallas_call | solution.py:68
  3.9 4.1 %collective-permute-start.9 = (bf16[16,5120]{1,0:T(8,128)(2,1)}, bf16[16,5120]{1,0:T(8,128)(2,1)S(1)}, u32[]{:S(2)}, u32[]{:S(2)}) collective-permute-start(bf16[16,5120]{1,0:T(8,128)(2,1)} %get-tuple-element.75), channel_id=1, source_target_pairs={{0,2},{1,3},{2,0},{3,1},{4,6},{5,7},{6,4},{7,5},{8,10},{9,11},{10,... | collective-permute-start | bytes 491528 | tf_op jit(solution)/shard_map/ppermute | solution.py:85
  9.8 3.7 %collective-permute-start = (bf16[256,512]{1,0:T(8,128)(2,1)S(1)}, bf16[256,512]{1,0:T(8,128)(2,1)S(1)}, u32[]{:S(2)}, u32[]{:S(2)}) collective-permute-start(bf16[256,512]{1,0:T(8,128)(2,1)S(1)} %bitcast.113), channel_id=1, source_target_pairs={{0,1},{1,2},{2,3},{4,5},{5,6},{6,7},{8,9},{9,10},{10,11},{12,13},{... | collective-permute-start | bytes 786440 | tf_op jit(solution)/shard_map/ppermute | solution.py:89
  14.2 4.0 %collective-permute-done.3 = bf16[16,1664]{1,0:T(8,128)(2,1)S(1)} collective-permute-done((bf16[16,1664]{1,0:T(8,128)(2,1)}, bf16[16,1664]{1,0:T(8,128)(2,1)S(1)}, u32[]{:S(2)}, u32[]{:S(2)}) %collective-permute-start.3) | collective-permute-done | bytes 53280 | tf_op jit(solution)/shard_map/ppermute | solution.py:85
  20.0 3.7 %collective-permute-done.4 = bf16[32,1664]{1,0:T(8,128)(2,1)S(1)} collective-permute-done((bf16[32,1664]{1,0:T(8,128)(2,1)S(1)}, bf16[32,1664]{1,0:T(8,128)(2,1)S(1)}, u32[]{:S(2)}, u32[]{:S(2)}) %collective-permute-start.4) | collective-permute-done | bytes 106528 | tf_op jit(solution)/shard_map/ppermute | solution.py:85
  28.5 2.9 %collective-permute-start.1 = (bf16[256,512]{1,0:T(8,128)(2,1)S(1)}, bf16[256,512]{1,0:T(8,128)(2,1)S(1)}, u32[]{:S(2)}, u32[]{:S(2)}) collective-permute-start(bf16[256,512]{1,0:T(8,128)(2,1)S(1)} %collective-permute-done.refs_1_), channel_id=1, source_target_pairs={{0,1},{1,2},{2,3},{4,5},{5,6},{6,7},{8,9},{9,10},{10,11},{12,13},{... | collective-permute-start | bytes 786440 | tf_op jit(solution)/shard_map/ppermute | solution.py:89
  31.8 3.2 %collective-permute-done.6 = bf16[48,1664]{1,0:T(8,128)(2,1)S(1)} collective-permute-done((bf16[48,1664]{1,0:T(8,128)(2,1)S(1)}, bf16[48,1664]{1,0:T(8,128)(2,1)S(1)}, u32[]{:S(2)}, u32[]{:S(2)}) %collective-permute-start.6) | collective-permute-done | bytes 159776 | tf_op jit(solution)/shard_map/ppermute | solution.py:85
  40.4 6.1 %collective-permute-start.2 = (bf16[256,512]{1,0:T(8,128)(2,1)S(1)}, bf16[256,512]{1,0:T(8,128)(2,1)S(1)}, u32[]{:S(2)}, u32[]{:S(2)}) collective-permute-start(bf16[256,512]{1,0:T(8,128)(2,1)S(1)} %collective-permute-done.1.refs_2_), channel_id=1, source_target_pairs={{0,1},{1,2},{2,3},{4,5},{5,6},{6,7},{8,9},{9,10},{10,11},{12,13},{... | collective-permute-start | bytes 786440 | tf_op jit(solution)/shard_map/ppermute | solution.py:89
  46.6 3.7 %collective-permute-done.2.refs_3_ = bf16[256,512]{1,0:T(8,128)(2,1)S(1)} collective-permute-done((bf16[256,512]{1,0:T(8,128)(2,1)S(1)}, bf16[256,512]{1,0:T(8,128)(2,1)S(1)}, u32[]{:S(2)}, u32[]{:S(2)}) %collective-permute-start.2) | collective-permute-done | bytes 262176 | tf_op jit(solution)/shard_map/ppermute | solution.py:89
  52.3 11.1 %attend.1 = (f32[256,512]{1,0:T(8,128)}, bf16[256,512]{1,0:T(8,128)(2,1)}, bf16[1024,512]{1,0:T(8,128)(2,1)}, bf16[1024,512]{1,0:T(8,128)(2,1)}, bf16[1024,512]{...) custom-call(s32[2]{0:T(128)} %pad_add_fusion.ids, bf16[256,512]{1,0:T(8,128)(2,1)} %bitcast.110, ...), custom_call_target="tpu_custom_call" | custom-call | flops 11000000512 | tf_op jit(solution)/shard_map/attend/pallas_call | solution.py:68
  68.5 7.9 %mlp.1 = (bf16[256,512]{1,0:T(8,128)(2,1)}, f32[256,512]{1,0:T(8,128)}, bf16[256,512]{1,0:T(8,128)(2,1)}, bf16[256,512]{1,0:T(8,128)(2,1)}, bf16[256,512]{1,0:T(...) custom-call(s32[2]{0:T(128)} %pad_add_fusion.ids, ...), custom_call_target="tpu_custom_call" | custom-call | flops 8000000000 | tf_op jit(solution)/shard_map/mlp/pallas_call | solution.py:68
  76.5 6.0 %mlp_grads.1 = (bf16[4,4,16,5120]{3,2,1,0:T(8,128)(2,1)}, bf16[4,4,16,5120]{3,2,1,0:T(8,128)(2,1)}) custom-call(s32[2]{0:T(128)} %pad_add_fusion.ids, bf16[256,512]{1,0:T(8,128)(2,1)} %get-tuple-element.88.n2, bf16[256,1536]{1,0:T(8,128)(2,1)} %get-tuple-element.89.hid, bf16[256,1536]{1,0:T(8,128)(2,1)} %get-tuple-element.90.dg, ...), custom_call_target="tpu_custom_call" | custom-call | flops 6000000000 | tf_op jit(solution)/shard_map/mlp_grads/pallas_call | solution.py:68
  82.6 7.6 %attend_back.2 = (bf16[256,256]{1,0:T(8,128)(2,1)}, bf16[1024,256]{1,0:T(8,128)(2,1)}, bf16[1024,256]{1,0:T(8,128)(2,1)}) custom-call(bf16[256,512]{1,0:T(8,128)(2,1)} %get-tuple-element.84.q, bf16[1024,512]{1,0:T(8,128)(2,1)} %get-tuple-element.85.k_in, bf16[1024,512]{1,0:T(8,128)(2,1)} %get-tuple-element.86.v_in, ...), custom_call_target="tpu_custom_call" | custom-call | flops 8000000000 | tf_op jit(solution)/shard_map/attend_back/pallas_call | solution.py:68
  94.6 7.7 %attend_back.3 = (bf16[256,256]{1,0:T(8,128)(2,1)}, bf16[1024,256]{1,0:T(8,128)(2,1)}, bf16[1024,256]{1,0:T(8,128)(2,1)}) custom-call(bf16[256,512]{1,0:T(8,128)(2,1)} %get-tuple-element.84.q, bf16[1024,512]{1,0:T(8,128)(2,1)} %get-tuple-element.85.k_in, bf16[1024,512]{1,0:T(8,128)(2,1)} %get-tuple-element.86.v_in, ...), custom_call_target="tpu_custom_call" | custom-call | flops 8000000000 | tf_op jit(solution)/shard_map/attend_back/pallas_call | solution.py:68
  102.3 4.6 %attend_grads.1 = (bf16[4,4,16,1536]{3,2,1,0:T(8,128)(2,1)}, bf16[4,4,16,1536]{3,2,1,0:T(8,128)(2,1)}) custom-call(s32[2]{0:T(128)} %pad_add_fusion.ids, bf16[1024,512]{1,0:T(8,128)(2,1)} %get-tuple-element.106.n1, bf16[256,256]{1,0:T(8,128)(2,1)} %get-tuple-element.97.refs_0_, bf16[1024,256]{1,0:T(8,128)(2,1)} %get-tuple-element.98.refs_1_, ...), custom_call_target="tpu_custom_call" | custom-call | tf_op jit(solution)/shard_map/attend_grads/pallas_call | solution.py:68
  110.0 4.4 %dn1.1 = (f32[256,512]{1,0:T(8,128)}, bf16[256,512]{1,0:T(8,128)(2,1)}, bf16[256,512]{1,0:T(8,128)(2,1)}, bf16[256,512]{1,0:T(8,128)(2,1)}) custom-call(bf16[256,256]{1,0:T(8,128)(2,1)} %get-tuple-element.97.refs_0_, bf16[1024,256]{1,0:T(8,128)(2,1)} %get-tuple-element.98.refs_1_, bf16[1024,256]{1,0:T(8,128)(2,1)} %get-tuple-element.99.refs_2_, ...), custom_call_target="tpu_custom_call" | custom-call | flops 4000000000 | tf_op jit(solution)/shard_map/dn1/pallas_call | solution.py:68
  120.4 6.6 %collective-permute-done.20 = bf16[256,512]{1,0:T(8,128)(2,1)S(1)} collective-permute-done((bf16[256,512]{1,0:T(8,128)(2,1)}, bf16[256,512]{1,0:T(8,128)(2,1)S(1)}, u32[]{:S(2)}, u32[]{:S(2)}) %collective-permute-start.20) | collective-permute-done | bytes 262176 | tf_op jit(solution)/shard_map/ppermute | solution.py:89
  134.1 3.2 %collective-permute-start.28 = (bf16[2,16,1536]{2,1,0:T(8,128)(2,1)S(1)}, bf16[2,16,1536]{2,1,0:T(8,128)(2,1)S(1)}, u32[]{:S(2)}, u32[]{:S(2)}) collective-permute-start(bf16[2,16,1536]{2,1,0:T(8,128)(2,1)S(1)} %pad_maximum_fusion.12), channel_id=1, source_target_pairs={{0,1},{1,0},{2,3},{3,2},{4,5},{5,4},{6,7},{7,6},{8,9},{9,8},{10,11... | collective-permute-start | bytes 294920 | tf_op jit(solution)/shard_map/ppermute | solution.py:85
  137.5 3.5 %collective-permute-done.28 = bf16[2,16,1536]{2,1,0:T(8,128)(2,1)S(1)} collective-permute-done((bf16[2,16,1536]{2,1,0:T(8,128)(2,1)S(1)}, bf16[2,16,1536]{2,1,0:T(8,128)(2,1)S(1)}, u32[]{:S(2)}, u32[]{:S(2)}) %collective-permute-start.28) | collective-permute-done | bytes 98336 | tf_op jit(solution)/shard_map/ppermute | solution.py:85
  141.0 4.4 %collective-permute-start.29 = (bf16[1,16,1536]{2,1,0:T(8,128)(2,1)S(1)}, bf16[1,16,1536]{2,1,0:T(8,128)(2,1)S(1)}, u32[]{:S(2)}, u32[]{:S(2)}) collective-permute-start(bf16[1,16,1536]{2,1,0:T(8,128)(2,1)S(1)} %add_convert_fusion.8), channel_id=1, source_target_pairs={{0,2},{1,3},{2,0},{3,1},{4,6},{5,7},{6,4},{7,5},{8,10},{9,11},{10,... | collective-permute-start | bytes 147464 | tf_op jit(solution)/shard_map/ppermute | solution.py:85
  148.1 4.4 %collective-permute-start.37 = (bf16[1,16,5120]{2,1,0:T(8,128)(2,1)S(1)}, bf16[1,16,5120]{2,1,0:T(8,128)(2,1)S(1)}, u32[]{:S(2)}, u32[]{:S(2)}) collective-permute-start(bf16[1,16,5120]{2,1,0:T(8,128)(2,1)S(1)} %add_convert_fusion.5), channel_id=1, source_target_pairs={{0,2},{1,3},{2,0},{3,1},{4,6},{5,7},{6,4},{7,5},{8,10},{9,11},{10,... | collective-permute-start | bytes 491528 | tf_op jit(solution)/shard_map/ppermute | solution.py:85
  157.3 2.9 %collective-permute-done.37 = bf16[1,16,5120]{2,1,0:T(8,128)(2,1)S(1)} collective-permute-done((bf16[1,16,5120]{2,1,0:T(8,128)(2,1)S(1)}, bf16[1,16,5120]{2,1,0:T(8,128)(2,1)S(1)}, u32[]{:S(2)}, u32[]{:S(2)}) %collective-permute-start.37) | collective-permute-done | bytes 163872 | tf_op jit(solution)/shard_map/ppermute | solution.py:85
  165.7 3.3 %collective-permute-done.39 = bf16[16,5120]{1,0:T(8,128)(2,1)S(1)} collective-permute-done((bf16[16,5120]{1,0:T(8,128)(2,1)S(1)}, bf16[16,5120]{1,0:T(8,128)(2,1)S(1)}, u32[]{:S(2)}, u32[]{:S(2)}) %collective-permute-start.39) | collective-permute-done | bytes 163872 | tf_op jit(solution)/shard_map/ppermute | solution.py:85
  175.9 3.2 %finish_b.1 = (f32[1376,128]{1,0:T(8,128)}, f32[1376,128]{1,0:T(8,128)}, f32[344,512]{1,0:T(8,128)}, f32[128,512]{1,0:T(8,128)}, f32[1,128]{1,0:T(1,128)}) custom-call(s32[2]{0:T(128)} %pad_add_fusion.ids, bf16[64,5120]{1,0:T(8,128)(2,1)} %copy-done.1, bf16[64,5120]{1,0:T(8,128)(2,1)} %copy-done.5, bf16[1376,128]{1,0:T(8,128)(2,1)} %bitcast.95, ...), custom_call_target="tpu_custom_call" | custom-call | tf_op jit(solution)/shard_map/finish_b/pallas_call | solution.py:68
  (175 shorter events, 62.9 us)
Async XLA Ops:
  3.9 19.9 %collective-permute-start.9 = (bf16[16,5120]{1,0:T(8,128)(2,1)}, bf16[16,5120]{1,0:T(8,128)(2,1)S(1)}, u32[]{:S(2)}, u32[]{:S(2)}) collective-permute-start(bf16[16,5120]{1,0:T(8,128)(2,1)} %get-tuple-element.75), channel_id=1, source_target_pairs={{0,2},{1,3},{2,0},{3,1},{4,6},{5,7},{6,4},{7,5},{8,10},{9,11},{10,... | collective-permute-start | bytes 491528 | tf_op jit(solution)/shard_map/ppermute | solution.py:85
  9.7 8.4 %collective-permute-start.3 = (bf16[16,1664]{1,0:T(8,128)(2,1)}, bf16[16,1664]{1,0:T(8,128)(2,1)S(1)}, u32[]{:S(2)}, u32[]{:S(2)}) collective-permute-start(bf16[16,1664]{1,0:T(8,128)(2,1)} %pack_a.1), channel_id=1, source_target_pairs={{0,2},{1,3},{2,0},{3,1},{4,6},{5,7},{6,4},{7,5},{8,10},{9,11},{10,... | collective-permute-start | bytes 159752 | tf_op jit(solution)/shard_map/ppermute | solution.py:85
  9.8 15.1 %collective-permute-start = (bf16[256,512]{1,0:T(8,128)(2,1)S(1)}, bf16[256,512]{1,0:T(8,128)(2,1)S(1)}, u32[]{:S(2)}, u32[]{:S(2)}) collective-permute-start(bf16[256,512]{1,0:T(8,128)(2,1)S(1)} %bitcast.113), channel_id=1, source_target_pairs={{0,1},{1,2},{2,3},{4,5},{5,6},{6,7},{8,9},{9,10},{10,11},{12,13},{... | collective-permute-start | bytes 786440 | tf_op jit(solution)/shard_map/ppermute | solution.py:89
  23.8 11.4 %collective-permute-start.10 = (bf16[32,5120]{1,0:T(8,128)(2,1)S(1)}, bf16[32,5120]{1,0:T(8,128)(2,1)S(1)}, u32[]{:S(2)}, u32[]{:S(2)}) collective-permute-start(bf16[32,5120]{1,0:T(8,128)(2,1)S(1)} %pad_maximum_fusion.6), channel_id=1, source_target_pairs={{0,1},{1,0},{2,3},{3,2},{4,5},{5,4},{6,7},{7,6},{8,9},{9,8},{10,11... | collective-permute-start | bytes 983048 | tf_op jit(solution)/shard_map/ppermute | solution.py:85
  26.5 8.5 %collective-permute-start.6 = (bf16[48,1664]{1,0:T(8,128)(2,1)S(1)}, bf16[48,1664]{1,0:T(8,128)(2,1)S(1)}, u32[]{:S(2)}, u32[]{:S(2)}) collective-permute-start(bf16[48,1664]{1,0:T(8,128)(2,1)S(1)} %pad_maximum_fusion.10), channel_id=1, source_target_pairs={{0,16},{4,20},{8,24},{12,28},{16,0},{20,4},{24,8},{28,12},{1,17},{... | collective-permute-start | bytes 479240 | tf_op jit(solution)/shard_map/ppermute | solution.py:85
  35.1 16.3 %collective-permute-start.8 = (bf16[192,1664]{1,0:T(8,128)(2,1)S(1)}, bf16[192,1664]{1,0:T(8,128)(2,1)S(1)}, u32[]{:S(2)}, u32[]{:S(2)}) collective-permute-start(bf16[192,1664]{1,0:T(8,128)(2,1)S(1)} %constant_dynamic-update-slice_fusion.refs_7_), channel_id=1, source_target_pairs={{0,4},{4,0},{8,12},{12,8},{16,20},{20,16},{24,28},{28,24},{1,5},{5... | collective-permute-start | bytes 1916936 | tf_op jit(solution)/shard_map/ppermute | solution.py:85
  36.7 9.8 %collective-permute-start.11 = (bf16[48,2560]{1,0:T(8,128)(2,1)S(1)}, bf16[48,2560]{1,0:T(8,128)(2,1)S(1)}, u32[]{:S(2)}, u32[]{:S(2)}) collective-permute-start(bf16[48,2560]{1,0:T(8,128)(2,1)S(1)} %get-tuple-element.77), channel_id=1, source_target_pairs={{0,8},{4,12},{8,0},{12,4},{16,24},{20,28},{24,16},{28,20},{1,9},{5... | collective-permute-start | bytes 737288 | tf_op jit(solution)/shard_map/ppermute | solution.py:85
  40.4 10.0 %collective-permute-start.2 = (bf16[256,512]{1,0:T(8,128)(2,1)S(1)}, bf16[256,512]{1,0:T(8,128)(2,1)S(1)}, u32[]{:S(2)}, u32[]{:S(2)}) collective-permute-start(bf16[256,512]{1,0:T(8,128)(2,1)S(1)} %collective-permute-done.1.refs_2_), channel_id=1, source_target_pairs={{0,1},{1,2},{2,3},{4,5},{5,6},{6,7},{8,9},{9,10},{10,11},{12,13},{... | collective-permute-start | bytes 786440 | tf_op jit(solution)/shard_map/ppermute | solution.py:89
  50.4 13.0 %collective-permute-start.14 = (bf16[96,2560]{1,0:T(8,128)(2,1)S(1)}, bf16[96,2560]{1,0:T(8,128)(2,1)S(1)}, u32[]{:S(2)}, u32[]{:S(2)}) collective-permute-start(bf16[96,2560]{1,0:T(8,128)(2,1)S(1)} %get-tuple-element.80), channel_id=1, source_target_pairs={{0,8},{4,12},{8,0},{12,4},{16,24},{20,28},{24,16},{28,20},{1,9},{5... | collective-permute-start | bytes 1474568 | tf_op jit(solution)/shard_map/ppermute | solution.py:85
  50.9 12.7 %collective-permute-start.12 = (bf16[96,2560]{1,0:T(8,128)(2,1)S(1)}, bf16[96,2560]{1,0:T(8,128)(2,1)S(1)}, u32[]{:S(2)}, u32[]{:S(2)}) collective-permute-start(bf16[96,2560]{1,0:T(8,128)(2,1)S(1)} %get-tuple-element.78), channel_id=1, source_target_pairs={{0,16},{4,20},{8,24},{12,28},{16,0},{20,4},{24,8},{28,12},{1,17},{... | collective-permute-start | bytes 1474568 | tf_op jit(solution)/shard_map/ppermute | solution.py:85
  91.4 17.1 %collective-permute-start.19 = (bf16[2,4,16,2560]{3,2,1,0:T(8,128)(2,1)S(1)}, bf16[2,4,16,2560]{3,2,1,0:T(8,128)(2,1)S(1)}, u32[]{:S(2)}, u32[]{:S(2)}) collective-permute-start(bf16[2,4,16,2560]{3,2,1,0:T(8,128)(2,1)S(1)} %stack.60), channel_id=1, source_target_pairs={{0,16},{4,20},{8,24},{12,28},{16,0},{20,4},{24,8},{28,12},{1,17},{... | collective-permute-start | bytes 1966088 | tf_op jit(solution)/shard_map/ppermute | solution.py:85
  93.0 16.8 %collective-permute-start.18 = (bf16[2,4,16,2560]{3,2,1,0:T(8,128)(2,1)S(1)}, bf16[2,4,16,2560]{3,2,1,0:T(8,128)(2,1)S(1)}, u32[]{:S(2)}, u32[]{:S(2)}) collective-permute-start(bf16[2,4,16,2560]{3,2,1,0:T(8,128)(2,1)S(1)} %pad_maximum_fusion.2), channel_id=1, source_target_pairs={{0,8},{4,12},{8,0},{12,4},{16,24},{20,28},{24,16},{28,20},{1,9},{5... | collective-permute-start | bytes 1966088 | tf_op jit(solution)/shard_map/ppermute | solution.py:85
  106.9 10.9 %collective-permute-start.23 = (bf16[4,4,16,1536]{3,2,1,0:T(8,128)(2,1)}, bf16[4,4,16,1536]{3,2,1,0:T(8,128)(2,1)S(1)}, u32[]{:S(2)}, u32[]{:S(2)}) collective-permute-start(bf16[4,4,16,1536]{3,2,1,0:T(8,128)(2,1)} %get-tuple-element.114), channel_id=1, source_target_pairs={{0,4},{4,0},{8,12},{12,8},{16,20},{20,16},{24,28},{28,24},{1,5},{5... | collective-permute-start | bytes 2359304 | tf_op jit(solution)/shard_map/ppermute | solution.py:85
  114.4 16.2 %collective-permute-start.35 = (bf16[1,4,16,2560]{3,2,1,0:T(8,128)(2,1)S(1)}, bf16[1,4,16,2560]{3,2,1,0:T(8,128)(2,1)S(1)}, u32[]{:S(2)}, u32[]{:S(2)}) collective-permute-start(bf16[1,4,16,2560]{3,2,1,0:T(8,128)(2,1)S(1)} %bitcast.98), channel_id=1, source_target_pairs={{0,8},{4,12},{8,0},{12,4},{16,24},{20,28},{24,16},{28,20},{1,9},{5... | collective-permute-start | bytes 983048 | tf_op jit(solution)/shard_map/ppermute | solution.py:85
  115.9 14.8 %collective-permute-start.34 = (bf16[1,4,16,2560]{3,2,1,0:T(8,128)(2,1)S(1)}, bf16[1,4,16,2560]{3,2,1,0:T(8,128)(2,1)S(1)}, u32[]{:S(2)}, u32[]{:S(2)}) collective-permute-start(bf16[1,4,16,2560]{3,2,1,0:T(8,128)(2,1)S(1)} %bitcast.99), channel_id=1, source_target_pairs={{0,16},{4,20},{8,24},{12,28},{16,0},{20,4},{24,8},{28,12},{1,17},{... | collective-permute-start | bytes 983048 | tf_op jit(solution)/shard_map/ppermute | solution.py:85
  116.4 10.6 %collective-permute-start.20 = (bf16[256,512]{1,0:T(8,128)(2,1)}, bf16[256,512]{1,0:T(8,128)(2,1)S(1)}, u32[]{:S(2)}, u32[]{:S(2)}) collective-permute-start(bf16[256,512]{1,0:T(8,128)(2,1)} %get-tuple-element.111), channel_id=1, source_target_pairs={{1,0},{2,1},{3,2},{5,4},{6,5},{7,6},{9,8},{10,9},{11,10},{13,12},{... | collective-permute-start | bytes 786440 | tf_op jit(solution)/shard_map/ppermute | solution.py:89
  118.2 10.5 %collective-permute-start.26 = (bf16[2,4,16,768]{3,2,1,0:T(8,128)(2,1)S(1)}, bf16[2,4,16,768]{3,2,1,0:T(8,128)(2,1)S(1)}, u32[]{:S(2)}, u32[]{:S(2)}) collective-permute-start(bf16[2,4,16,768]{3,2,1,0:T(8,128)(2,1)S(1)} %stack.54), channel_id=1, source_target_pairs={{0,16},{4,20},{8,24},{12,28},{16,0},{20,4},{24,8},{28,12},{1,17},{... | collective-permute-start | bytes 589832 | tf_op jit(solution)/shard_map/ppermute | solution.py:85
  119.8 9.5 %collective-permute-start.24 = (bf16[2,4,16,768]{3,2,1,0:T(8,128)(2,1)S(1)}, bf16[2,4,16,768]{3,2,1,0:T(8,128)(2,1)S(1)}, u32[]{:S(2)}, u32[]{:S(2)}) collective-permute-start(bf16[2,4,16,768]{3,2,1,0:T(8,128)(2,1)S(1)} %pad_maximum_fusion.8), channel_id=1, source_target_pairs={{0,8},{4,12},{8,0},{12,4},{16,24},{20,28},{24,16},{28,20},{1,9},{5... | collective-permute-start | bytes 589832 | tf_op jit(solution)/shard_map/ppermute | solution.py:85
  127.1 13.9 %collective-permute-start.21 = (bf16[256,512]{1,0:T(8,128)(2,1)S(1)}, bf16[256,512]{1,0:T(8,128)(2,1)S(1)}, u32[]{:S(2)}, u32[]{:S(2)}) collective-permute-start(bf16[256,512]{1,0:T(8,128)(2,1)S(1)} %add_convert_fusion.3), channel_id=1, source_target_pairs={{1,0},{2,1},{3,2},{5,4},{6,5},{7,6},{9,8},{10,9},{11,10},{13,12},{... | collective-permute-start | bytes 786440 | tf_op jit(solution)/shard_map/ppermute | solution.py:89
  137.4 10.7 %collective-permute-start.36 = (bf16[2,16,5120]{2,1,0:T(8,128)(2,1)S(1)}, bf16[2,16,5120]{2,1,0:T(8,128)(2,1)S(1)}, u32[]{:S(2)}, u32[]{:S(2)}) collective-permute-start(bf16[2,16,5120]{2,1,0:T(8,128)(2,1)S(1)} %pad_maximum_fusion.7), channel_id=1, source_target_pairs={{0,1},{1,0},{2,3},{3,2},{4,5},{5,4},{6,7},{7,6},{8,9},{9,8},{10,11... | collective-permute-start | bytes 983048 | tf_op jit(solution)/shard_map/ppermute | solution.py:85
  148.1 12.1 %collective-permute-start.37 = (bf16[1,16,5120]{2,1,0:T(8,128)(2,1)S(1)}, bf16[1,16,5120]{2,1,0:T(8,128)(2,1)S(1)}, u32[]{:S(2)}, u32[]{:S(2)}) collective-permute-start(bf16[1,16,5120]{2,1,0:T(8,128)(2,1)S(1)} %add_convert_fusion.5), channel_id=1, source_target_pairs={{0,2},{1,3},{2,0},{3,1},{4,6},{5,7},{6,4},{7,5},{8,10},{9,11},{10,... | collective-permute-start | bytes 491528 | tf_op jit(solution)/shard_map/ppermute | solution.py:85
  153.8 8.8 %collective-permute-start.30 = (bf16[16,1536]{1,0:T(8,128)(2,1)S(1)}, bf16[16,1536]{1,0:T(8,128)(2,1)S(1)}, u32[]{:S(2)}, u32[]{:S(2)}) collective-permute-start(bf16[16,1536]{1,0:T(8,128)(2,1)S(1)} %fusion.18), channel_id=1, source_target_pairs={{0,8},{4,12},{8,0},{12,4},{16,24},{20,28},{24,16},{28,20},{1,9},{5... | collective-permute-start | bytes 147464 | tf_op jit(solution)/shard_map/ppermute | solution.py:85
  155.3 13.8 %collective-permute-start.31 = (bf16[16,1536]{1,0:T(8,128)(2,1)S(1)}, bf16[16,1536]{1,0:T(8,128)(2,1)S(1)}, u32[]{:S(2)}, u32[]{:S(2)}) collective-permute-start(bf16[16,1536]{1,0:T(8,128)(2,1)S(1)} %fusion.18), channel_id=1, source_target_pairs={{0,16},{4,20},{8,24},{12,28},{16,0},{20,4},{24,8},{28,12},{1,17},{... | collective-permute-start | bytes 147464 | tf_op jit(solution)/shard_map/ppermute | solution.py:85
  155.9 13.2 %collective-permute-start.32 = (bf16[16,1536]{1,0:T(8,128)(2,1)S(1)}, bf16[16,1536]{1,0:T(8,128)(2,1)S(1)}, u32[]{:S(2)}, u32[]{:S(2)}) collective-permute-start(bf16[16,1536]{1,0:T(8,128)(2,1)S(1)} %fusion.18), channel_id=1, source_target_pairs={{0,24},{4,28},{8,16},{12,20},{16,8},{20,12},{24,0},{28,4},{1,25},{... | collective-permute-start | bytes 147464 | tf_op jit(solution)/shard_map/ppermute | solution.py:85
  (42 other events, 286.2 us)

commit v4 on v3

--- a/solution.py
+++ b/solution.py
@@ -20,7 +20,7 @@
 BF16 = jnp.bfloat16
 VMEM = pl.BlockSpec(memory_space=pltpu.VMEM)
 SMEM = pl.BlockSpec(memory_space=pltpu.SMEM)
-PARAMS = pltpu.CompilerParams(vmem_limit_bytes=56 * 1024 * 1024)
+PARAMS = pltpu.CompilerParams(vmem_limit_bytes=32 * 1024 * 1024)
 
 
 class Plan:
@@ -65,6 +65,7 @@
 
 def call(body, outs, name, args, scratch=(), us=0):
     specs = [SMEM if a.dtype == jnp.int32 and a.ndim == 1 else VMEM for a in args]
+    args = [a if s is SMEM else near(a) for a, s in zip(args, specs)]
     return pl.pallas_call(
         body,
         out_shape=outs,
@@ -75,6 +76,10 @@
         cost_estimate=pl.CostEstimate(flops=us * 10**9, bytes_accessed=0, transcendentals=0),
         name=name,
     )(*args)
+
+
+def near(value):
+    return pltpu.with_memory_space_constraint(value, pltpu.VMEM)
 
 
 def sds(shape, dtype):
@@ -582,7 +587,7 @@
     if plan.down % 8 == 0:
         return call(
             functools.partial(pack_b_kernel, plan),
-            [sds((plan.rows, plan.wide_b), BF16), sds((SR, plan.wide_b), BF16)],
+            [pltpu.VMEM((plan.rows, plan.wide_b), BF16), pltpu.VMEM((SR, plan.wide_b), BF16)],
             "pack_b",
             (ids, w_gate.T, w_up.T, w_out, w_down),
         )
@@ -647,7 +652,7 @@
     gains = jnp.stack([norm1_gain, norm2_gain])
     (slab_a,) = call(
         functools.partial(pack_a_kernel, plan),
-        [sds((SR, plan.wide_a), BF16)],
+        [pltpu.VMEM((SR, plan.wide_a), BF16)],
         "pack_a",
         (ids, *own_a, norm1_gain.reshape(1, -1), norm2_gain.reshape(1, -1)),
         us=2,
@@ -676,13 +681,13 @@
     attn, q, k_all, v_all, n1, lse, wa = call(
         functools.partial(attend_kernel, plan),
         [
-            sds((n, D), F32),
-            sds((n, D), BF16),
-            sds((full, D), BF16),
-            sds((full, D), BF16),
-            sds((full, D), BF16),
-            sds((H // 2, 1, 2 * n), F32),
-            sds((D, 3 * D), BF16),
+            pltpu.VMEM((n, D), F32),
+            pltpu.VMEM((n, D), BF16),
+            pltpu.VMEM((full, D), BF16),
+            pltpu.VMEM((full, D), BF16),
+            pltpu.VMEM((full, D), BF16),
+            pltpu.VMEM((H // 2, 1, 2 * n), F32),
+            pltpu.VMEM((D, 3 * D), BF16),
         ],
         "attend",
         (ids, *parts, *own_a, mine_a, part_a, gain1, cosine, sines, reach),
@@ -696,14 +701,14 @@
         functools.partial(mlp_kernel, plan),
         [
             sds((n, D), BF16),
-            sds((n, D), F32),
-            sds((n, D), BF16),
-            sds((n, D), BF16),
-            sds((n, D), BF16),
-            sds((n, ffp), BF16),
-            sds((n, ffp), BF16),
-            sds((n, ffp), BF16),
-            sds((n, D), BF16),
+            pltpu.VMEM((n, D), F32),
+            pltpu.VMEM((n, D), BF16),
+            pltpu.VMEM((n, D), BF16),
+            pltpu.VMEM((n, D), BF16),
+            pltpu.VMEM((n, ffp), BF16),
+            pltpu.VMEM((n, ffp), BF16),
+            pltpu.VMEM((n, ffp), BF16),
+            pltpu.VMEM((n, D), BF16),
         ],
         "mlp",
         (ids, attn, x0, gain2, cot, own_b, *mine_b, *part_b),
@@ -711,7 +716,7 @@
         us=8,
     )
 
-    slabs_b = sds((plan.half, g, SR, plan.wide_b), BF16)
+    slabs_b = pltpu.VMEM((plan.half, g, SR, plan.wide_b), BF16)
     keep_b, send_b = call(
         functools.partial(mlp_grads_kernel, plan),
         [slabs_b, slabs_b],
@@ -727,7 +732,7 @@
     def attend_back(first, dattn):
         return call(
             functools.partial(attend_back_kernel, plan, first, count),
-            [sds((n, wide), BF16), sds((full, wide), BF16), sds((full, wide), BF16)],
+            [pltpu.VMEM((n, wide), BF16), pltpu.VMEM((full, wide), BF16), pltpu.VMEM((full, wide), BF16)],
             "attend_back",
             (q, k_all, v_all, attn, dattn, lse, cosine, sines, reach),
             [
@@ -746,7 +751,7 @@
     if steps:
         terms_b = plane_step(plan, terms_b)
 
-    slabs_a = sds((plan.half, g, SR, 3 * D), BF16)
+    slabs_a = pltpu.VMEM((plan.half, g, SR, 3 * D), BF16)
     keep_a, send_a = call(
         functools.partial(attend_grads_kernel, plan, halves),
         [slabs_a, slabs_a],
@@ -757,7 +762,7 @@
     )
     own, *sends = call(
         functools.partial(input_kernel, plan, halves),
-        [sds((n, D), F32)] + [sds((n, D), BF16)] * (g - 1),
+        [pltpu.VMEM((n, D), F32)] + [pltpu.VMEM((n, D), BF16)] * (g - 1),
         "dn1",
         (*back, tie(wa, keep_a, *arrays_of(terms_b))),
         us=4,

time: 180 us -> 158 us (0.88)
  Pallas kernels: 61.5 us -> 34.2 us
  waiting for transfers between devices: 46.9 us -> 52 us
  local copies, waits for them, and re-layouts: 4.48 us -> 8.73 us
  other arithmetic: 4.64 us -> 2.75 us
    pallas_call x12, Pallas kernels: 61.5 us -> 34.2 us  [call(): pl.pallas_call(body, out_shape=outs, in_specs=specs, out_specs=[VMEM] * l...]
    ppermute x36, waiting for transfers between devices: 33.8 us -> 40.1 us  [swap(): return lax.ppermute(value, axis, [(i, i ^ k) for i in range(size)])]
    unnamed x57 -> x53, local copies, waits for them, and re-layouts: 3.5 us -> 8.32 us
    ppermute x6, starting transfers between devices: 16.7 us -> 13.7 us  [shift(): lax.ppermute(value, 'grp', [(i, i + k) for i in range(size) if 0 <= i + k...]
  transfers between devices with their start and end apart: 42 -> 42, of which waited for: 20 -> 25; matrix products, arithmetic and copies ran while one was open for 2% -> 1% of each run, Pallas kernels for 23% -> 15%
where the time goes in v4:
time: 158 us
  starting transfers between devices  58.8 us (37%)
  waiting for transfers between devices  52 us (33%)
  Pallas kernels  34.2 us (22%)
  local copies, waits for them, and re-layouts  8.73 us (6%)
  other arithmetic  2.75 us (2%)
    ppermute x36, starting transfers between devices, swap(): return lax.ppermute(value, axis, [(i, i ^ k) for i in range(size)])  45.1 us
    ppermute x36, waiting for transfers between devices, swap(): return lax.ppermute(value, axis, [(i, i ^ k) for i in range(size)])  40.1 us
    pallas_call x12, Pallas kernels, call(): pl.pallas_call(body, out_shape=outs, in_specs=specs, out_specs=[VMEM] * l...  34.2 us
    ppermute x6, starting transfers between devices, shift(): lax.ppermute(value, 'grp', [(i, i + k) for i in range(size) if 0 <= i + k...  13.7 us
    ppermute x6, waiting for transfers between devices, shift(): lax.ppermute(value, 'grp', [(i, i + k) for i in range(size) if 0 <= i + k...  12 us
    unnamed x53, local copies, waits for them, and re-layouts  8.32 us
  transfers between devices with their start and end apart: 42, of which 25 were waited for; matrix products, arithmetic and copies ran while one was open for 1% of the time, Pallas kernels for 15%

profile of v4, /device:TPU:0, one launch (start us, length us, event | category | flops | bytes accessed | tf_op | source)
XLA Modules:
  0.0 157.7 jit_solution(9185017120496124592)
XLA Ops:
  5.4 4.1 %collective-permute-start.9 = (bf16[16,5120]{1,0:T(8,128)(2,1)S(1)}, bf16[16,5120]{1,0:T(8,128)(2,1)S(1)}, u32[]{:S(2)}, u32[]{:S(2)}) collective-permute-start(bf16[16,5120]{1,0:T(8,128)(2,1)S(1)} %get-tuple-element.75), channel_id=1, source_target_pairs={{0,2},{1,3},{2,0},{3,1},{4,6},{5,7},{6,4},{7,5},{8,10},{9,11},{10,... | collective-permute-start | bytes 491528 | tf_op jit(solution)/shard_map/ppermute | solution.py:90
  14.5 3.5 %collective-permute-start = (bf16[256,512]{1,0:T(8,128)(2,1)S(1)}, bf16[256,512]{1,0:T(8,128)(2,1)S(1)}, u32[]{:S(2)}, u32[]{:S(2)}) collective-permute-start(bf16[256,512]{1,0:T(8,128)(2,1)S(1)} %bitcast.106), channel_id=1, source_target_pairs={{0,1},{1,2},{2,3},{4,5},{5,6},{6,7},{8,9},{9,10},{10,11},{12,13},{... | collective-permute-start | bytes 786440 | tf_op jit(solution)/shard_map/ppermute | solution.py:94
  20.9 4.6 %collective-permute-done.4 = bf16[32,1664]{1,0:T(8,128)(2,1)S(1)} collective-permute-done((bf16[32,1664]{1,0:T(8,128)(2,1)S(1)}, bf16[32,1664]{1,0:T(8,128)(2,1)S(1)}, u32[]{:S(2)}, u32[]{:S(2)}) %collective-permute-start.4) | collective-permute-done | bytes 106528 | tf_op jit(solution)/shard_map/ppermute | solution.py:90
  25.6 2.5 %collective-permute-start.10 = (bf16[32,5120]{1,0:T(8,128)(2,1)S(1)}, bf16[32,5120]{1,0:T(8,128)(2,1)S(1)}, u32[]{:S(2)}, u32[]{:S(2)}) collective-permute-start(bf16[32,5120]{1,0:T(8,128)(2,1)S(1)} %pad_maximum_fusion.6), channel_id=1, source_target_pairs={{0,1},{1,0},{2,3},{3,2},{4,5},{5,4},{6,7},{7,6},{8,9},{9,8},{10,11... | collective-permute-start | bytes 983048 | tf_op jit(solution)/shard_map/ppermute | solution.py:90
  31.7 1.9 %collective-permute-start.1 = (bf16[256,512]{1,0:T(8,128)(2,1)S(1)}, bf16[256,512]{1,0:T(8,128)(2,1)S(1)}, u32[]{:S(2)}, u32[]{:S(2)}) collective-permute-start(bf16[256,512]{1,0:T(8,128)(2,1)S(1)} %collective-permute-done.refs_1_), channel_id=1, source_target_pairs={{0,1},{1,2},{2,3},{4,5},{5,6},{6,7},{8,9},{9,10},{10,11},{12,13},{... | collective-permute-start | bytes 786440 | tf_op jit(solution)/shard_map/ppermute | solution.py:94
  35.1 2.9 %collective-permute-done.6 = bf16[48,1664]{1,0:T(8,128)(2,1)S(1)} collective-permute-done((bf16[48,1664]{1,0:T(8,128)(2,1)S(1)}, bf16[48,1664]{1,0:T(8,128)(2,1)S(1)}, u32[]{:S(2)}, u32[]{:S(2)}) %collective-permute-start.6) | collective-permute-done | bytes 159776 | tf_op jit(solution)/shard_map/ppermute | solution.py:90
  42.7 4.4 %collective-permute-start.2 = (bf16[256,512]{1,0:T(8,128)(2,1)S(1)}, bf16[256,512]{1,0:T(8,128)(2,1)S(1)}, u32[]{:S(2)}, u32[]{:S(2)}) collective-permute-start(bf16[256,512]{1,0:T(8,128)(2,1)S(1)} %collective-permute-done.1.refs_2_), channel_id=1, source_target_pairs={{0,1},{1,2},{2,3},{4,5},{5,6},{6,7},{8,9},{9,10},{10,11},{12,13},{... | collective-permute-start | bytes 786440 | tf_op jit(solution)/shard_map/ppermute | solution.py:94
  47.3 3.6 %collective-permute-done.2.refs_3_ = bf16[256,512]{1,0:T(8,128)(2,1)S(1)} collective-permute-done((bf16[256,512]{1,0:T(8,128)(2,1)S(1)}, bf16[256,512]{1,0:T(8,128)(2,1)S(1)}, u32[]{:S(2)}, u32[]{:S(2)}) %collective-permute-start.2) | collective-permute-done | bytes 262176 | tf_op jit(solution)/shard_map/ppermute | solution.py:94
  52.0 8.1 %attend.1 = (f32[256,512]{1,0:T(8,128)S(1)}, bf16[256,512]{1,0:T(8,128)(2,1)S(1)}, bf16[1024,512]{1,0:T(8,128)(2,1)S(1)}, bf16[1024,512]{1,0:T(8,128)(2,1)S(1)},...) custom-call(s32[2]{0:T(128)S(1)} %pad_add_fusion.ids, ...), custom_call_target="tpu_custom_call" | custom-call | flops 11000000512 | tf_op jit(solution)/shard_map/attend/pallas_call | solution.py:69
  64.6 4.9 %mlp.1 = (bf16[256,512]{1,0:T(8,128)(2,1)}, f32[256,512]{1,0:T(8,128)S(1)}, bf16[256,512]{1,0:T(8,128)(2,1)S(1)}, bf16[256,512]{1,0:T(8,128)(2,1)S(1)}, bf16[256...) custom-call(s32[2]{0:T(128)S(1)} %pad_add_fusion.ids, ...), custom_call_target="tpu_custom_call" | custom-call | flops 8000000000 | tf_op jit(solution)/shard_map/mlp/pallas_call | solution.py:69
  69.6 2.5 %mlp_grads.1 = (bf16[4,4,16,5120]{3,2,1,0:T(8,128)(2,1)S(1)}, bf16[4,4,16,5120]{3,2,1,0:T(8,128)(2,1)S(1)}) custom-call(s32[2]{0:T(128)S(1)} %pad_add_fusion.ids, bf16[256,512]{1,0:T(8,128)(2,1)S(1)} %get-tuple-element.88.n2, bf16[256,1536]{1,0:T(8,128)(2,1)S(1)} %get-tuple-element.89.hid, bf16[256,1536]{1,0:T(8,128)(2,1)S(1)} %get-tuple-element.90.dg, ...), custom_call_target="tpu_custom_call" | custom-call | flops 6000000000 | tf_op jit(solution)/shard_map/mlp_grads/pallas_call | solution.py:69
  72.3 4.3 %attend_back.2 = (bf16[256,256]{1,0:T(8,128)(2,1)S(1)}, bf16[1024,256]{1,0:T(8,128)(2,1)S(1)}, bf16[1024,256]{1,0:T(8,128)(2,1)S(1)}) custom-call(bf16[256,512]{1,0:T(8,128)(2,1)S(1)} %get-tuple-element.84.q, bf16[1024,512]{1,0:T(8,128)(2,1)S(1)} %get-tuple-element.85.k_in, bf16[1024,512]{1,0:T(8,128)(2,1)S(1)} %get-tuple-element.86.v_in, ...), custom_call_target="tpu_custom_call" | custom-call | flops 8000000000 | tf_op jit(solution)/shard_map/attend_back/pallas_call | solution.py:69
  81.2 4.6 %attend_back.3 = (bf16[256,256]{1,0:T(8,128)(2,1)S(1)}, bf16[1024,256]{1,0:T(8,128)(2,1)S(1)}, bf16[1024,256]{1,0:T(8,128)(2,1)S(1)}) custom-call(bf16[256,512]{1,0:T(8,128)(2,1)S(1)} %get-tuple-element.84.q, bf16[1024,512]{1,0:T(8,128)(2,1)S(1)} %get-tuple-element.85.k_in, bf16[1024,512]{1,0:T(8,128)(2,1)S(1)} %get-tuple-element.86.v_in, ...), custom_call_target="tpu_custom_call" | custom-call | flops 8000000000 | tf_op jit(solution)/shard_map/attend_back/pallas_call | solution.py:69
  85.8 2.1 %attend_grads.1 = (bf16[4,4,16,1536]{3,2,1,0:T(8,128)(2,1)S(1)}, bf16[4,4,16,1536]{3,2,1,0:T(8,128)(2,1)S(1)}) custom-call(s32[2]{0:T(128)S(1)} %pad_add_fusion.ids, bf16[1024,512]{1,0:T(8,128)(2,1)S(1)} %get-tuple-element.106.n1, bf16[256,256]{1,0:T(8,128)(2,1)S(1)} %get-tuple-element.97.refs_0_, bf16[1024,256]{1,0:T(8,128)(2,1)S(1)} %get-tuple-element.98.refs_1_, ...), custom_call_target="tpu_custom_call" | custom-call | tf_op jit(solution)/shard_map/attend_grads/pallas_call | solution.py:69
  87.9 7.2 %collective-permute-done.19 = bf16[2,4,16,2560]{3,2,1,0:T(8,128)(2,1)S(1)} collective-permute-done((bf16[2,4,16,2560]{3,2,1,0:T(8,128)(2,1)S(1)}, bf16[2,4,16,2560]{3,2,1,0:T(8,128)(2,1)S(1)}, u32[]{:S(2)}, u32[]{:S(2)}) %collective-permute-start.19) | collective-permute-done | bytes 655392 | tf_op jit(solution)/shard_map/ppermute | solution.py:90
  103.7 5.7 %collective-permute-done.20 = bf16[256,512]{1,0:T(8,128)(2,1)S(1)} collective-permute-done((bf16[256,512]{1,0:T(8,128)(2,1)S(1)}, bf16[256,512]{1,0:T(8,128)(2,1)S(1)}, u32[]{:S(2)}, u32[]{:S(2)}) %collective-permute-start.20) | collective-permute-done | bytes 262176 | tf_op jit(solution)/shard_map/ppermute | solution.py:94
  113.7 2.9 %collective-permute-done.27 = bf16[1,4,16,768]{3,2,1,0:T(8,128)(2,1)S(1)} collective-permute-done((bf16[1,4,16,768]{3,2,1,0:T(8,128)(2,1)S(1)}, bf16[1,4,16,768]{3,2,1,0:T(8,128)(2,1)S(1)}, u32[]{:S(2)}, u32[]{:S(2)}) %collective-permute-start.27) | collective-permute-done | bytes 98336 | tf_op jit(solution)/shard_map/ppermute | solution.py:90
  117.3 3.1 %collective-permute-start.28 = (bf16[2,16,1536]{2,1,0:T(8,128)(2,1)S(1)}, bf16[2,16,1536]{2,1,0:T(8,128)(2,1)S(1)}, u32[]{:S(2)}, u32[]{:S(2)}) collective-permute-start(bf16[2,16,1536]{2,1,0:T(8,128)(2,1)S(1)} %pad_maximum_fusion.12), channel_id=1, source_target_pairs={{0,1},{1,0},{2,3},{3,2},{4,5},{5,4},{6,7},{7,6},{8,9},{9,8},{10,11... | collective-permute-start | bytes 294920 | tf_op jit(solution)/shard_map/ppermute | solution.py:90
  120.5 3.3 %collective-permute-done.28 = bf16[2,16,1536]{2,1,0:T(8,128)(2,1)S(1)} collective-permute-done((bf16[2,16,1536]{2,1,0:T(8,128)(2,1)S(1)}, bf16[2,16,1536]{2,1,0:T(8,128)(2,1)S(1)}, u32[]{:S(2)}, u32[]{:S(2)}) %collective-permute-start.28) | collective-permute-done | bytes 98336 | tf_op jit(solution)/shard_map/ppermute | solution.py:90
  123.9 4.5 %collective-permute-start.29 = (bf16[1,16,1536]{2,1,0:T(8,128)(2,1)S(1)}, bf16[1,16,1536]{2,1,0:T(8,128)(2,1)S(1)}, u32[]{:S(2)}, u32[]{:S(2)}) collective-permute-start(bf16[1,16,1536]{2,1,0:T(8,128)(2,1)S(1)} %add_convert_fusion.8), channel_id=1, source_target_pairs={{0,2},{1,3},{2,0},{3,1},{4,6},{5,7},{6,4},{7,5},{8,10},{9,11},{10,... | collective-permute-start | bytes 147464 | tf_op jit(solution)/shard_map/ppermute | solution.py:90
  131.1 4.4 %collective-permute-start.37 = (bf16[1,16,5120]{2,1,0:T(8,128)(2,1)S(1)}, bf16[1,16,5120]{2,1,0:T(8,128)(2,1)S(1)}, u32[]{:S(2)}, u32[]{:S(2)}) collective-permute-start(bf16[1,16,5120]{2,1,0:T(8,128)(2,1)S(1)} %add_convert_fusion.5), channel_id=1, source_target_pairs={{0,2},{1,3},{2,0},{3,1},{4,6},{5,7},{6,4},{7,5},{8,10},{9,11},{10,... | collective-permute-start | bytes 491528 | tf_op jit(solution)/shard_map/ppermute | solution.py:90
  140.2 2.8 %collective-permute-done.37 = bf16[1,16,5120]{2,1,0:T(8,128)(2,1)S(1)} collective-permute-done((bf16[1,16,5120]{2,1,0:T(8,128)(2,1)S(1)}, bf16[1,16,5120]{2,1,0:T(8,128)(2,1)S(1)}, u32[]{:S(2)}, u32[]{:S(2)}) %collective-permute-start.37) | collective-permute-done | bytes 163872 | tf_op jit(solution)/shard_map/ppermute | solution.py:90
  148.5 2.8 %collective-permute-done.39 = bf16[16,5120]{1,0:T(8,128)(2,1)S(1)} collective-permute-done((bf16[16,5120]{1,0:T(8,128)(2,1)S(1)}, bf16[16,5120]{1,0:T(8,128)(2,1)S(1)}, u32[]{:S(2)}, u32[]{:S(2)}) %collective-permute-start.39) | collective-permute-done | bytes 163872 | tf_op jit(solution)/shard_map/ppermute | solution.py:90
  155.5 2.2 %finish_b.1 = (f32[1376,128]{1,0:T(8,128)}, f32[1376,128]{1,0:T(8,128)}, f32[344,512]{1,0:T(8,128)}, f32[128,512]{1,0:T(8,128)}, f32[1,128]{1,0:T(1,128)}) custom-call(s32[2]{0:T(128)S(1)} %pad_add_fusion.ids, bf16[64,5120]{1,0:T(8,128)(2,1)S(1)} %constant_dynamic-update-slice_fusion.8.mine, bf16[64,5120]{1,0:T(8,128)(2,1)S(1)} %collective-permute-done.41.part, ...), custom_call_target="tpu_custom_call" | custom-call | tf_op jit(solution)/shard_map/finish_b/pallas_call | solution.py:69
  (171 shorter events, 63.2 us)
Async XLA Ops:
  5.4 20.2 %collective-permute-start.9 = (bf16[16,5120]{1,0:T(8,128)(2,1)S(1)}, bf16[16,5120]{1,0:T(8,128)(2,1)S(1)}, u32[]{:S(2)}, u32[]{:S(2)}) collective-permute-start(bf16[16,5120]{1,0:T(8,128)(2,1)S(1)} %get-tuple-element.75), channel_id=1, source_target_pairs={{0,2},{1,3},{2,0},{3,1},{4,6},{5,7},{6,4},{7,5},{8,10},{9,11},{10,... | collective-permute-start | bytes 491528 | tf_op jit(solution)/shard_map/ppermute | solution.py:90
  14.5 13.6 %collective-permute-start = (bf16[256,512]{1,0:T(8,128)(2,1)S(1)}, bf16[256,512]{1,0:T(8,128)(2,1)S(1)}, u32[]{:S(2)}, u32[]{:S(2)}) collective-permute-start(bf16[256,512]{1,0:T(8,128)(2,1)S(1)} %bitcast.106), channel_id=1, source_target_pairs={{0,1},{1,2},{2,3},{4,5},{5,6},{6,7},{8,9},{9,10},{10,11},{12,13},{... | collective-permute-start | bytes 786440 | tf_op jit(solution)/shard_map/ppermute | solution.py:94
  25.6 12.5 %collective-permute-start.10 = (bf16[32,5120]{1,0:T(8,128)(2,1)S(1)}, bf16[32,5120]{1,0:T(8,128)(2,1)S(1)}, u32[]{:S(2)}, u32[]{:S(2)}) collective-permute-start(bf16[32,5120]{1,0:T(8,128)(2,1)S(1)} %pad_maximum_fusion.6), channel_id=1, source_target_pairs={{0,1},{1,0},{2,3},{3,2},{4,5},{5,4},{6,7},{7,6},{8,9},{9,8},{10,11... | collective-permute-start | bytes 983048 | tf_op jit(solution)/shard_map/ppermute | solution.py:90
  29.7 8.3 %collective-permute-start.6 = (bf16[48,1664]{1,0:T(8,128)(2,1)S(1)}, bf16[48,1664]{1,0:T(8,128)(2,1)S(1)}, u32[]{:S(2)}, u32[]{:S(2)}) collective-permute-start(bf16[48,1664]{1,0:T(8,128)(2,1)S(1)} %pad_maximum_fusion.10), channel_id=1, source_target_pairs={{0,16},{4,20},{8,24},{12,28},{16,0},{20,4},{24,8},{28,12},{1,17},{... | collective-permute-start | bytes 479240 | tf_op jit(solution)/shard_map/ppermute | solution.py:90
  31.7 7.9 %collective-permute-start.1 = (bf16[256,512]{1,0:T(8,128)(2,1)S(1)}, bf16[256,512]{1,0:T(8,128)(2,1)S(1)}, u32[]{:S(2)}, u32[]{:S(2)}) collective-permute-start(bf16[256,512]{1,0:T(8,128)(2,1)S(1)} %collective-permute-done.refs_1_), channel_id=1, source_target_pairs={{0,1},{1,2},{2,3},{4,5},{5,6},{6,7},{8,9},{9,10},{10,11},{12,13},{... | collective-permute-start | bytes 786440 | tf_op jit(solution)/shard_map/ppermute | solution.py:94
  38.1 13.9 %collective-permute-start.8 = (bf16[192,1664]{1,0:T(8,128)(2,1)S(1)}, bf16[192,1664]{1,0:T(8,128)(2,1)S(1)}, u32[]{:S(2)}, u32[]{:S(2)}) collective-permute-start(bf16[192,1664]{1,0:T(8,128)(2,1)S(1)} %constant_dynamic-update-slice_fusion.refs_7_), channel_id=1, source_target_pairs={{0,4},{4,0},{8,12},{12,8},{16,20},{20,16},{24,28},{28,24},{1,5},{5... | collective-permute-start | bytes 1916936 | tf_op jit(solution)/shard_map/ppermute | solution.py:90
  42.7 8.3 %collective-permute-start.2 = (bf16[256,512]{1,0:T(8,128)(2,1)S(1)}, bf16[256,512]{1,0:T(8,128)(2,1)S(1)}, u32[]{:S(2)}, u32[]{:S(2)}) collective-permute-start(bf16[256,512]{1,0:T(8,128)(2,1)S(1)} %collective-permute-done.1.refs_2_), channel_id=1, source_target_pairs={{0,1},{1,2},{2,3},{4,5},{5,6},{6,7},{8,9},{9,10},{10,11},{12,13},{... | collective-permute-start | bytes 786440 | tf_op jit(solution)/shard_map/ppermute | solution.py:94
  50.9 9.5 %collective-permute-start.14 = (bf16[96,2560]{1,0:T(8,128)(2,1)S(1)}, bf16[96,2560]{1,0:T(8,128)(2,1)S(1)}, u32[]{:S(2)}, u32[]{:S(2)}) collective-permute-start(bf16[96,2560]{1,0:T(8,128)(2,1)S(1)} %get-tuple-element.80), channel_id=1, source_target_pairs={{0,8},{4,12},{8,0},{12,4},{16,24},{20,28},{24,16},{28,20},{1,9},{5... | collective-permute-start | bytes 1474568 | tf_op jit(solution)/shard_map/ppermute | solution.py:90
  51.5 9.3 %collective-permute-start.12 = (bf16[96,2560]{1,0:T(8,128)(2,1)S(1)}, bf16[96,2560]{1,0:T(8,128)(2,1)S(1)}, u32[]{:S(2)}, u32[]{:S(2)}) collective-permute-start(bf16[96,2560]{1,0:T(8,128)(2,1)S(1)} %get-tuple-element.78), channel_id=1, source_target_pairs={{0,16},{4,20},{8,24},{12,28},{16,0},{20,4},{24,8},{28,12},{1,17},{... | collective-permute-start | bytes 1474568 | tf_op jit(solution)/shard_map/ppermute | solution.py:90
  78.3 16.9 %collective-permute-start.19 = (bf16[2,4,16,2560]{3,2,1,0:T(8,128)(2,1)S(1)}, bf16[2,4,16,2560]{3,2,1,0:T(8,128)(2,1)S(1)}, u32[]{:S(2)}, u32[]{:S(2)}) collective-permute-start(bf16[2,4,16,2560]{3,2,1,0:T(8,128)(2,1)S(1)} %stack.60), channel_id=1, source_target_pairs={{0,16},{4,20},{8,24},{12,28},{16,0},{20,4},{24,8},{28,12},{1,17},{... | collective-permute-start | bytes 1966088 | tf_op jit(solution)/shard_map/ppermute | solution.py:90
  79.6 16.6 %collective-permute-start.18 = (bf16[2,4,16,2560]{3,2,1,0:T(8,128)(2,1)S(1)}, bf16[2,4,16,2560]{3,2,1,0:T(8,128)(2,1)S(1)}, u32[]{:S(2)}, u32[]{:S(2)}) collective-permute-start(bf16[2,4,16,2560]{3,2,1,0:T(8,128)(2,1)S(1)} %pad_maximum_fusion.2), channel_id=1, source_target_pairs={{0,8},{4,12},{8,0},{12,4},{16,24},{20,28},{24,16},{28,20},{1,9},{5... | collective-permute-start | bytes 1966088 | tf_op jit(solution)/shard_map/ppermute | solution.py:90
  87.8 13.3 %collective-permute-start.23 = (bf16[4,4,16,1536]{3,2,1,0:T(8,128)(2,1)S(1)}, bf16[4,4,16,1536]{3,2,1,0:T(8,128)(2,1)S(1)}, u32[]{:S(2)}, u32[]{:S(2)}) collective-permute-start(bf16[4,4,16,1536]{3,2,1,0:T(8,128)(2,1)S(1)} %get-tuple-element.114), channel_id=1, source_target_pairs={{0,4},{4,0},{8,12},{12,8},{16,20},{20,16},{24,28},{28,24},{1,5},{5... | collective-permute-start | bytes 2359304 | tf_op jit(solution)/shard_map/ppermute | solution.py:90
  97.8 15.7 %collective-permute-start.35 = (bf16[1,4,16,2560]{3,2,1,0:T(8,128)(2,1)S(1)}, bf16[1,4,16,2560]{3,2,1,0:T(8,128)(2,1)S(1)}, u32[]{:S(2)}, u32[]{:S(2)}) collective-permute-start(bf16[1,4,16,2560]{3,2,1,0:T(8,128)(2,1)S(1)} %bitcast.113), channel_id=1, source_target_pairs={{0,8},{4,12},{8,0},{12,4},{16,24},{20,28},{24,16},{28,20},{1,9},{5... | collective-permute-start | bytes 983048 | tf_op jit(solution)/shard_map/ppermute | solution.py:90
  99.3 14.2 %collective-permute-start.34 = (bf16[1,4,16,2560]{3,2,1,0:T(8,128)(2,1)S(1)}, bf16[1,4,16,2560]{3,2,1,0:T(8,128)(2,1)S(1)}, u32[]{:S(2)}, u32[]{:S(2)}) collective-permute-start(bf16[1,4,16,2560]{3,2,1,0:T(8,128)(2,1)S(1)} %bitcast.114), channel_id=1, source_target_pairs={{0,16},{4,20},{8,24},{12,28},{16,0},{20,4},{24,8},{28,12},{1,17},{... | collective-permute-start | bytes 983048 | tf_op jit(solution)/shard_map/ppermute | solution.py:90
  99.8 9.6 %collective-permute-start.20 = (bf16[256,512]{1,0:T(8,128)(2,1)S(1)}, bf16[256,512]{1,0:T(8,128)(2,1)S(1)}, u32[]{:S(2)}, u32[]{:S(2)}) collective-permute-start(bf16[256,512]{1,0:T(8,128)(2,1)S(1)} %get-tuple-element.111), channel_id=1, source_target_pairs={{1,0},{2,1},{3,2},{5,4},{6,5},{7,6},{9,8},{10,9},{11,10},{13,12},{... | collective-permute-start | bytes 786440 | tf_op jit(solution)/shard_map/ppermute | solution.py:94
  101.5 10.4 %collective-permute-start.26 = (bf16[2,4,16,768]{3,2,1,0:T(8,128)(2,1)S(1)}, bf16[2,4,16,768]{3,2,1,0:T(8,128)(2,1)S(1)}, u32[]{:S(2)}, u32[]{:S(2)}) collective-permute-start(bf16[2,4,16,768]{3,2,1,0:T(8,128)(2,1)S(1)} %stack.54), channel_id=1, source_target_pairs={{0,16},{4,20},{8,24},{12,28},{16,0},{20,4},{24,8},{28,12},{1,17},{... | collective-permute-start | bytes 589832 | tf_op jit(solution)/shard_map/ppermute | solution.py:90
  103.1 9.5 %collective-permute-start.24 = (bf16[2,4,16,768]{3,2,1,0:T(8,128)(2,1)S(1)}, bf16[2,4,16,768]{3,2,1,0:T(8,128)(2,1)S(1)}, u32[]{:S(2)}, u32[]{:S(2)}) collective-permute-start(bf16[2,4,16,768]{3,2,1,0:T(8,128)(2,1)S(1)} %pad_maximum_fusion.8), channel_id=1, source_target_pairs={{0,8},{4,12},{8,0},{12,4},{16,24},{20,28},{24,16},{28,20},{1,9},{5... | collective-permute-start | bytes 589832 | tf_op jit(solution)/shard_map/ppermute | solution.py:90
  109.5 14.4 %collective-permute-start.21 = (bf16[256,512]{1,0:T(8,128)(2,1)S(1)}, bf16[256,512]{1,0:T(8,128)(2,1)S(1)}, u32[]{:S(2)}, u32[]{:S(2)}) collective-permute-start(bf16[256,512]{1,0:T(8,128)(2,1)S(1)} %add_convert_fusion.3), channel_id=1, source_target_pairs={{1,0},{2,1},{3,2},{5,4},{6,5},{7,6},{9,8},{10,9},{11,10},{13,12},{... | collective-permute-start | bytes 786440 | tf_op jit(solution)/shard_map/ppermute | solution.py:94
  120.4 10.6 %collective-permute-start.36 = (bf16[2,16,5120]{2,1,0:T(8,128)(2,1)S(1)}, bf16[2,16,5120]{2,1,0:T(8,128)(2,1)S(1)}, u32[]{:S(2)}, u32[]{:S(2)}) collective-permute-start(bf16[2,16,5120]{2,1,0:T(8,128)(2,1)S(1)} %pad_maximum_fusion.7), channel_id=1, source_target_pairs={{0,1},{1,0},{2,3},{3,2},{4,5},{5,4},{6,7},{7,6},{8,9},{9,8},{10,11... | collective-permute-start | bytes 983048 | tf_op jit(solution)/shard_map/ppermute | solution.py:90
  128.5 8.3 %collective-permute-start.22 = (bf16[256,512]{1,0:T(8,128)(2,1)S(1)}, bf16[256,512]{1,0:T(8,128)(2,1)S(1)}, u32[]{:S(2)}, u32[]{:S(2)}) collective-permute-start(bf16[256,512]{1,0:T(8,128)(2,1)S(1)} %add_convert_fusion.2), channel_id=1, source_target_pairs={{1,0},{2,1},{3,2},{5,4},{6,5},{7,6},{9,8},{10,9},{11,10},{13,12},{... | collective-permute-start | bytes 786440 | tf_op jit(solution)/shard_map/ppermute | solution.py:94
  131.1 12.0 %collective-permute-start.37 = (bf16[1,16,5120]{2,1,0:T(8,128)(2,1)S(1)}, bf16[1,16,5120]{2,1,0:T(8,128)(2,1)S(1)}, u32[]{:S(2)}, u32[]{:S(2)}) collective-permute-start(bf16[1,16,5120]{2,1,0:T(8,128)(2,1)S(1)} %add_convert_fusion.5), channel_id=1, source_target_pairs={{0,2},{1,3},{2,0},{3,1},{4,6},{5,7},{6,4},{7,5},{8,10},{9,11},{10,... | collective-permute-start | bytes 491528 | tf_op jit(solution)/shard_map/ppermute | solution.py:90
  136.7 8.3 %collective-permute-start.30 = (bf16[16,1536]{1,0:T(8,128)(2,1)S(1)}, bf16[16,1536]{1,0:T(8,128)(2,1)S(1)}, u32[]{:S(2)}, u32[]{:S(2)}) collective-permute-start(bf16[16,1536]{1,0:T(8,128)(2,1)S(1)} %fusion.18), channel_id=1, source_target_pairs={{0,8},{4,12},{8,0},{12,4},{16,24},{20,28},{24,16},{28,20},{1,9},{5... | collective-permute-start | bytes 147464 | tf_op jit(solution)/shard_map/ppermute | solution.py:90
  137.9 13.6 %collective-permute-start.31 = (bf16[16,1536]{1,0:T(8,128)(2,1)S(1)}, bf16[16,1536]{1,0:T(8,128)(2,1)S(1)}, u32[]{:S(2)}, u32[]{:S(2)}) collective-permute-start(bf16[16,1536]{1,0:T(8,128)(2,1)S(1)} %fusion.18), channel_id=1, source_target_pairs={{0,16},{4,20},{8,24},{12,28},{16,0},{20,4},{24,8},{28,12},{1,17},{... | collective-permute-start | bytes 147464 | tf_op jit(solution)/shard_map/ppermute | solution.py:90
  138.7 12.8 %collective-permute-start.32 = (bf16[16,1536]{1,0:T(8,128)(2,1)S(1)}, bf16[16,1536]{1,0:T(8,128)(2,1)S(1)}, u32[]{:S(2)}, u32[]{:S(2)}) collective-permute-start(bf16[16,1536]{1,0:T(8,128)(2,1)S(1)} %fusion.18), channel_id=1, source_target_pairs={{0,24},{4,28},{8,16},{12,20},{16,8},{20,12},{24,0},{28,4},{1,25},{... | collective-permute-start | bytes 147464 | tf_op jit(solution)/shard_map/ppermute | solution.py:90
  (40 other events, 162.1 us)

commit v5 on v4

--- a/solution.py
+++ b/solution.py
@@ -63,9 +63,13 @@
     return dot(left, right, ((0,), (0,)))
 
 
-def call(body, outs, name, args, scratch=(), us=0):
+def call(body, outs, name, args, scratch=(), us=0, far=()):
     specs = [SMEM if a.dtype == jnp.int32 and a.ndim == 1 else VMEM for a in args]
-    args = [a if s is SMEM else near(a) for a, s in zip(args, specs)]
+    spaces = [pltpu.HBM if any(a is b for b in far) else pltpu.VMEM for a in args]
+    args = [
+        pltpu.with_memory_space_constraint(a, space) if spec is VMEM else a
+        for a, space, spec in zip(args, spaces, specs)
+    ]
     return pl.pallas_call(
         body,
         out_shape=outs,
@@ -78,10 +82,6 @@
     )(*args)
 
 
-def near(value):
-    return pltpu.with_memory_space_constraint(value, pltpu.VMEM)
-
-
 def sds(shape, dtype):
     return jax.ShapeDtypeStruct(shape, dtype)
 
@@ -148,15 +148,15 @@
     return jnp.concatenate([value[:HD, :count], value[HD:, count:]], axis=0).T
 
 
-def mask_bias(plan, reach, bias_ref):
+def mask_bias(plan, reach, bias_ref, parts):
     n = plan.local
     key = lax.broadcasted_iota(jnp.int32, (n, n), 0)
     query = lax.broadcasted_iota(jnp.int32, (n, n), 1)
-    for k in range(plan.grp):
+    for i, k in enumerate(parts):
         offset = query - key + k * n
         seen = (offset >= 0) & (offset <= reach)
         bias = jnp.where(seen, 0.0, NEGATIVE).astype(F32)
-        bias_ref[k * n : (k + 1) * n, :] = jnp.concatenate([bias, bias], axis=1)
+        bias_ref[i * n : (i + 1) * n, :] = jnp.concatenate([bias, bias], axis=1)
 
 
 def each_slice(plan, place, slice_id, mine, part, store):
@@ -267,7 +267,7 @@
         wa_ref[pl.ds(aligned(z * plan.rows + s * SR), SR), :] = rows[:, : 3 * D]
 
     each_slice(plan, place, slice_id, [mine], [part], store)
-    mask_bias(plan, reach[...], bias_ref)
+    mask_bias(plan, reach[...], bias_ref, range(g))
     gains = gain[...]
     for k in range(g):
         x = parts[k][...].astype(F32)
@@ -376,73 +376,63 @@
     spread(plan, ids[0], ids[1], keep, send, copy)
 
 
-def attend_back_kernel(plan, first, count, q, k_in, v_in, attn, dattn, lse, cosine, sines, reach, dq_ref, dk_ref, dv_ref, bias_ref, dq_scr, dk_scr):
-    mask_bias(plan, reach[...], bias_ref)
+def attend_back_kernel(plan, low, high, *refs):
+    q, k_in, v_in, attn, dattn, lse, cosine, sines, reach, wa = refs[:10]
+    first, last = high == plan.grp, low == 0
+    refs = refs[10:]
+    if not first:
+        dq_in, refs = refs[0], refs[1:]
+    dk_ref, dv_ref, dq_ref = refs[:3]
+    dn1_refs = refs[3 : 3 + high - low]
+    bias_ref, dk_scr, dq_scr = refs[3 + high - low :]
+    n = plan.local
+    keys_of = slice(low * n, high * n)
+    mask_bias(plan, reach[...], bias_ref, range(low, high))
 
     def pair(i, carry):
-        lanes = pl.ds(pl.multiple_of((first + i) * PAIR, PAIR), PAIR)
-        outs = pl.ds(pl.multiple_of(i * PAIR, PAIR), PAIR)
+        lanes = pl.ds(pl.multiple_of(i * PAIR, PAIR), PAIR)
         q2 = two_heads(q[:, lanes])
         da = dattn[:, lanes]
         da2 = two_heads(da)
-        prod = two_heads(da.astype(F32) * attn[:, lanes])
-        ones = jnp.ones((8, PAIR), F32)
-        mean = lax.dot_general(
-            ones, prod, (((1,), (1,)), ((), ())), precision=lax.Precision.HIGHEST,
-            preferred_element_type=F32,
-        )[0:1, :]
-        keys = k_in[:, lanes]
-        values = v_in[:, lanes]
-        prob = jnp.exp(against(keys, q2) + (bias_ref[...] - lse[first + i]))
+        mean = row_sums(two_heads(da.astype(F32) * attn[:, lanes]))
+        keys = k_in[keys_of, lanes]
+        values = v_in[keys_of, lanes]
+        prob = jnp.exp(against(keys, q2) + (bias_ref[...] - lse[i]))
         dprob = against(values, da2)
         dscore = (prob * (dprob - mean)).astype(BF16)
-        dv_ref[:, outs] = mm(prob.astype(BF16), da2).astype(BF16)
-        dk_scr[:, outs] = mm(dscore, q2)
-        dq_scr[:, outs] = one_pair(rows_of(keys, dscore)) * (HD**-0.5)
+        dv_ref[:, lanes] = mm(prob.astype(BF16), da2).astype(BF16)
+        dk_scr[:, lanes] = mm(dscore, q2)
+        dq = one_pair(rows_of(keys, dscore)) * (HD**-0.5)
+        dq_scr[:, lanes] = dq if first else dq + dq_in[:, lanes]
         return carry
 
-    lax.fori_loop(0, count, pair, 0)
+    lax.fori_loop(0, H // 2, pair, 0)
+    dq = dq_scr[...]
+    if last:
+        dq = rotate_back(dq, cosine[:n, :], sines[:n, :]).astype(BF16)
+    dq_ref[...] = dq
+    for i, k in enumerate(range(low, high)):
+        rows, at = slice(i * n, (i + 1) * n), slice(k * n, (k + 1) * n)
+        dk = rotate_back(dk_scr[rows, :], cosine[at, :], sines[at, :]).astype(BF16)
+        dk_ref[rows, :] = dk
+        dn1 = against(dk, wa[:, D : 2 * D]) + against(dv_ref[rows, :], wa[:, 2 * D :])
+        if k == 0:
+            dn1 = dn1 + against(dq, wa[:, :D])
+        dn1_refs[i][...] = dn1.astype(dn1_refs[i].dtype)
+
+
+def attend_grads_kernel(plan, pieces, ids, n1, dq, *refs):
+    keys, values = refs[: len(pieces)], refs[len(pieces) : 2 * len(pieces)]
+    keep, send, ga_ref = refs[2 * len(pieces) :]
     n = plan.local
-    dq_ref[...] = rotate_back(dq_scr[...], cosine[:n, :], sines[:n, :]).astype(BF16)
-    for k in range(plan.grp):
-        rows = slice(k * n, (k + 1) * n)
-        dk_ref[rows, :] = rotate_back(dk_scr[rows, :], cosine[rows, :], sines[rows, :]).astype(BF16)
-
-
-def input_kernel(plan, halves, *refs):
-    back = refs[: 3 * halves]
-    wa, own_ref = refs[3 * halves : 3 * halves + 2]
-    sends = refs[3 * halves + 2 :]
-    n = plan.local
-    wide = D // halves
-    for k in reversed(range(plan.grp)):
-        rows = slice(k * n, (k + 1) * n)
-        dn1 = None
-        for h in range(halves):
-            dq, dk, dv = back[3 * h : 3 * h + 3]
-            at = h * wide
-            term = against(dk[rows, :], wa[:, D + at : D + at + wide])
-            term = term + against(dv[rows, :], wa[:, 2 * D + at : 2 * D + at + wide])
-            if k == 0:
-                term = term + against(dq[...], wa[:, at : at + wide])
-            dn1 = term if dn1 is None else dn1 + term
-        if k == 0:
-            own_ref[...] = dn1
-        else:
-            sends[k - 1][...] = dn1.astype(BF16)
-
-
-def attend_grads_kernel(plan, halves, ids, n1, *refs):
-    back = refs[: 3 * halves]
-    keep, send, ga_ref = refs[3 * halves :]
     n1_t = n1[...].T
-    wide = D // halves
-    for h in range(halves):
-        dq, dk, dv = back[3 * h : 3 * h + 3]
-        at = h * wide
-        ga_ref[:, at : at + wide] = mm(n1_t[:, : plan.local], dq[...]).astype(BF16)
-        ga_ref[:, D + at : D + at + wide] = mm(n1_t, dk[...]).astype(BF16)
-        ga_ref[:, 2 * D + at : 2 * D + at + wide] = mm(n1_t, dv[...]).astype(BF16)
+    ga_ref[:, :D] = mm(n1_t[:, :n], dq[...]).astype(BF16)
+    for i, grads in enumerate((keys, values)):
+        total = None
+        for (low, high), grad in zip(pieces, grads):
+            term = mm(n1_t[:, low * n : high * n], grad[...])
+            total = term if total is None else total + term
+        ga_ref[:, (i + 1) * D : (i + 2) * D] = total.astype(BF16)
 
     def copy(z, s, target, o, k):
         target[o, k] = ga_ref[pl.ds(aligned(z * plan.rows + s * SR), SR), :]
@@ -471,32 +461,31 @@
     out_ref[...] = dx1[...] + scale * (e1 - unit * jnp.mean(e1 * unit, axis=1, keepdims=True))
 
 
-def fetch_line(plan, slab):
-    blocks = [slab]
-    for bit in reversed(plan.line):
-        got = swap("grp", bit, plan.grp, jnp.concatenate(blocks, axis=0))
-        blocks += jnp.split(got, len(blocks), axis=0)
-    return jnp.concatenate(blocks[1:], axis=0)
-
-
-def fetch_plane(plan, block):
-    return jnp.concatenate(
-        [block] + [swap("rep", 2 * o, plan.rep, block) for o in range(1, plan.half)], axis=0
-    )
-
-
-def fetch_plane_halves(plan, block, after):
-    terms = []
-    for half, bits in zip(column_halves(block), (plan.plane, plan.plane[::-1])):
-        terms.append(({0: half}, bits))
-    for step in range(len(plan.plane)):
-        done = []
-        for blocks, bits in terms:
-            moved = tie(jnp.concatenate(list(blocks.values()), axis=0), *after[step : step + 1])
-            got = jnp.split(swap("rep", 2 * bits[step], plan.rep, moved), len(blocks), axis=0)
-            done.append((blocks | {o ^ bits[step]: g for o, g in zip(list(blocks), got)}, bits))
-        terms = done
-    return [jnp.concatenate([mine[o] for o in range(plan.half)], axis=0) for mine, _ in terms]
+def join(*values):
+    return lax.optimization_barrier(values)
+
+
+def line_step(plan, bit, blocks):
+    return swap("grp", bit, plan.grp, jnp.concatenate(blocks, axis=0))
+
+
+def fetch_plane(plan, block, *beside):
+    got = [swap("rep", 2 * o, plan.rep, block) for o in range(1, plan.half)]
+    joined = join(*got, *beside)
+    return [jnp.concatenate([block, *joined[: len(got)]], axis=0), *joined[len(got) :]]
+
+
+def halves_move(plan, terms, step):
+    moved = [jnp.concatenate(list(blocks.values()), axis=0) for blocks, _ in terms]
+    return [swap("rep", 2 * bits[step], plan.rep, m) for m, (_, bits) in zip(moved, terms)]
+
+
+def halves_take(plan, terms, step, got):
+    done = []
+    for whole, (blocks, bits) in zip(got, terms):
+        new = jnp.split(whole, len(blocks), axis=0)
+        done.append((blocks | {o ^ bits[step]: g for o, g in zip(list(blocks), new)}, bits))
+    return done
 
 
 def column_halves(value):
@@ -533,15 +522,15 @@
 
 
 def plane_step(plan, terms, before=(), after=()):
+    arrived = []
+    for mine, bits in terms:
+        moved = tie(jnp.stack([mine[o] for o in mine if o & bits[0]]), *before)
+        arrived.append(swap("rep", 2 * bits[0], plan.rep, moved))
+    *arrived, _ = lax.optimization_barrier((*arrived, tuple(after)))
     done = []
-    for mine, bits in terms:
+    for got, (mine, bits) in zip(arrived, terms):
         leave = [o for o in mine if o & bits[0]]
-        moved = tie(jnp.stack([mine[o] for o in leave]), *before)
-        got = swap("rep", 2 * bits[0], plan.rep, moved)
-        kept = {}
-        for i, o in enumerate(leave):
-            kept[o ^ bits[0]] = add(tie(mine[o ^ bits[0]], *after), got[i])
-        done.append((kept, bits[1:]))
+        done.append(({o ^ bits[0]: add(mine[o ^ bits[0]], got[i]) for i, o in enumerate(leave)}, bits[1:]))
     return done
 
 
@@ -565,7 +554,7 @@
 
 
 def share(plan, final):
-    mine = fetch_plane(plan, final)
+    (mine,) = fetch_plane(plan, final)
     return mine, fetch_core(plan, mine)
 
 
@@ -590,6 +579,8 @@
             [pltpu.VMEM((plan.rows, plan.wide_b), BF16), pltpu.VMEM((SR, plan.wide_b), BF16)],
             "pack_b",
             (ids, w_gate.T, w_up.T, w_out, w_down),
+            us=3,
+            far=(w_out, w_down),
         )
     rows = jnp.pad(w_down, ((0, plan.down_pad - plan.down), (0, 0)))
     rows = rows.reshape(plan.slices, plan.pieces, SR, D).transpose(0, 2, 1, 3)
@@ -615,6 +606,7 @@
             "finish_b",
             (ids, *final, w_gate.T, w_up.T, line),
             [pltpu.VMEM((plan.rows, plan.wide_b), BF16)],
+            far=(line,),
         )
         return gate.T, up.T, down, out, norm.reshape(-1)
     (grads,) = call(
@@ -650,29 +642,54 @@
 
     own_a = (w_query, w_key, w_value)
     gains = jnp.stack([norm1_gain, norm2_gain])
+    lines = (norm1_gain.reshape(1, -1), norm2_gain.reshape(1, -1))
     (slab_a,) = call(
         functools.partial(pack_a_kernel, plan),
         [pltpu.VMEM((SR, plan.wide_a), BF16)],
         "pack_a",
-        (ids, *own_a, norm1_gain.reshape(1, -1), norm2_gain.reshape(1, -1)),
+        (ids, *own_a, *lines),
         us=2,
-    )
-    own_b, slab_b = pack_b(plan, ids, w_gate, w_up, w_out, w_down)
-
-    parts = [x0]
-    for _ in range(1, g):
+        far=(*own_a, *lines),
+    )
+    own_b, slab_b = pack_b(plan, ids, w_gate, w_up, w_out, tie(w_down, slab_a))
+    parts, blocks_a, blocks_b = [x0], [slab_a], [slab_b]
+    for i, bit in enumerate(reversed(plan.line)):
+        got = line_step(plan, bit, blocks_a)
+        if i == 0:
+            got, first = join(got, shift(1, g, x0))
+            parts.append(first)
+        else:
+            got, blocks_b[-1] = join(got, blocks_b[-1])
+        blocks_a += jnp.split(got, len(blocks_a), axis=0)
+        count = len(blocks_b)
+        blocks_b = [*blocks_b, line_step(plan, bit, blocks_b)]
+        if i:
+            blocks_b = [*blocks_b[:count], *jnp.split(blocks_b[count], count, axis=0)]
+    block_a = jnp.concatenate(blocks_a[1:], axis=0)
+    block_b = jnp.concatenate(blocks_b[1:], axis=0)
+    for _ in range(2, g - 2):
         parts.append(shift(1, g, parts[-1]))
-    block_a = fetch_line(plan, slab_a)
-    block_b = fetch_line(plan, slab_b)
-    mine_a = fetch_plane(plan, tie(block_a, parts[1]))
-    mine_b = fetch_plane_halves(plan, tie(block_b, mine_a), (parts[-2], parts[-1]))
-    part_a = fetch_core(plan, mine_a)
-
-    lines = [mine_a[i * SR : i * SR + 2, 3 * D : 3 * D + plan.rows] for i in range(g - 1)]
+    mine_a, moving = fetch_plane(plan, block_a, shift(1, g, parts[-1]))
+    if g > 3:
+        parts.append(moving)
+        moving = shift(1, g, moving)
+    terms = [
+        ({0: half}, bits)
+        for half, bits in zip(column_halves(block_b), (plan.plane, plan.plane[::-1]))
+    ]
+    arriving = halves_move(plan, terms, 0) if plan.plane else []
+    *arriving, moving = join(*arriving, moving)
+    for step in range(1, len(plan.plane)):
+        terms = halves_take(plan, terms, step - 1, arriving)
+        arriving = halves_move(plan, terms, step)
+    parts.append(moving)
+    part_a = fetch_core(plan, tie(mine_a, moving))
+
+    tiles = [mine_a[i * SR : i * SR + 2, 3 * D : 3 * D + plan.rows] for i in range(g - 1)]
     order = jnp.bitwise_xor(jnp.arange(g, dtype=jnp.int32), place)
     chosen = sum(
         jnp.where((order == k)[:, None, None], tile[None], 0).astype(F32)
-        for k, tile in zip([0, *plan.order], [gains, *lines])
+        for k, tile in zip([0, *plan.order], [gains, *tiles])
     )
     gain1 = chosen[:, 0].reshape(1, D)
     gain2 = chosen[:, 1].reshape(1, D)
@@ -693,8 +710,13 @@
         (ids, *parts, *own_a, mine_a, part_a, gain1, cosine, sines, reach),
         [pltpu.VMEM((full, 2 * n), F32)],
         us=11,
-    )
-    part_b = [fetch_core(plan, tie(half, attn)) for half in mine_b]
+        far=own_a,
+    )
+    *arriving, attn = join(*arriving, attn)
+    if plan.plane:
+        terms = halves_take(plan, terms, len(plan.plane) - 1, arriving)
+    mine_b = [jnp.concatenate([mine[o] for o in range(plan.half)], axis=0) for mine, _ in terms]
+    part_b = [fetch_core(plan, half) for half in mine_b]
 
     ffp = plan.ffp
     output, dx1, dout, dattn, n2, hid, dg, dup, attn_low = call(
@@ -725,65 +747,64 @@
         [pltpu.VMEM((D, plan.tall_b), BF16), pltpu.VMEM((ffp, D), BF16)],
         us=6,
     )
-    halves = 2
-    count = H // 2 // halves
-    wide = D // halves
-
-    def attend_back(first, dattn):
-        return call(
-            functools.partial(attend_back_kernel, plan, first, count),
-            [pltpu.VMEM((n, wide), BF16), pltpu.VMEM((full, wide), BF16), pltpu.VMEM((full, wide), BF16)],
-            "attend_back",
-            (q, k_all, v_all, attn, dattn, lse, cosine, sines, reach),
-            [
-                pltpu.VMEM((full, 2 * n), F32),
-                pltpu.VMEM((n, wide), F32),
-                pltpu.VMEM((full, wide), F32),
-            ],
-            us=8,
-        )
-
-    back = list(attend_back(0, tie(dattn, keep_b)))
     core_b = combine_cores(plan, keep_b, send_b)
-    back += attend_back(count, tie(dattn, core_b, back[0]))
     terms_b = plane_terms(plan, core_b)
     steps = len(plan.plane)
     if steps:
         terms_b = plane_step(plan, terms_b)
 
-    slabs_a = pltpu.VMEM((plan.half, g, SR, 3 * D), BF16)
-    keep_a, send_a = call(
-        functools.partial(attend_grads_kernel, plan, halves),
-        [slabs_a, slabs_a],
-        "attend_grads",
-        (ids, n1, *back),
-        [pltpu.VMEM((D, 3 * D), BF16)],
-        us=0,
-    )
-    own, *sends = call(
-        functools.partial(input_kernel, plan, halves),
-        [pltpu.VMEM((n, D), F32)] + [pltpu.VMEM((n, D), BF16)] * (g - 1),
-        "dn1",
-        (*back, tie(wa, keep_a, *arrays_of(terms_b))),
-        us=4,
-    )
-    moving = sends[g - 2]
-    hops = []
+    pieces = [(k, k + 1) for k in reversed(range(2, g))] + [(0, min(2, g))]
+    dq, carry, dks, dvs, sends, hops = None, [], [], [], {}, []
+    for low, high in pieces:
+        count = high - low
+        dk, dv, dq, *dn1 = call(
+            functools.partial(attend_back_kernel, plan, low, high),
+            [
+                pltpu.VMEM((count * n, D), BF16),
+                pltpu.VMEM((count * n, D), BF16),
+                pltpu.VMEM((n, D), BF16 if low == 0 else F32),
+                *[pltpu.VMEM((n, D), F32 if k == 0 else BF16) for k in range(low, high)],
+            ],
+            "attend_back",
+            (q, k_all, v_all, attn, tie(dattn, core_b if carry else keep_b), lse, cosine, sines, reach, wa, *carry),
+            [
+                pltpu.VMEM((count * n, 2 * n), F32),
+                pltpu.VMEM((count * n, D), F32),
+                pltpu.VMEM((n, D), F32),
+            ],
+            us=8,
+        )
+        carry = [dq]
+        dks.append(dk)
+        dvs.append(dv)
+        sends |= dict(zip(range(low, high), dn1))
+    own = sends[0]
+    moving = sends[g - 1]
     for k in reversed(range(1, g)):
         moving = shift(-1, g, moving)
         hops.append(moving)
         if k > 1:
-            moving = add(moving, sends[k - 2])
+            moving = add(tie(moving, *arrays_of(terms_b)), sends[k - 1])
+
+    slabs_a = pltpu.VMEM((plan.half, g, SR, 3 * D), BF16)
+    keep_a, send_a = call(
+        functools.partial(attend_grads_kernel, plan, pieces),
+        [slabs_a, slabs_a],
+        "attend_grads",
+        (ids, tie(n1, *arrays_of(terms_b)), dq, *dks, *dvs),
+        [pltpu.VMEM((D, 3 * D), BF16)],
+        us=4,
+    )
     core_a = combine_cores(plan, keep_a, send_a)
-    terms_a = plane_terms(plan, tie(core_a, own))
+    terms_a = plane_terms(plan, core_a)
     for step in range(steps):
         if step:
-            terms_b = plane_step(plan, terms_b, after=(own,))
+            terms_b = plane_step(plan, terms_b, after=(keep_a,))
         terms_a = plane_step(plan, terms_a)
     total_a = jnp.concatenate([mine[0] for mine, _ in terms_a], axis=-1)
     total_b = jnp.concatenate([mine[0] for mine, _ in terms_b], axis=-1)
-    final_b = share(plan, tie(combine_line(plan, total_b, (own, hops[0])), hops[1]))
-    final_a = share(plan, tie(combine_line(plan, total_a, (hops[0], hops[1])), hops[-1]))
+    final_b = share(plan, combine_line(plan, total_b, (own, hops[-1])))
+    final_a = share(plan, combine_line(plan, total_a, (own, hops[-1])))
     (input_grad,) = call(
         functools.partial(residual_kernel, plan),
         [sds((n, D), F32)],
@@ -800,6 +821,7 @@
         (ids, *final_a, *own_a, norm1_gain.reshape(1, -1)),
         [pltpu.VMEM((plan.rows, 3 * D), BF16)],
         us=2,
+        far=own_a,
     )
     return (
         output.reshape(tokens.shape),

time: 158 us -> 151 us (0.956)
  local copies, waits for them, and re-layouts: 8.73 us -> 0.38 us
  Pallas kernels: 34.2 us -> 39.1 us
  starting transfers between devices: 58.8 us -> 54 us
    unnamed x53 -> x25, local copies, waits for them, and re-layouts: 8.32 us -> 0.14 us
    pallas_call x12, Pallas kernels: 34.2 us -> 39.1 us  [call(): pl.pallas_call(body, out_shape=outs, in_specs=specs, out_specs=[VMEM] * l...]
    ppermute x36, starting transfers between devices: 45.1 us -> 41.9 us  [swap(): return lax.ppermute(value, axis, [(i, i ^ k) for i in range(size)])]
    ppermute x6, waiting for transfers between devices: 12 us -> 14.8 us  [shift(): lax.ppermute(value, 'grp', [(i, i + k) for i in range(size) if 0 <= i + k...]
  transfers between devices with their start and end apart: 42 -> 42, of which waited for: 25 -> 23; matrix products, arithmetic and copies ran while one was open for 1% -> 2% of each run, Pallas kernels for 15% -> 19%
where the time goes in v5:
time: 151 us
  starting transfers between devices  54 us (36%)
  waiting for transfers between devices  53.5 us (35%)
  Pallas kernels  39.1 us (26%)
  other arithmetic  2.75 us (2%)
    ppermute x36, starting transfers between devices, swap(): return lax.ppermute(value, axis, [(i, i ^ k) for i in range(size)])  41.9 us
    pallas_call x12, Pallas kernels, call(): pl.pallas_call(body, out_shape=outs, in_specs=specs, out_specs=[VMEM] * l...  39.1 us
    ppermute x36, waiting for transfers between devices, swap(): return lax.ppermute(value, axis, [(i, i ^ k) for i in range(size)])  38.7 us
    ppermute x6, waiting for transfers between devices, shift(): lax.ppermute(value, 'grp', [(i, i + k) for i in range(size) if 0 <= i + k...  14.8 us
    ppermute x6, starting transfers between devices, shift(): lax.ppermute(value, 'grp', [(i, i + k) for i in range(size) if 0 <= i + k...  12.1 us
  transfers between devices with their start and end apart: 42, of which 23 were waited for; matrix products, arithmetic and copies ran while one was open for 2% of the time, Pallas kernels for 19%

profile of v5, /device:TPU:0, one launch (start us, length us, event | category | flops | bytes accessed | tf_op | source)
XLA Modules:
  0.0 150.9 jit_solution(12604304053521426128)
XLA Ops:
  1.9 4.1 %collective-permute-start = (bf16[16,1664]{1,0:T(8,128)(2,1)S(1)}, bf16[16,1664]{1,0:T(8,128)(2,1)S(1)}, u32[]{:S(2)}, u32[]{:S(2)}) collective-permute-start(bf16[16,1664]{1,0:T(8,128)(2,1)S(1)} %pack_a.1), channel_id=1, source_target_pairs={{0,2},{1,3},{2,0},{3,1},{4,6},{5,7},{6,4},{7,5},{8,10},{9,11},{10,... | collective-permute-start | bytes 159752 | tf_op jit(solution)/shard_map/ppermute | solution.py:90
  6.0 3.5 %collective-permute-start.1 = (bf16[256,512]{1,0:T(8,128)(2,1)S(1)}, bf16[256,512]{1,0:T(8,128)(2,1)S(1)}, u32[]{:S(2)}, u32[]{:S(2)}) collective-permute-start(bf16[256,512]{1,0:T(8,128)(2,1)S(1)} %bitcast.45), channel_id=1, source_target_pairs={{0,1},{1,2},{2,3},{4,5},{5,6},{6,7},{8,9},{9,10},{10,11},{12,13},{... | collective-permute-start | bytes 786440 | tf_op jit(solution)/shard_map/ppermute | solution.py:94
  11.4 4.7 %collective-permute-done.1.refs_1_ = bf16[256,512]{1,0:T(8,128)(2,1)S(1)} collective-permute-done((bf16[256,512]{1,0:T(8,128)(2,1)S(1)}, bf16[256,512]{1,0:T(8,128)(2,1)S(1)}, u32[]{:S(2)}, u32[]{:S(2)}) %collective-permute-start.1) | collective-permute-done | bytes 262176 | tf_op jit(solution)/shard_map/ppermute | solution.py:94
  16.2 2.5 %collective-permute-start.2 = (bf16[32,1664]{1,0:T(8,128)(2,1)S(1)}, bf16[32,1664]{1,0:T(8,128)(2,1)S(1)}, u32[]{:S(2)}, u32[]{:S(2)}) collective-permute-start(bf16[32,1664]{1,0:T(8,128)(2,1)S(1)} %pad_maximum_fusion.11), channel_id=1, source_target_pairs={{0,1},{1,0},{2,3},{3,2},{4,5},{5,4},{6,7},{7,6},{8,9},{9,8},{10,11... | collective-permute-start | bytes 319496 | tf_op jit(solution)/shard_map/ppermute | solution.py:90
  29.5 3.6 %collective-permute-done.8 = bf16[48,1664]{1,0:T(8,128)(2,1)S(1)} collective-permute-done((bf16[48,1664]{1,0:T(8,128)(2,1)S(1)}, bf16[48,1664]{1,0:T(8,128)(2,1)S(1)}, u32[]{:S(2)}, u32[]{:S(2)}) %collective-permute-start.8) | collective-permute-done | bytes 159776 | tf_op jit(solution)/shard_map/ppermute | solution.py:90
  33.1 2.7 %collective-permute-start.11 = (bf16[256,512]{1,0:T(8,128)(2,1)S(1)}, bf16[256,512]{1,0:T(8,128)(2,1)S(1)}, u32[]{:S(2)}, u32[]{:S(2)}) collective-permute-start(bf16[256,512]{1,0:T(8,128)(2,1)S(1)} %collective-permute-done.10.refs_2_), channel_id=1, source_target_pairs={{0,1},{1,2},{2,3},{4,5},{5,6},{6,7},{8,9},{9,10},{10,11},{12,13},{... | collective-permute-start | bytes 786440 | tf_op jit(solution)/shard_map/ppermute | solution.py:94
  39.6 2.5 %collective-permute-done.5 = bf16[48,2560]{1,0:T(8,128)(2,1)S(1)} collective-permute-done((bf16[48,2560]{1,0:T(8,128)(2,1)S(1)}, bf16[48,2560]{1,0:T(8,128)(2,1)S(1)}, u32[]{:S(2)}, u32[]{:S(2)}) %collective-permute-start.5) | collective-permute-done | bytes 245792 | tf_op jit(solution)/shard_map/ppermute | solution.py:90
  45.2 8.6 %attend.1 = (f32[256,512]{1,0:T(8,128)S(1)}, bf16[256,512]{1,0:T(8,128)(2,1)S(1)}, bf16[1024,512]{1,0:T(8,128)(2,1)S(1)}, bf16[1024,512]{1,0:T(8,128)(2,1)S(1)},...) custom-call(s32[2]{0:T(128)S(1)} %pad_add_fusion.ids, ...), custom_call_target="tpu_custom_call" | custom-call | flops 11000000512 | tf_op jit(solution)/shard_map/attend/pallas_call | solution.py:73
  53.9 2.6 %collective-permute-done.13 = bf16[96,2560]{1,0:T(8,128)(2,1)S(1)} collective-permute-done((bf16[96,2560]{1,0:T(8,128)(2,1)S(1)}, bf16[96,2560]{1,0:T(8,128)(2,1)S(1)}, u32[]{:S(2)}, u32[]{:S(2)}) %collective-permute-start.13) | collective-permute-done | bytes 491552 | tf_op jit(solution)/shard_map/ppermute | solution.py:90
  61.9 4.9 %mlp.1 = (bf16[256,512]{1,0:T(8,128)(2,1)}, f32[256,512]{1,0:T(8,128)S(1)}, bf16[256,512]{1,0:T(8,128)(2,1)S(1)}, bf16[256,512]{1,0:T(8,128)(2,1)S(1)}, bf16[256...) custom-call(s32[2]{0:T(128)S(1)} %pad_add_fusion.ids, ...), custom_call_target="tpu_custom_call" | custom-call | flops 8000000000 | tf_op jit(solution)/shard_map/mlp/pallas_call | solution.py:73
  66.9 2.5 %mlp_grads.1 = (bf16[4,4,16,5120]{3,2,1,0:T(8,128)(2,1)S(1)}, bf16[4,4,16,5120]{3,2,1,0:T(8,128)(2,1)S(1)}) custom-call(s32[2]{0:T(128)S(1)} %pad_add_fusion.ids, bf16[256,512]{1,0:T(8,128)(2,1)S(1)} %get-tuple-element.118.n2, bf16[256,1536]{1,0:T(8,128)(2,1)S(1)} %get-tuple-element.119.hid, bf16[256,1536]{1,0:T(8,128)(2,1)S(1)} %get-tuple-element.120.dg, ...), custom_call_target="tpu_custom_call" | custom-call | flops 6000000000 | tf_op jit(solution)/shard_map/mlp_grads/pallas_call | solution.py:73
  69.6 3.6 %attend_back.3 = (bf16[256,512]{1,0:T(8,128)(2,1)S(1)}, bf16[256,512]{1,0:T(8,128)(2,1)S(1)}, f32[256,512]{1,0:T(8,128)S(1)}, bf16[256,512]{1,0:T(8,128)(2,1)S(1)}) custom-call(bf16[256,512]{1,0:T(8,128)(2,1)S(1)} %get-tuple-element.114.refs_0_, bf16[1024,512]{1,0:T(8,128)(2,1)S(1)} %get-tuple-element.115.refs_1_, ...), custom_call_target="tpu_custom_call" | custom-call | flops 8000000000 | tf_op jit(solution)/shard_map/attend_back/pallas_call | solution.py:73
  77.9 3.6 %attend_back.4 = (bf16[256,512]{1,0:T(8,128)(2,1)S(1)}, bf16[256,512]{1,0:T(8,128)(2,1)S(1)}, f32[256,512]{1,0:T(8,128)S(1)}, bf16[256,512]{1,0:T(8,128)(2,1)S(1)}) custom-call(bf16[256,512]{1,0:T(8,128)(2,1)S(1)} %get-tuple-element.114.refs_0_, bf16[1024,512]{1,0:T(8,128)(2,1)S(1)} %get-tuple-element.115.refs_1_, ...), custom_call_target="tpu_custom_call" | custom-call | flops 8000000000 | tf_op jit(solution)/shard_map/attend_back/pallas_call | solution.py:73
  81.6 5.7 %attend_back.5 = (bf16[512,512]{1,0:T(8,128)(2,1)S(1)}, bf16[512,512]{1,0:T(8,128)(2,1)S(1)}, bf16[256,512]{1,0:T(8,128)(2,1)S(1)}, f32[256,512]{1,0:T(8,128)S(1)}, bf16[256,512]{1,0:T(8,128)(2,1)S(1)}) custom-call(bf16[256,512]{1,0:T(8,128)(2,1)S(1)} %get-tuple-element.114.refs_0_, bf16[1024,512]{1,0:T(8,128)(2,1)S(1)} %get-tuple-element.115.refs_1_, ...), custom_call_target="tpu_custom_call" | custom-call | flops 8000000000 | tf_op jit(solution)/shard_map/attend_back/pallas_call | solution.py:73
  87.2 5.7 %collective-permute-done.19 = bf16[2,4,16,2560]{3,2,1,0:T(8,128)(2,1)S(1)} collective-permute-done((bf16[2,4,16,2560]{3,2,1,0:T(8,128)(2,1)S(1)}, bf16[2,4,16,2560]{3,2,1,0:T(8,128)(2,1)S(1)}, u32[]{:S(2)}, u32[]{:S(2)}) %collective-permute-start.19) | collective-permute-done | bytes 655392 | tf_op jit(solution)/shard_map/ppermute | solution.py:90
  99.4 5.7 %collective-permute-done.21 = bf16[256,512]{1,0:T(8,128)(2,1)S(1)} collective-permute-done((bf16[256,512]{1,0:T(8,128)(2,1)S(1)}, bf16[256,512]{1,0:T(8,128)(2,1)S(1)}, u32[]{:S(2)}, u32[]{:S(2)}) %collective-permute-start.21) | collective-permute-done | bytes 262176 | tf_op jit(solution)/shard_map/ppermute | solution.py:94
  105.4 2.9 %collective-permute-start.36 = (bf16[2,16,5120]{2,1,0:T(8,128)(2,1)S(1)}, bf16[2,16,5120]{2,1,0:T(8,128)(2,1)S(1)}, u32[]{:S(2)}, u32[]{:S(2)}) collective-permute-start(bf16[2,16,5120]{2,1,0:T(8,128)(2,1)S(1)} %pad_maximum_fusion.7), channel_id=1, source_target_pairs={{0,1},{1,0},{2,3},{3,2},{4,5},{5,4},{6,7},{7,6},{8,9},{9,8},{10,11... | collective-permute-start | bytes 983048 | tf_op jit(solution)/shard_map/ppermute | solution.py:90
  111.9 2.5 %collective-permute-done.24 = bf16[2,4,16,768]{3,2,1,0:T(8,128)(2,1)S(1)} collective-permute-done((bf16[2,4,16,768]{3,2,1,0:T(8,128)(2,1)S(1)}, bf16[2,4,16,768]{3,2,1,0:T(8,128)(2,1)S(1)}, u32[]{:S(2)}, u32[]{:S(2)}) %collective-permute-start.24) | collective-permute-done | bytes 196640 | tf_op jit(solution)/shard_map/ppermute | solution.py:90
  117.4 2.7 %collective-permute-done.22.refs_4_ = bf16[256,512]{1,0:T(8,128)(2,1)S(1)} collective-permute-done((bf16[256,512]{1,0:T(8,128)(2,1)S(1)}, bf16[256,512]{1,0:T(8,128)(2,1)S(1)}, u32[]{:S(2)}, u32[]{:S(2)}) %collective-permute-start.22) | collective-permute-done | bytes 262176 | tf_op jit(solution)/shard_map/ppermute | solution.py:94
  120.1 4.2 %collective-permute-start.37 = (bf16[1,16,5120]{2,1,0:T(8,128)(2,1)S(1)}, bf16[1,16,5120]{2,1,0:T(8,128)(2,1)S(1)}, u32[]{:S(2)}, u32[]{:S(2)}) collective-permute-start(bf16[1,16,5120]{2,1,0:T(8,128)(2,1)S(1)} %add_convert_fusion.9), channel_id=1, source_target_pairs={{0,2},{1,3},{2,0},{3,1},{4,6},{5,7},{6,4},{7,5},{8,10},{9,11},{10,... | collective-permute-start | bytes 491528 | tf_op jit(solution)/shard_map/ppermute | solution.py:90
  124.5 4.0 %collective-permute-done.37 = bf16[1,16,5120]{2,1,0:T(8,128)(2,1)S(1)} collective-permute-done((bf16[1,16,5120]{2,1,0:T(8,128)(2,1)S(1)}, bf16[1,16,5120]{2,1,0:T(8,128)(2,1)S(1)}, u32[]{:S(2)}, u32[]{:S(2)}) %collective-permute-start.37) | collective-permute-done | bytes 163872 | tf_op jit(solution)/shard_map/ppermute | solution.py:90
  132.2 2.1 %collective-permute-start.29 = (bf16[1,16,1536]{2,1,0:T(8,128)(2,1)S(1)}, bf16[1,16,1536]{2,1,0:T(8,128)(2,1)S(1)}, u32[]{:S(2)}, u32[]{:S(2)}) collective-permute-start(bf16[1,16,1536]{2,1,0:T(8,128)(2,1)S(1)} %add_convert_fusion.18), channel_id=1, source_target_pairs={{0,2},{1,3},{2,0},{3,1},{4,6},{5,7},{6,4},{7,5},{8,10},{9,11},{10,... | collective-permute-start | bytes 147464 | tf_op jit(solution)/shard_map/ppermute | solution.py:90
  134.3 4.1 %collective-permute-done.39 = bf16[16,5120]{1,0:T(8,128)(2,1)S(1)} collective-permute-done((bf16[16,5120]{1,0:T(8,128)(2,1)S(1)}, bf16[16,5120]{1,0:T(8,128)(2,1)S(1)}, u32[]{:S(2)}, u32[]{:S(2)}) %collective-permute-start.39) | collective-permute-done | bytes 163872 | tf_op jit(solution)/shard_map/ppermute | solution.py:90
  148.5 2.4 %finish_b.1 = (f32[1376,128]{1,0:T(8,128)}, f32[1376,128]{1,0:T(8,128)}, f32[344,512]{1,0:T(8,128)}, f32[128,512]{1,0:T(8,128)}, f32[1,128]{1,0:T(1,128)}) custom-call(s32[2]{0:T(128)S(1)} %pad_add_fusion.ids, bf16[64,5120]{1,0:T(8,128)(2,1)S(1)} %pad_maximum_fusion.3.mine, bf16[64,5120]{1,0:T(8,128)(2,1)S(1)} %collective-permute-done.41.part, ...), custom_call_target="tpu_custom_call" | custom-call | tf_op jit(solution)/shard_map/finish_b/pallas_call | solution.py:73
  (141 shorter events, 58.1 us)
Async XLA Ops:
  1.9 9.5 %collective-permute-start = (bf16[16,1664]{1,0:T(8,128)(2,1)S(1)}, bf16[16,1664]{1,0:T(8,128)(2,1)S(1)}, u32[]{:S(2)}, u32[]{:S(2)}) collective-permute-start(bf16[16,1664]{1,0:T(8,128)(2,1)S(1)} %pack_a.1), channel_id=1, source_target_pairs={{0,2},{1,3},{2,0},{3,1},{4,6},{5,7},{6,4},{7,5},{8,10},{9,11},{10,... | collective-permute-start | bytes 159752 | tf_op jit(solution)/shard_map/ppermute | solution.py:90
  6.0 10.2 %collective-permute-start.1 = (bf16[256,512]{1,0:T(8,128)(2,1)S(1)}, bf16[256,512]{1,0:T(8,128)(2,1)S(1)}, u32[]{:S(2)}, u32[]{:S(2)}) collective-permute-start(bf16[256,512]{1,0:T(8,128)(2,1)S(1)} %bitcast.45), channel_id=1, source_target_pairs={{0,1},{1,2},{2,3},{4,5},{5,6},{6,7},{8,9},{9,10},{10,11},{12,13},{... | collective-permute-start | bytes 786440 | tf_op jit(solution)/shard_map/ppermute | solution.py:94
  11.0 9.8 %collective-permute-start.3 = (bf16[16,5120]{1,0:T(8,128)(2,1)S(1)}, bf16[16,5120]{1,0:T(8,128)(2,1)S(1)}, u32[]{:S(2)}, u32[]{:S(2)}) collective-permute-start(bf16[16,5120]{1,0:T(8,128)(2,1)S(1)} %get-tuple-element.96), channel_id=1, source_target_pairs={{0,2},{1,3},{2,0},{3,1},{4,6},{5,7},{6,4},{7,5},{8,10},{9,11},{10,... | collective-permute-start | bytes 491528 | tf_op jit(solution)/shard_map/ppermute | solution.py:90
  18.8 9.6 %collective-permute-start.10 = (bf16[256,512]{1,0:T(8,128)(2,1)S(1)}, bf16[256,512]{1,0:T(8,128)(2,1)S(1)}, u32[]{:S(2)}, u32[]{:S(2)}) collective-permute-start(bf16[256,512]{1,0:T(8,128)(2,1)S(1)} %collective-permute-done.1.refs_1_), channel_id=1, source_target_pairs={{0,1},{1,2},{2,3},{4,5},{5,6},{6,7},{8,9},{9,10},{10,11},{12,13},{... | collective-permute-start | bytes 786440 | tf_op jit(solution)/shard_map/ppermute | solution.py:94
  24.2 8.9 %collective-permute-start.8 = (bf16[48,1664]{1,0:T(8,128)(2,1)S(1)}, bf16[48,1664]{1,0:T(8,128)(2,1)S(1)}, u32[]{:S(2)}, u32[]{:S(2)}) collective-permute-start(bf16[48,1664]{1,0:T(8,128)(2,1)S(1)} %get-tuple-element.202), channel_id=1, source_target_pairs={{0,16},{4,20},{8,24},{12,28},{16,0},{20,4},{24,8},{28,12},{1,17},{... | collective-permute-start | bytes 479240 | tf_op jit(solution)/shard_map/ppermute | solution.py:90
  25.7 7.4 %collective-permute-start.9 = (bf16[48,1664]{1,0:T(8,128)(2,1)S(1)}, bf16[48,1664]{1,0:T(8,128)(2,1)S(1)}, u32[]{:S(2)}, u32[]{:S(2)}) collective-permute-start(bf16[48,1664]{1,0:T(8,128)(2,1)S(1)} %get-tuple-element.202), channel_id=1, source_target_pairs={{0,24},{4,28},{8,16},{12,20},{16,8},{20,12},{24,0},{28,4},{1,25},{... | collective-permute-start | bytes 479240 | tf_op jit(solution)/shard_map/ppermute | solution.py:90
  26.2 9.6 %collective-permute-start.4 = (bf16[32,5120]{1,0:T(8,128)(2,1)S(1)}, bf16[32,5120]{1,0:T(8,128)(2,1)S(1)}, u32[]{:S(2)}, u32[]{:S(2)}) collective-permute-start(bf16[32,5120]{1,0:T(8,128)(2,1)S(1)} %pad_maximum_fusion.6), channel_id=1, source_target_pairs={{0,1},{1,0},{2,3},{3,2},{4,5},{5,4},{6,7},{7,6},{8,9},{9,8},{10,11... | collective-permute-start | bytes 983048 | tf_op jit(solution)/shard_map/ppermute | solution.py:90
  42.7 13.7 %collective-permute-start.13 = (bf16[96,2560]{1,0:T(8,128)(2,1)S(1)}, bf16[96,2560]{1,0:T(8,128)(2,1)S(1)}, u32[]{:S(2)}, u32[]{:S(2)}) collective-permute-start(bf16[96,2560]{1,0:T(8,128)(2,1)S(1)} %pad_maximum_fusion.5), channel_id=1, source_target_pairs={{0,8},{4,12},{8,0},{12,4},{16,24},{20,28},{24,16},{28,20},{1,9},{5... | collective-permute-start | bytes 1474568 | tf_op jit(solution)/shard_map/ppermute | solution.py:90
  44.3 13.4 %collective-permute-start.12 = (bf16[96,2560]{1,0:T(8,128)(2,1)S(1)}, bf16[96,2560]{1,0:T(8,128)(2,1)S(1)}, u32[]{:S(2)}, u32[]{:S(2)}) collective-permute-start(bf16[96,2560]{1,0:T(8,128)(2,1)S(1)} %pad_maximum_fusion.4), channel_id=1, source_target_pairs={{0,16},{4,20},{8,24},{12,28},{16,0},{20,4},{24,8},{28,12},{1,17},{... | collective-permute-start | bytes 1474568 | tf_op jit(solution)/shard_map/ppermute | solution.py:90
  73.2 22.7 %collective-permute-start.18 = (bf16[256,512]{1,0:T(8,128)(2,1)S(1)}, bf16[256,512]{1,0:T(8,128)(2,1)S(1)}, u32[]{:S(2)}, u32[]{:S(2)}) collective-permute-start(bf16[256,512]{1,0:T(8,128)(2,1)S(1)} %get-tuple-element.134), channel_id=1, source_target_pairs={{1,0},{2,1},{3,2},{5,4},{6,5},{7,6},{9,8},{10,9},{11,10},{13,12},{... | collective-permute-start | bytes 786440 | tf_op jit(solution)/shard_map/ppermute | solution.py:94
  75.9 17.1 %collective-permute-start.19 = (bf16[2,4,16,2560]{3,2,1,0:T(8,128)(2,1)S(1)}, bf16[2,4,16,2560]{3,2,1,0:T(8,128)(2,1)S(1)}, u32[]{:S(2)}, u32[]{:S(2)}) collective-permute-start(bf16[2,4,16,2560]{3,2,1,0:T(8,128)(2,1)S(1)} %pad_maximum_fusion.2), channel_id=1, source_target_pairs={{0,8},{4,12},{8,0},{12,4},{16,24},{20,28},{24,16},{28,20},{1,9},{5... | collective-permute-start | bytes 1966088 | tf_op jit(solution)/shard_map/ppermute | solution.py:90
  76.5 16.7 %collective-permute-start.20 = (bf16[2,4,16,2560]{3,2,1,0:T(8,128)(2,1)S(1)}, bf16[2,4,16,2560]{3,2,1,0:T(8,128)(2,1)S(1)}, u32[]{:S(2)}, u32[]{:S(2)}) collective-permute-start(bf16[2,4,16,2560]{3,2,1,0:T(8,128)(2,1)S(1)} %stack.48), channel_id=1, source_target_pairs={{0,16},{4,20},{8,24},{12,28},{16,0},{20,4},{24,8},{28,12},{1,17},{... | collective-permute-start | bytes 1966088 | tf_op jit(solution)/shard_map/ppermute | solution.py:90
  93.5 11.6 %collective-permute-start.34 = (bf16[1,4,16,2560]{3,2,1,0:T(8,128)(2,1)S(1)}, bf16[1,4,16,2560]{3,2,1,0:T(8,128)(2,1)S(1)}, u32[]{:S(2)}, u32[]{:S(2)}) collective-permute-start(bf16[1,4,16,2560]{3,2,1,0:T(8,128)(2,1)S(1)} %get-tuple-element.182), channel_id=1, source_target_pairs={{0,16},{4,20},{8,24},{12,28},{16,0},{20,4},{24,8},{28,12},{1,17},{... | collective-permute-start | bytes 983048 | tf_op jit(solution)/shard_map/ppermute | solution.py:90
  95.1 10.1 %collective-permute-start.35 = (bf16[1,4,16,2560]{3,2,1,0:T(8,128)(2,1)S(1)}, bf16[1,4,16,2560]{3,2,1,0:T(8,128)(2,1)S(1)}, u32[]{:S(2)}, u32[]{:S(2)}) collective-permute-start(bf16[1,4,16,2560]{3,2,1,0:T(8,128)(2,1)S(1)} %get-tuple-element.177), channel_id=1, source_target_pairs={{0,8},{4,12},{8,0},{12,4},{16,24},{20,28},{24,16},{28,20},{1,9},{5... | collective-permute-start | bytes 983048 | tf_op jit(solution)/shard_map/ppermute | solution.py:90
  96.0 9.1 %collective-permute-start.21 = (bf16[256,512]{1,0:T(8,128)(2,1)S(1)}, bf16[256,512]{1,0:T(8,128)(2,1)S(1)}, u32[]{:S(2)}, u32[]{:S(2)}) collective-permute-start(bf16[256,512]{1,0:T(8,128)(2,1)S(1)} %add_convert_fusion.7), channel_id=1, source_target_pairs={{1,0},{2,1},{3,2},{5,4},{6,5},{7,6},{9,8},{10,9},{11,10},{13,12},{... | collective-permute-start | bytes 786440 | tf_op jit(solution)/shard_map/ppermute | solution.py:94
  99.4 9.0 %collective-permute-start.23 = (bf16[4,4,16,1536]{3,2,1,0:T(8,128)(2,1)S(1)}, bf16[4,4,16,1536]{3,2,1,0:T(8,128)(2,1)S(1)}, u32[]{:S(2)}, u32[]{:S(2)}) collective-permute-start(bf16[4,4,16,1536]{3,2,1,0:T(8,128)(2,1)S(1)} %get-tuple-element.151), channel_id=1, source_target_pairs={{0,4},{4,0},{8,12},{12,8},{16,20},{20,16},{24,28},{28,24},{1,5},{5... | collective-permute-start | bytes 2359304 | tf_op jit(solution)/shard_map/ppermute | solution.py:90
  105.4 12.0 %collective-permute-start.36 = (bf16[2,16,5120]{2,1,0:T(8,128)(2,1)S(1)}, bf16[2,16,5120]{2,1,0:T(8,128)(2,1)S(1)}, u32[]{:S(2)}, u32[]{:S(2)}) collective-permute-start(bf16[2,16,5120]{2,1,0:T(8,128)(2,1)S(1)} %pad_maximum_fusion.7), channel_id=1, source_target_pairs={{0,1},{1,0},{2,3},{3,2},{4,5},{5,4},{6,7},{7,6},{8,9},{9,8},{10,11... | collective-permute-start | bytes 983048 | tf_op jit(solution)/shard_map/ppermute | solution.py:90
  110.6 9.5 %collective-permute-start.22 = (bf16[256,512]{1,0:T(8,128)(2,1)S(1)}, bf16[256,512]{1,0:T(8,128)(2,1)S(1)}, u32[]{:S(2)}, u32[]{:S(2)}) collective-permute-start(bf16[256,512]{1,0:T(8,128)(2,1)S(1)} %add_convert_fusion.6), channel_id=1, source_target_pairs={{1,0},{2,1},{3,2},{5,4},{6,5},{7,6},{9,8},{10,9},{11,10},{13,12},{... | collective-permute-start | bytes 786440 | tf_op jit(solution)/shard_map/ppermute | solution.py:94
  116.5 7.8 %collective-permute-start.26 = (bf16[1,4,16,768]{3,2,1,0:T(8,128)(2,1)S(1)}, bf16[1,4,16,768]{3,2,1,0:T(8,128)(2,1)S(1)}, u32[]{:S(2)}, u32[]{:S(2)}) collective-permute-start(bf16[1,4,16,768]{3,2,1,0:T(8,128)(2,1)S(1)} %get-tuple-element.188), channel_id=1, source_target_pairs={{0,16},{4,20},{8,24},{12,28},{16,0},{20,4},{24,8},{28,12},{1,17},{... | collective-permute-start | bytes 294920 | tf_op jit(solution)/shard_map/ppermute | solution.py:90
  116.9 7.4 %collective-permute-start.27 = (bf16[1,4,16,768]{3,2,1,0:T(8,128)(2,1)S(1)}, bf16[1,4,16,768]{3,2,1,0:T(8,128)(2,1)S(1)}, u32[]{:S(2)}, u32[]{:S(2)}) collective-permute-start(bf16[1,4,16,768]{3,2,1,0:T(8,128)(2,1)S(1)} %get-tuple-element.187), channel_id=1, source_target_pairs={{0,8},{4,12},{8,0},{12,4},{16,24},{20,28},{24,16},{28,20},{1,9},{5... | collective-permute-start | bytes 294920 | tf_op jit(solution)/shard_map/ppermute | solution.py:90
  120.1 8.4 %collective-permute-start.37 = (bf16[1,16,5120]{2,1,0:T(8,128)(2,1)S(1)}, bf16[1,16,5120]{2,1,0:T(8,128)(2,1)S(1)}, u32[]{:S(2)}, u32[]{:S(2)}) collective-permute-start(bf16[1,16,5120]{2,1,0:T(8,128)(2,1)S(1)} %add_convert_fusion.9), channel_id=1, source_target_pairs={{0,2},{1,3},{2,0},{3,1},{4,6},{5,7},{6,4},{7,5},{8,10},{9,11},{10,... | collective-permute-start | bytes 491528 | tf_op jit(solution)/shard_map/ppermute | solution.py:90
  124.4 7.7 %collective-permute-start.28 = (bf16[2,16,1536]{2,1,0:T(8,128)(2,1)S(1)}, bf16[2,16,1536]{2,1,0:T(8,128)(2,1)S(1)}, u32[]{:S(2)}, u32[]{:S(2)}) collective-permute-start(bf16[2,16,1536]{2,1,0:T(8,128)(2,1)S(1)} %pad_maximum_fusion.12), channel_id=1, source_target_pairs={{0,1},{1,0},{2,3},{3,2},{4,5},{5,4},{6,7},{7,6},{8,9},{9,8},{10,11... | collective-permute-start | bytes 294920 | tf_op jit(solution)/shard_map/ppermute | solution.py:90
  130.3 8.1 %collective-permute-start.39 = (bf16[16,5120]{1,0:T(8,128)(2,1)S(1)}, bf16[16,5120]{1,0:T(8,128)(2,1)S(1)}, u32[]{:S(2)}, u32[]{:S(2)}) collective-permute-start(bf16[16,5120]{1,0:T(8,128)(2,1)S(1)} %fusion.4), channel_id=1, source_target_pairs={{0,16},{4,20},{8,24},{12,28},{16,0},{20,4},{24,8},{28,12},{1,17},{... | collective-permute-start | bytes 491528 | tf_op jit(solution)/shard_map/ppermute | solution.py:90
  130.4 8.0 %collective-permute-start.40 = (bf16[16,5120]{1,0:T(8,128)(2,1)S(1)}, bf16[16,5120]{1,0:T(8,128)(2,1)S(1)}, u32[]{:S(2)}, u32[]{:S(2)}) collective-permute-start(bf16[16,5120]{1,0:T(8,128)(2,1)S(1)} %fusion.4), channel_id=1, source_target_pairs={{0,24},{4,28},{8,16},{12,20},{16,8},{20,12},{24,0},{28,4},{1,25},{... | collective-permute-start | bytes 491528 | tf_op jit(solution)/shard_map/ppermute | solution.py:90
  (28 other events, 144.9 us)

commit v6 on v5

--- a/solution.py
+++ b/solution.py
@@ -803,7 +803,7 @@
         terms_a = plane_step(plan, terms_a)
     total_a = jnp.concatenate([mine[0] for mine, _ in terms_a], axis=-1)
     total_b = jnp.concatenate([mine[0] for mine, _ in terms_b], axis=-1)
-    final_b = share(plan, combine_line(plan, total_b, (own, hops[-1])))
+    final_b = share(plan, combine_line(plan, total_b, (own, own)))
     final_a = share(plan, combine_line(plan, total_a, (own, hops[-1])))
     (input_grad,) = call(
         functools.partial(residual_kernel, plan),

time: 151 us -> 149 us (0.987)
    ppermute x6, waiting for transfers between devices: 14.8 us -> 12.1 us  [shift(): lax.ppermute(value, 'grp', [(i, i + k) for i in range(size) if 0 <= i + k...]
    ppermute x36, waiting for transfers between devices: 38.7 us -> 40.5 us  [swap(): return lax.ppermute(value, axis, [(i, i ^ k) for i in range(size)])]
  transfers between devices with their start and end apart: 42 -> 42, of which waited for: 23 -> 25; matrix products, arithmetic and copies ran while one was open for 2% -> 2% of each run, Pallas kernels for 19% -> 19%
where the time goes in v6:
time: 149 us
  starting transfers between devices  52.8 us (35%)
  waiting for transfers between devices  52.5 us (35%)
  Pallas kernels  39.1 us (26%)
  other arithmetic  2.75 us (2%)
    ppermute x36, starting transfers between devices, swap(): return lax.ppermute(value, axis, [(i, i ^ k) for i in range(size)])  40.7 us
    ppermute x36, waiting for transfers between devices, swap(): return lax.ppermute(value, axis, [(i, i ^ k) for i in range(size)])  40.5 us
    pallas_call x12, Pallas kernels, call(): pl.pallas_call(body, out_shape=outs, in_specs=specs, out_specs=[VMEM] * l...  39.1 us
    ppermute x6, starting transfers between devices, shift(): lax.ppermute(value, 'grp', [(i, i + k) for i in range(size) if 0 <= i + k...  12.1 us
    ppermute x6, waiting for transfers between devices, shift(): lax.ppermute(value, 'grp', [(i, i + k) for i in range(size) if 0 <= i + k...  12.1 us
  transfers between devices with their start and end apart: 42, of which 25 were waited for; matrix products, arithmetic and copies ran while one was open for 2% of the time, Pallas kernels for 19%

profile of v6, /device:TPU:0, one launch (start us, length us, event | category | flops | bytes accessed | tf_op | source)
XLA Modules:
  0.0 148.8 jit_solution(12532333200401039046)
XLA Ops:
  1.9 4.1 %collective-permute-start = (bf16[16,1664]{1,0:T(8,128)(2,1)S(1)}, bf16[16,1664]{1,0:T(8,128)(2,1)S(1)}, u32[]{:S(2)}, u32[]{:S(2)}) collective-permute-start(bf16[16,1664]{1,0:T(8,128)(2,1)S(1)} %pack_a.1), channel_id=1, source_target_pairs={{0,2},{1,3},{2,0},{3,1},{4,6},{5,7},{6,4},{7,5},{8,10},{9,11},{10,... | collective-permute-start | bytes 159752 | tf_op jit(solution)/shard_map/ppermute | solution.py:90
  6.0 3.5 %collective-permute-start.1 = (bf16[256,512]{1,0:T(8,128)(2,1)S(1)}, bf16[256,512]{1,0:T(8,128)(2,1)S(1)}, u32[]{:S(2)}, u32[]{:S(2)}) collective-permute-start(bf16[256,512]{1,0:T(8,128)(2,1)S(1)} %bitcast.45), channel_id=1, source_target_pairs={{0,1},{1,2},{2,3},{4,5},{5,6},{6,7},{8,9},{9,10},{10,11},{12,13},{... | collective-permute-start | bytes 786440 | tf_op jit(solution)/shard_map/ppermute | solution.py:94
  11.4 4.7 %collective-permute-done.1.refs_1_ = bf16[256,512]{1,0:T(8,128)(2,1)S(1)} collective-permute-done((bf16[256,512]{1,0:T(8,128)(2,1)S(1)}, bf16[256,512]{1,0:T(8,128)(2,1)S(1)}, u32[]{:S(2)}, u32[]{:S(2)}) %collective-permute-start.1) | collective-permute-done | bytes 262176 | tf_op jit(solution)/shard_map/ppermute | solution.py:94
  16.2 2.5 %collective-permute-start.2 = (bf16[32,1664]{1,0:T(8,128)(2,1)S(1)}, bf16[32,1664]{1,0:T(8,128)(2,1)S(1)}, u32[]{:S(2)}, u32[]{:S(2)}) collective-permute-start(bf16[32,1664]{1,0:T(8,128)(2,1)S(1)} %pad_maximum_fusion.11), channel_id=1, source_target_pairs={{0,1},{1,0},{2,3},{3,2},{4,5},{5,4},{6,7},{7,6},{8,9},{9,8},{10,11... | collective-permute-start | bytes 319496 | tf_op jit(solution)/shard_map/ppermute | solution.py:90
  29.5 3.6 %collective-permute-done.8 = bf16[48,1664]{1,0:T(8,128)(2,1)S(1)} collective-permute-done((bf16[48,1664]{1,0:T(8,128)(2,1)S(1)}, bf16[48,1664]{1,0:T(8,128)(2,1)S(1)}, u32[]{:S(2)}, u32[]{:S(2)}) %collective-permute-start.8) | collective-permute-done | bytes 159776 | tf_op jit(solution)/shard_map/ppermute | solution.py:90
  33.1 2.7 %collective-permute-start.11 = (bf16[256,512]{1,0:T(8,128)(2,1)S(1)}, bf16[256,512]{1,0:T(8,128)(2,1)S(1)}, u32[]{:S(2)}, u32[]{:S(2)}) collective-permute-start(bf16[256,512]{1,0:T(8,128)(2,1)S(1)} %collective-permute-done.10.refs_2_), channel_id=1, source_target_pairs={{0,1},{1,2},{2,3},{4,5},{5,6},{6,7},{8,9},{9,10},{10,11},{12,13},{... | collective-permute-start | bytes 786440 | tf_op jit(solution)/shard_map/ppermute | solution.py:94
  39.6 2.5 %collective-permute-done.5 = bf16[48,2560]{1,0:T(8,128)(2,1)S(1)} collective-permute-done((bf16[48,2560]{1,0:T(8,128)(2,1)S(1)}, bf16[48,2560]{1,0:T(8,128)(2,1)S(1)}, u32[]{:S(2)}, u32[]{:S(2)}) %collective-permute-start.5) | collective-permute-done | bytes 245792 | tf_op jit(solution)/shard_map/ppermute | solution.py:90
  45.2 8.6 %attend.1 = (f32[256,512]{1,0:T(8,128)S(1)}, bf16[256,512]{1,0:T(8,128)(2,1)S(1)}, bf16[1024,512]{1,0:T(8,128)(2,1)S(1)}, bf16[1024,512]{1,0:T(8,128)(2,1)S(1)},...) custom-call(s32[2]{0:T(128)S(1)} %pad_add_fusion.ids, ...), custom_call_target="tpu_custom_call" | custom-call | flops 11000000512 | tf_op jit(solution)/shard_map/attend/pallas_call | solution.py:73
  53.9 2.6 %collective-permute-done.13 = bf16[96,2560]{1,0:T(8,128)(2,1)S(1)} collective-permute-done((bf16[96,2560]{1,0:T(8,128)(2,1)S(1)}, bf16[96,2560]{1,0:T(8,128)(2,1)S(1)}, u32[]{:S(2)}, u32[]{:S(2)}) %collective-permute-start.13) | collective-permute-done | bytes 491552 | tf_op jit(solution)/shard_map/ppermute | solution.py:90
  61.9 4.9 %mlp.1 = (bf16[256,512]{1,0:T(8,128)(2,1)}, f32[256,512]{1,0:T(8,128)S(1)}, bf16[256,512]{1,0:T(8,128)(2,1)S(1)}, bf16[256,512]{1,0:T(8,128)(2,1)S(1)}, bf16[256...) custom-call(s32[2]{0:T(128)S(1)} %pad_add_fusion.ids, ...), custom_call_target="tpu_custom_call" | custom-call | flops 8000000000 | tf_op jit(solution)/shard_map/mlp/pallas_call | solution.py:73
  66.9 2.5 %mlp_grads.1 = (bf16[4,4,16,5120]{3,2,1,0:T(8,128)(2,1)S(1)}, bf16[4,4,16,5120]{3,2,1,0:T(8,128)(2,1)S(1)}) custom-call(s32[2]{0:T(128)S(1)} %pad_add_fusion.ids, bf16[256,512]{1,0:T(8,128)(2,1)S(1)} %get-tuple-element.118.n2, bf16[256,1536]{1,0:T(8,128)(2,1)S(1)} %get-tuple-element.119.hid, bf16[256,1536]{1,0:T(8,128)(2,1)S(1)} %get-tuple-element.120.dg, ...), custom_call_target="tpu_custom_call" | custom-call | flops 6000000000 | tf_op jit(solution)/shard_map/mlp_grads/pallas_call | solution.py:73
  69.6 3.6 %attend_back.3 = (bf16[256,512]{1,0:T(8,128)(2,1)S(1)}, bf16[256,512]{1,0:T(8,128)(2,1)S(1)}, f32[256,512]{1,0:T(8,128)S(1)}, bf16[256,512]{1,0:T(8,128)(2,1)S(1)}) custom-call(bf16[256,512]{1,0:T(8,128)(2,1)S(1)} %get-tuple-element.114.refs_0_, bf16[1024,512]{1,0:T(8,128)(2,1)S(1)} %get-tuple-element.115.refs_1_, ...), custom_call_target="tpu_custom_call" | custom-call | flops 8000000000 | tf_op jit(solution)/shard_map/attend_back/pallas_call | solution.py:73
  77.9 3.6 %attend_back.4 = (bf16[256,512]{1,0:T(8,128)(2,1)S(1)}, bf16[256,512]{1,0:T(8,128)(2,1)S(1)}, f32[256,512]{1,0:T(8,128)S(1)}, bf16[256,512]{1,0:T(8,128)(2,1)S(1)}) custom-call(bf16[256,512]{1,0:T(8,128)(2,1)S(1)} %get-tuple-element.114.refs_0_, bf16[1024,512]{1,0:T(8,128)(2,1)S(1)} %get-tuple-element.115.refs_1_, ...), custom_call_target="tpu_custom_call" | custom-call | flops 8000000000 | tf_op jit(solution)/shard_map/attend_back/pallas_call | solution.py:73
  81.6 5.7 %attend_back.5 = (bf16[512,512]{1,0:T(8,128)(2,1)S(1)}, bf16[512,512]{1,0:T(8,128)(2,1)S(1)}, bf16[256,512]{1,0:T(8,128)(2,1)S(1)}, f32[256,512]{1,0:T(8,128)S(1)}, bf16[256,512]{1,0:T(8,128)(2,1)S(1)}) custom-call(bf16[256,512]{1,0:T(8,128)(2,1)S(1)} %get-tuple-element.114.refs_0_, bf16[1024,512]{1,0:T(8,128)(2,1)S(1)} %get-tuple-element.115.refs_1_, ...), custom_call_target="tpu_custom_call" | custom-call | flops 8000000000 | tf_op jit(solution)/shard_map/attend_back/pallas_call | solution.py:73
  87.2 5.7 %collective-permute-done.19 = bf16[2,4,16,2560]{3,2,1,0:T(8,128)(2,1)S(1)} collective-permute-done((bf16[2,4,16,2560]{3,2,1,0:T(8,128)(2,1)S(1)}, bf16[2,4,16,2560]{3,2,1,0:T(8,128)(2,1)S(1)}, u32[]{:S(2)}, u32[]{:S(2)}) %collective-permute-start.19) | collective-permute-done | bytes 655392 | tf_op jit(solution)/shard_map/ppermute | solution.py:90
  99.4 5.7 %collective-permute-done.21 = bf16[256,512]{1,0:T(8,128)(2,1)S(1)} collective-permute-done((bf16[256,512]{1,0:T(8,128)(2,1)S(1)}, bf16[256,512]{1,0:T(8,128)(2,1)S(1)}, u32[]{:S(2)}, u32[]{:S(2)}) %collective-permute-start.21) | collective-permute-done | bytes 262176 | tf_op jit(solution)/shard_map/ppermute | solution.py:94
  105.4 2.9 %collective-permute-start.36 = (bf16[2,16,5120]{2,1,0:T(8,128)(2,1)S(1)}, bf16[2,16,5120]{2,1,0:T(8,128)(2,1)S(1)}, u32[]{:S(2)}, u32[]{:S(2)}) collective-permute-start(bf16[2,16,5120]{2,1,0:T(8,128)(2,1)S(1)} %pad_maximum_fusion.7), channel_id=1, source_target_pairs={{0,1},{1,0},{2,3},{3,2},{4,5},{5,4},{6,7},{7,6},{8,9},{9,8},{10,11... | collective-permute-start | bytes 983048 | tf_op jit(solution)/shard_map/ppermute | solution.py:90
  111.9 2.5 %collective-permute-done.24 = bf16[2,4,16,768]{3,2,1,0:T(8,128)(2,1)S(1)} collective-permute-done((bf16[2,4,16,768]{3,2,1,0:T(8,128)(2,1)S(1)}, bf16[2,4,16,768]{3,2,1,0:T(8,128)(2,1)S(1)}, u32[]{:S(2)}, u32[]{:S(2)}) %collective-permute-start.24) | collective-permute-done | bytes 196640 | tf_op jit(solution)/shard_map/ppermute | solution.py:90
  117.4 2.8 %collective-permute-start.37 = (bf16[1,16,5120]{2,1,0:T(8,128)(2,1)S(1)}, bf16[1,16,5120]{2,1,0:T(8,128)(2,1)S(1)}, u32[]{:S(2)}, u32[]{:S(2)}) collective-permute-start(bf16[1,16,5120]{2,1,0:T(8,128)(2,1)S(1)} %add_convert_fusion.9), channel_id=1, source_target_pairs={{0,2},{1,3},{2,0},{3,1},{4,6},{5,7},{6,4},{7,5},{8,10},{9,11},{10,... | collective-permute-start | bytes 491528 | tf_op jit(solution)/shard_map/ppermute | solution.py:90
  121.7 2.5 %collective-permute-done.37 = bf16[1,16,5120]{2,1,0:T(8,128)(2,1)S(1)} collective-permute-done((bf16[1,16,5120]{2,1,0:T(8,128)(2,1)S(1)}, bf16[1,16,5120]{2,1,0:T(8,128)(2,1)S(1)}, u32[]{:S(2)}, u32[]{:S(2)}) %collective-permute-start.37) | collective-permute-done | bytes 163872 | tf_op jit(solution)/shard_map/ppermute | solution.py:90
  125.6 3.2 %collective-permute-start.39 = (bf16[16,5120]{1,0:T(8,128)(2,1)S(1)}, bf16[16,5120]{1,0:T(8,128)(2,1)S(1)}, u32[]{:S(2)}, u32[]{:S(2)}) collective-permute-start(bf16[16,5120]{1,0:T(8,128)(2,1)S(1)} %fusion.4), channel_id=1, source_target_pairs={{0,16},{4,20},{8,24},{12,28},{16,0},{20,4},{24,8},{28,12},{1,17},{... | collective-permute-start | bytes 491528 | tf_op jit(solution)/shard_map/ppermute | solution.py:90
  130.2 4.3 %collective-permute-done.39 = bf16[16,5120]{1,0:T(8,128)(2,1)S(1)} collective-permute-done((bf16[16,5120]{1,0:T(8,128)(2,1)S(1)}, bf16[16,5120]{1,0:T(8,128)(2,1)S(1)}, u32[]{:S(2)}, u32[]{:S(2)}) %collective-permute-start.39) | collective-permute-done | bytes 163872 | tf_op jit(solution)/shard_map/ppermute | solution.py:90
  140.6 2.2 %collective-permute-done.32 = bf16[16,1536]{1,0:T(8,128)(2,1)S(1)} collective-permute-done((bf16[16,1536]{1,0:T(8,128)(2,1)S(1)}, bf16[16,1536]{1,0:T(8,128)(2,1)S(1)}, u32[]{:S(2)}, u32[]{:S(2)}) %collective-permute-start.32) | collective-permute-done | bytes 49184 | tf_op jit(solution)/shard_map/ppermute | solution.py:90
  146.4 2.4 %finish_b.1 = (f32[1376,128]{1,0:T(8,128)}, f32[1376,128]{1,0:T(8,128)}, f32[344,512]{1,0:T(8,128)}, f32[128,512]{1,0:T(8,128)}, f32[1,128]{1,0:T(1,128)}) custom-call(s32[2]{0:T(128)S(1)} %pad_add_fusion.ids, bf16[64,5120]{1,0:T(8,128)(2,1)S(1)} %pad_maximum_fusion.3.mine, bf16[64,5120]{1,0:T(8,128)(2,1)S(1)} %collective-permute-done.41.part, ...), custom_call_target="tpu_custom_call" | custom-call | tf_op jit(solution)/shard_map/finish_b/pallas_call | solution.py:73
  (141 shorter events, 58.1 us)
Async XLA Ops:
  1.9 9.5 %collective-permute-start = (bf16[16,1664]{1,0:T(8,128)(2,1)S(1)}, bf16[16,1664]{1,0:T(8,128)(2,1)S(1)}, u32[]{:S(2)}, u32[]{:S(2)}) collective-permute-start(bf16[16,1664]{1,0:T(8,128)(2,1)S(1)} %pack_a.1), channel_id=1, source_target_pairs={{0,2},{1,3},{2,0},{3,1},{4,6},{5,7},{6,4},{7,5},{8,10},{9,11},{10,... | collective-permute-start | bytes 159752 | tf_op jit(solution)/shard_map/ppermute | solution.py:90
  6.0 10.2 %collective-permute-start.1 = (bf16[256,512]{1,0:T(8,128)(2,1)S(1)}, bf16[256,512]{1,0:T(8,128)(2,1)S(1)}, u32[]{:S(2)}, u32[]{:S(2)}) collective-permute-start(bf16[256,512]{1,0:T(8,128)(2,1)S(1)} %bitcast.45), channel_id=1, source_target_pairs={{0,1},{1,2},{2,3},{4,5},{5,6},{6,7},{8,9},{9,10},{10,11},{12,13},{... | collective-permute-start | bytes 786440 | tf_op jit(solution)/shard_map/ppermute | solution.py:94
  11.0 9.8 %collective-permute-start.3 = (bf16[16,5120]{1,0:T(8,128)(2,1)S(1)}, bf16[16,5120]{1,0:T(8,128)(2,1)S(1)}, u32[]{:S(2)}, u32[]{:S(2)}) collective-permute-start(bf16[16,5120]{1,0:T(8,128)(2,1)S(1)} %get-tuple-element.96), channel_id=1, source_target_pairs={{0,2},{1,3},{2,0},{3,1},{4,6},{5,7},{6,4},{7,5},{8,10},{9,11},{10,... | collective-permute-start | bytes 491528 | tf_op jit(solution)/shard_map/ppermute | solution.py:90
  18.8 9.6 %collective-permute-start.10 = (bf16[256,512]{1,0:T(8,128)(2,1)S(1)}, bf16[256,512]{1,0:T(8,128)(2,1)S(1)}, u32[]{:S(2)}, u32[]{:S(2)}) collective-permute-start(bf16[256,512]{1,0:T(8,128)(2,1)S(1)} %collective-permute-done.1.refs_1_), channel_id=1, source_target_pairs={{0,1},{1,2},{2,3},{4,5},{5,6},{6,7},{8,9},{9,10},{10,11},{12,13},{... | collective-permute-start | bytes 786440 | tf_op jit(solution)/shard_map/ppermute | solution.py:94
  22.6 6.9 %collective-permute-start.7 = (bf16[48,1664]{1,0:T(8,128)(2,1)S(1)}, bf16[48,1664]{1,0:T(8,128)(2,1)S(1)}, u32[]{:S(2)}, u32[]{:S(2)}) collective-permute-start(bf16[48,1664]{1,0:T(8,128)(2,1)S(1)} %get-tuple-element.202), channel_id=1, source_target_pairs={{0,8},{4,12},{8,0},{12,4},{16,24},{20,28},{24,16},{28,20},{1,9},{5... | collective-permute-start | bytes 479240 | tf_op jit(solution)/shard_map/ppermute | solution.py:90
  24.2 8.9 %collective-permute-start.8 = (bf16[48,1664]{1,0:T(8,128)(2,1)S(1)}, bf16[48,1664]{1,0:T(8,128)(2,1)S(1)}, u32[]{:S(2)}, u32[]{:S(2)}) collective-permute-start(bf16[48,1664]{1,0:T(8,128)(2,1)S(1)} %get-tuple-element.202), channel_id=1, source_target_pairs={{0,16},{4,20},{8,24},{12,28},{16,0},{20,4},{24,8},{28,12},{1,17},{... | collective-permute-start | bytes 479240 | tf_op jit(solution)/shard_map/ppermute | solution.py:90
  25.7 7.4 %collective-permute-start.9 = (bf16[48,1664]{1,0:T(8,128)(2,1)S(1)}, bf16[48,1664]{1,0:T(8,128)(2,1)S(1)}, u32[]{:S(2)}, u32[]{:S(2)}) collective-permute-start(bf16[48,1664]{1,0:T(8,128)(2,1)S(1)} %get-tuple-element.202), channel_id=1, source_target_pairs={{0,24},{4,28},{8,16},{12,20},{16,8},{20,12},{24,0},{28,4},{1,25},{... | collective-permute-start | bytes 479240 | tf_op jit(solution)/shard_map/ppermute | solution.py:90
  26.2 9.6 %collective-permute-start.4 = (bf16[32,5120]{1,0:T(8,128)(2,1)S(1)}, bf16[32,5120]{1,0:T(8,128)(2,1)S(1)}, u32[]{:S(2)}, u32[]{:S(2)}) collective-permute-start(bf16[32,5120]{1,0:T(8,128)(2,1)S(1)} %pad_maximum_fusion.6), channel_id=1, source_target_pairs={{0,1},{1,0},{2,3},{3,2},{4,5},{5,4},{6,7},{7,6},{8,9},{9,8},{10,11... | collective-permute-start | bytes 983048 | tf_op jit(solution)/shard_map/ppermute | solution.py:90
  42.7 13.7 %collective-permute-start.13 = (bf16[96,2560]{1,0:T(8,128)(2,1)S(1)}, bf16[96,2560]{1,0:T(8,128)(2,1)S(1)}, u32[]{:S(2)}, u32[]{:S(2)}) collective-permute-start(bf16[96,2560]{1,0:T(8,128)(2,1)S(1)} %pad_maximum_fusion.5), channel_id=1, source_target_pairs={{0,8},{4,12},{8,0},{12,4},{16,24},{20,28},{24,16},{28,20},{1,9},{5... | collective-permute-start | bytes 1474568 | tf_op jit(solution)/shard_map/ppermute | solution.py:90
  44.3 13.4 %collective-permute-start.12 = (bf16[96,2560]{1,0:T(8,128)(2,1)S(1)}, bf16[96,2560]{1,0:T(8,128)(2,1)S(1)}, u32[]{:S(2)}, u32[]{:S(2)}) collective-permute-start(bf16[96,2560]{1,0:T(8,128)(2,1)S(1)} %pad_maximum_fusion.4), channel_id=1, source_target_pairs={{0,16},{4,20},{8,24},{12,28},{16,0},{20,4},{24,8},{28,12},{1,17},{... | collective-permute-start | bytes 1474568 | tf_op jit(solution)/shard_map/ppermute | solution.py:90
  73.2 22.7 %collective-permute-start.18 = (bf16[256,512]{1,0:T(8,128)(2,1)S(1)}, bf16[256,512]{1,0:T(8,128)(2,1)S(1)}, u32[]{:S(2)}, u32[]{:S(2)}) collective-permute-start(bf16[256,512]{1,0:T(8,128)(2,1)S(1)} %get-tuple-element.134), channel_id=1, source_target_pairs={{1,0},{2,1},{3,2},{5,4},{6,5},{7,6},{9,8},{10,9},{11,10},{13,12},{... | collective-permute-start | bytes 786440 | tf_op jit(solution)/shard_map/ppermute | solution.py:94
  75.9 17.1 %collective-permute-start.19 = (bf16[2,4,16,2560]{3,2,1,0:T(8,128)(2,1)S(1)}, bf16[2,4,16,2560]{3,2,1,0:T(8,128)(2,1)S(1)}, u32[]{:S(2)}, u32[]{:S(2)}) collective-permute-start(bf16[2,4,16,2560]{3,2,1,0:T(8,128)(2,1)S(1)} %pad_maximum_fusion.2), channel_id=1, source_target_pairs={{0,8},{4,12},{8,0},{12,4},{16,24},{20,28},{24,16},{28,20},{1,9},{5... | collective-permute-start | bytes 1966088 | tf_op jit(solution)/shard_map/ppermute | solution.py:90
  76.5 16.7 %collective-permute-start.20 = (bf16[2,4,16,2560]{3,2,1,0:T(8,128)(2,1)S(1)}, bf16[2,4,16,2560]{3,2,1,0:T(8,128)(2,1)S(1)}, u32[]{:S(2)}, u32[]{:S(2)}) collective-permute-start(bf16[2,4,16,2560]{3,2,1,0:T(8,128)(2,1)S(1)} %stack.48), channel_id=1, source_target_pairs={{0,16},{4,20},{8,24},{12,28},{16,0},{20,4},{24,8},{28,12},{1,17},{... | collective-permute-start | bytes 1966088 | tf_op jit(solution)/shard_map/ppermute | solution.py:90
  93.5 11.6 %collective-permute-start.34 = (bf16[1,4,16,2560]{3,2,1,0:T(8,128)(2,1)S(1)}, bf16[1,4,16,2560]{3,2,1,0:T(8,128)(2,1)S(1)}, u32[]{:S(2)}, u32[]{:S(2)}) collective-permute-start(bf16[1,4,16,2560]{3,2,1,0:T(8,128)(2,1)S(1)} %get-tuple-element.182), channel_id=1, source_target_pairs={{0,16},{4,20},{8,24},{12,28},{16,0},{20,4},{24,8},{28,12},{1,17},{... | collective-permute-start | bytes 983048 | tf_op jit(solution)/shard_map/ppermute | solution.py:90
  95.1 10.1 %collective-permute-start.35 = (bf16[1,4,16,2560]{3,2,1,0:T(8,128)(2,1)S(1)}, bf16[1,4,16,2560]{3,2,1,0:T(8,128)(2,1)S(1)}, u32[]{:S(2)}, u32[]{:S(2)}) collective-permute-start(bf16[1,4,16,2560]{3,2,1,0:T(8,128)(2,1)S(1)} %get-tuple-element.177), channel_id=1, source_target_pairs={{0,8},{4,12},{8,0},{12,4},{16,24},{20,28},{24,16},{28,20},{1,9},{5... | collective-permute-start | bytes 983048 | tf_op jit(solution)/shard_map/ppermute | solution.py:90
  96.0 9.1 %collective-permute-start.21 = (bf16[256,512]{1,0:T(8,128)(2,1)S(1)}, bf16[256,512]{1,0:T(8,128)(2,1)S(1)}, u32[]{:S(2)}, u32[]{:S(2)}) collective-permute-start(bf16[256,512]{1,0:T(8,128)(2,1)S(1)} %add_convert_fusion.7), channel_id=1, source_target_pairs={{1,0},{2,1},{3,2},{5,4},{6,5},{7,6},{9,8},{10,9},{11,10},{13,12},{... | collective-permute-start | bytes 786440 | tf_op jit(solution)/shard_map/ppermute | solution.py:94
  99.4 9.0 %collective-permute-start.23 = (bf16[4,4,16,1536]{3,2,1,0:T(8,128)(2,1)S(1)}, bf16[4,4,16,1536]{3,2,1,0:T(8,128)(2,1)S(1)}, u32[]{:S(2)}, u32[]{:S(2)}) collective-permute-start(bf16[4,4,16,1536]{3,2,1,0:T(8,128)(2,1)S(1)} %get-tuple-element.151), channel_id=1, source_target_pairs={{0,4},{4,0},{8,12},{12,8},{16,20},{20,16},{24,28},{28,24},{1,5},{5... | collective-permute-start | bytes 2359304 | tf_op jit(solution)/shard_map/ppermute | solution.py:90
  105.4 12.0 %collective-permute-start.36 = (bf16[2,16,5120]{2,1,0:T(8,128)(2,1)S(1)}, bf16[2,16,5120]{2,1,0:T(8,128)(2,1)S(1)}, u32[]{:S(2)}, u32[]{:S(2)}) collective-permute-start(bf16[2,16,5120]{2,1,0:T(8,128)(2,1)S(1)} %pad_maximum_fusion.7), channel_id=1, source_target_pairs={{0,1},{1,0},{2,3},{3,2},{4,5},{5,4},{6,7},{7,6},{8,9},{9,8},{10,11... | collective-permute-start | bytes 983048 | tf_op jit(solution)/shard_map/ppermute | solution.py:90
  110.6 18.3 %collective-permute-start.22 = (bf16[256,512]{1,0:T(8,128)(2,1)S(1)}, bf16[256,512]{1,0:T(8,128)(2,1)S(1)}, u32[]{:S(2)}, u32[]{:S(2)}) collective-permute-start(bf16[256,512]{1,0:T(8,128)(2,1)S(1)} %add_convert_fusion.6), channel_id=1, source_target_pairs={{1,0},{2,1},{3,2},{5,4},{6,5},{7,6},{9,8},{10,9},{11,10},{13,12},{... | collective-permute-start | bytes 786440 | tf_op jit(solution)/shard_map/ppermute | solution.py:94
  117.4 6.8 %collective-permute-start.37 = (bf16[1,16,5120]{2,1,0:T(8,128)(2,1)S(1)}, bf16[1,16,5120]{2,1,0:T(8,128)(2,1)S(1)}, u32[]{:S(2)}, u32[]{:S(2)}) collective-permute-start(bf16[1,16,5120]{2,1,0:T(8,128)(2,1)S(1)} %add_convert_fusion.9), channel_id=1, source_target_pairs={{0,2},{1,3},{2,0},{3,1},{4,6},{5,7},{6,4},{7,5},{8,10},{9,11},{10,... | collective-permute-start | bytes 491528 | tf_op jit(solution)/shard_map/ppermute | solution.py:90
  121.6 7.2 %collective-permute-start.28 = (bf16[2,16,1536]{2,1,0:T(8,128)(2,1)S(1)}, bf16[2,16,1536]{2,1,0:T(8,128)(2,1)S(1)}, u32[]{:S(2)}, u32[]{:S(2)}) collective-permute-start(bf16[2,16,1536]{2,1,0:T(8,128)(2,1)S(1)} %pad_maximum_fusion.12), channel_id=1, source_target_pairs={{0,1},{1,0},{2,3},{3,2},{4,5},{5,4},{6,7},{7,6},{8,9},{9,8},{10,11... | collective-permute-start | bytes 294920 | tf_op jit(solution)/shard_map/ppermute | solution.py:90
  125.6 8.9 %collective-permute-start.39 = (bf16[16,5120]{1,0:T(8,128)(2,1)S(1)}, bf16[16,5120]{1,0:T(8,128)(2,1)S(1)}, u32[]{:S(2)}, u32[]{:S(2)}) collective-permute-start(bf16[16,5120]{1,0:T(8,128)(2,1)S(1)} %fusion.4), channel_id=1, source_target_pairs={{0,16},{4,20},{8,24},{12,28},{16,0},{20,4},{24,8},{28,12},{1,17},{... | collective-permute-start | bytes 491528 | tf_op jit(solution)/shard_map/ppermute | solution.py:90
  128.9 6.7 %collective-permute-start.40 = (bf16[16,5120]{1,0:T(8,128)(2,1)S(1)}, bf16[16,5120]{1,0:T(8,128)(2,1)S(1)}, u32[]{:S(2)}, u32[]{:S(2)}) collective-permute-start(bf16[16,5120]{1,0:T(8,128)(2,1)S(1)} %fusion.4), channel_id=1, source_target_pairs={{0,24},{4,28},{8,16},{12,20},{16,8},{20,12},{24,0},{28,4},{1,25},{... | collective-permute-start | bytes 491528 | tf_op jit(solution)/shard_map/ppermute | solution.py:90
  139.2 7.2 %collective-permute-start.41 = (bf16[64,5120]{1,0:T(8,128)(2,1)S(1)}, bf16[64,5120]{1,0:T(8,128)(2,1)S(1)}, u32[]{:S(2)}, u32[]{:S(2)}) collective-permute-start(bf16[64,5120]{1,0:T(8,128)(2,1)S(1)} %pad_maximum_fusion.3.mine), channel_id=1, source_target_pairs={{0,4},{4,0},{8,12},{12,8},{16,20},{20,16},{24,28},{28,24},{1,5},{5... | collective-permute-start | bytes 1966088 | tf_op jit(solution)/shard_map/ppermute | solution.py:90
  (28 other events, 141.6 us)
